TPU v7x, 32 devices: a whole 2x2x4 slice. The times are simulated.
32 devices in a mesh: data: 32 (over z, y, x, core).
Axes of the slice: x: 2, y: 2, z: 4, core: 2. Of those that a mesh axis runs over, the one named last changes fastest.
Arguments:
- w_in: float32 [16, 512, 2048], replicated
- w_out: float32 [16, 2048, 512], replicated
- mom_in: float32 [16, 512, 2048], replicated
- mom_out: float32 [16, 2048, 512], replicated
- x_first: bfloat16 [2048, 512], P('data')
- y_first: bfloat16 [2048, 512], P('data')
- x_second: bfloat16 [2048, 512], P('data')
- y_second: bfloat16 [2048, 512], P('data')
Outputs:
- output 1: float32 [16, 512, 2048], replicated
- output 2: float32 [16, 2048, 512], replicated
- output 3: float32 [16, 512, 2048], replicated
- output 4: float32 [16, 2048, 512], replicated
- output 5: float32 [2048], P('data')
- output 6: float32 [2048, 512], P('data')
All inputs are finite; a program needn't handle non-finite values.
Results may differ from a plain program's by a relative error of at most 0.00803043.
Values are sent between devices in bfloat16 or wider.
A program may use at most 2.25 GiB of HBM per device.

v0:
```python
import jax
import jax.numpy as jnp
from jax import lax
from jax.sharding import PartitionSpec as P

LR_SCALE = 1.0
MOMENTUM = 0.9
ROW_CONTRACT = (((0,), (0,)), ((), ()))
COL_CONTRACT = (((1,), (1,)), ((), ()))


def forward_stack(w_in_list, w_out_list, h_cur):
    saved_acts = []
    for w_in_l, w_out_l in zip(w_in_list, w_out_list):
        h_bf = h_cur.astype(jnp.bfloat16)
        pre_act = jnp.dot(h_bf, w_in_l, preferred_element_type=jnp.float32)
        act_bf = jax.nn.gelu(pre_act).astype(jnp.bfloat16)
        h_cur = h_cur + jnp.dot(act_bf, w_out_l, preferred_element_type=jnp.float32)
        saved_acts.append((h_bf, pre_act, act_bf))
    return h_cur, saved_acts


def layer_backward(w_in_l, w_out_l, saved_layer, err_row, need_err):
    h_bf, pre_act, act_bf = saved_layer
    err_bf = err_row.astype(jnp.bfloat16)
    grad_out = lax.dot_general(act_bf, err_bf, ROW_CONTRACT, preferred_element_type=jnp.float32)
    d_act = lax.dot_general(err_bf, w_out_l, COL_CONTRACT, preferred_element_type=jnp.float32)
    d_pre = jax.vjp(jax.nn.gelu, pre_act)[1](d_act)[0].astype(jnp.bfloat16)
    grad_in = lax.dot_general(h_bf, d_pre, ROW_CONTRACT, preferred_element_type=jnp.float32)
    if need_err:
        err_row = err_row + lax.dot_general(d_pre, w_in_l, COL_CONTRACT, preferred_element_type=jnp.float32)
    return grad_in.astype(jnp.bfloat16), grad_out.astype(jnp.bfloat16), err_row


def apply_update(weights, moments, grad_sum, step_size):
    mom_new = MOMENTUM * moments + grad_sum.astype(jnp.float32)
    return weights - step_size * mom_new, mom_new


def solution(mesh):
    groups = mesh.shape["data"]
    rows_spec = P("data", None)

    def local_steps(w_in, w_out, mom_in, mom_out, x_first, y_first, x_second, y_second):
        layers = w_in.shape[0]
        tok_local, model_dim = x_first.shape
        step_size = LR_SCALE / layers
        w_in_list = [w_in[layer_idx].astype(jnp.bfloat16) for layer_idx in range(layers)]
        w_out_list = [w_out[layer_idx].astype(jnp.bfloat16) for layer_idx in range(layers)]
        h_last, saved_acts = forward_stack(w_in_list, w_out_list, x_first.astype(jnp.float32))
        err_row = (h_last - y_first.astype(jnp.float32)) * (1.0 / (tok_local * groups * model_dim))
        sums_in = [None] * layers
        sums_out = [None] * layers
        for layer_idx in reversed(range(layers)):
            grad_in, grad_out, err_row = layer_backward(w_in_list[layer_idx], w_out_list[layer_idx], saved_acts[layer_idx], err_row, layer_idx > 0)
            sums_in[layer_idx], sums_out[layer_idx] = lax.psum((grad_in, grad_out), "data")
        w_in_new, mom_in_new = apply_update(w_in, mom_in, jnp.stack(sums_in), step_size)
        w_out_new, mom_out_new = apply_update(w_out, mom_out, jnp.stack(sums_out), step_size)
        new_in_list = [w_in_new[layer_idx].astype(jnp.bfloat16) for layer_idx in range(layers)]
        new_out_list = [w_out_new[layer_idx].astype(jnp.bfloat16) for layer_idx in range(layers)]
        h_next, unused = forward_stack(new_in_list, new_out_list, x_second.astype(jnp.float32))
        row_diff = h_next - y_second.astype(jnp.float32)
        loss_rows = jnp.sum(row_diff * row_diff, axis=-1) / (2 * model_dim)
        return w_in_new, w_out_new, mom_in_new, mom_out_new, loss_rows, h_next

    return jax.shard_map(local_steps, mesh=mesh, in_specs=(P(), P(), P(), P(), rows_spec, rows_spec, rows_spec, rows_spec), out_specs=(P(), P(), P(), P(), P("data"), rows_spec), check_vma=False)
```

profile of v0, /device:TPU:0, one launch (start us, length us, event | category | flops | bytes accessed | tf_op | source)
XLA Modules:
  0.0 1929.4 jit_solution(8319758598548648992)
XLA Ops:
  7.2 32.4 %convert.73 = bf16[16,2048,512]{2,1,0:T(8,128)(2,1)} convert(f32[16,2048,512]{2,1,0:T(8,128)} %param.9) | non-fusion elementwise | flops 16777216 | bytes 100663296 | tf_op jit(solution)/shard_map/convert.62
  39.6 32.4 %convert.72 = bf16[16,512,2048]{2,1,0:T(8,128)(2,1)} convert(f32[16,512,2048]{2,1,0:T(8,128)} %param.8) | non-fusion elementwise | flops 16777216 | bytes 100663296 | tf_op jit(solution)/shard_map/convert.63
  76.3 2.5 fusion.67
  78.9 2.7 fusion.156
  81.5 2.7 fusion.71
  84.2 2.7 fusion.154
  125.3 2.4 fusion.287
  128.5 2.9 fusion.280
  132.1 2.4 fusion.273
  135.3 2.4 fusion.266
  138.5 2.4 fusion.259
  141.7 2.4 fusion.252
  144.9 2.4 fusion.245
  148.1 2.4 fusion.238
  151.3 2.4 fusion.231
  154.5 2.4 fusion.224
  157.7 2.4 fusion.217
  164.2 2.6 fusion.203
  167.5 2.4 fusion.196
  170.7 2.4 fusion.189
  206.2 4.3 fusion
  210.5 3.0 fusion.16
  213.5 3.1 fusion.1
  243.8 2.5 fusion.15
  246.3 62.5 %copy.30 = f32[16,512,2048]{1,2,0:T(8,128)} copy(f32[16,512,2048]{2,1,0:T(8,128)} %param.8) | data formatting | bytes 134217728 | tf_op args[0]
  308.8 62.5 %copy.14 = f32[16,512,2048]{1,2,0:T(8,128)} copy(f32[16,512,2048]{2,1,0:T(8,128)} %param.10) | data formatting | bytes 134217728 | tf_op args[2]
  371.2 1111.3 %all-reduce.3.cloned.1.call-done = (bf16[1,512,2048]{1,2,0:T(8,128)(2,1)}, bf16[1,512,2048]{1,2,0:T(8,128)(2,1)}, bf16[1,512,2048]{1,2,0:T(8,128)(2,1)}, bf16[1,...) async-done(((bf16[1,512,2048]{1,2,0:T(8,128)(2,1)}, ...) | async-done | bytes 67108880 | tf_op jit(solution)/shard_map/psum | solution.py:56
  1482.6 3.2 constant_dynamic-update-slice_fusion.15
  1509.1 104.8 %fusion.649 = (bf16[16,512,2048]{1,2,0:T(8,128)(2,1)}, f32[16,512,2048]{1,2,0:T(8,128)}, f32[16,512,2048]{1,2,0:T(8,128)}) fusion(f32[16,512,2048]{1,2,0:T(8,128)} %copy.30, bf16[16,512,2048]{1,2,0:T(8,128)(2,1)} %constant_dynamic-update-slice_fusion, f32[16,512,2048]{1,2,0:T(8,128)} %copy.14), kind=kLoop, calls=%fused_computation.832 | loop fusion | flops 100663296 | bytes 335544320 | tf_op jit(solution)/shard_map/convert.31
  1614.0 62.5 %copy.31 = f32[16,512,2048]{2,1,0:T(8,128)} copy(f32[16,512,2048]{1,2,0:T(8,128)} %get-tuple-element.45) | data formatting | bytes 134217728
  1676.4 62.6 %copy.32 = f32[16,512,2048]{2,1,0:T(8,128)} copy(f32[16,512,2048]{1,2,0:T(8,128)} %get-tuple-element.46) | data formatting | bytes 134217728
  1762.1 105.4 %fusion.650 = (bf16[16,2048,512]{2,1,0:T(8,128)(2,1)}, f32[16,2048,512]{2,1,0:T(8,128)}, f32[16,2048,512]{2,1,0:T(8,128)}) fusion(f32[16,2048,512]{2,1,0:T(8,128)} %param.9, bf16[16,2048,512]{2,1,0:T(8,128)(2,1)} %constant_dynamic-update-slice_fusion.16, f32[16,2048,512]{2,1,0:T(8,128)} %param.11), kind=kLoop, calls=%fused_computation.833 | loop fusion | flops 100663296 | bytes 335544320 | tf_op jit(solution)/shard_map/convert.30
  1867.5 3.3 fusion.159
  1870.9 3.3 fusion.160
  1874.2 3.3 fusion.161
  1877.5 3.3 fusion.162
  1880.9 3.3 fusion.163
  1884.2 3.3 fusion.164
  1887.6 3.3 fusion.165
  1890.9 3.3 fusion.166
  1894.3 3.3 fusion.167
  1897.6 3.3 fusion.168
  1901.0 3.3 fusion.169
  1904.3 3.3 fusion.170
  1907.7 3.3 fusion.171
  1911.0 3.3 fusion.172
  1914.4 3.4 fusion.173
  1917.8 4.1 multiply_reduce_fusion
  (220 shorter events, 162.9 us)
Async XLA Ops:
  7.2 1475.4 %all-reduce.3.cloned.1.call-start = ((), (), s32[]{:S(2)}) async-start(), calls=%async_computation | async-start | bytes 134217728 | tf_op jit(solution)/shard_map/psum | solution.py:56
  39.6 32.4 %copy-start.53 = (bf16[64,512]{1,0:T(8,128)(2,1)S(1)}, bf16[64,512]{1,0:T(8,128)(2,1)}, u32[]{:S(2)}) copy-start(bf16[64,512]{1,0:T(8,128)(2,1)} %param.12) | copy-start | bytes 196612
  74.1 25.3 %copy-start = (bf16[16,512,2048]{2,1,0:T(8,128)(2,1)S(1)}, bf16[16,512,2048]{2,1,0:T(8,128)(2,1)}, u32[]{:S(2)}) copy-start(bf16[16,512,2048]{2,1,0:T(8,128)(2,1)} %convert.72) | copy-start | bytes 100663296
  120.1 3.1 copy-start.54
  141.0 4.0 copy-start.32
  144.2 4.0 copy-start.34
  147.4 4.0 copy-start.36
  150.6 4.0 copy-start.38
  153.8 4.0 copy-start.40
  157.0 4.0 copy-start.42
  160.2 4.0 copy-start.44
  163.4 4.1 copy-start.46
  166.7 4.0 copy-start.48
  169.9 5.3 copy-start.50
  173.1 31.6 %copy-start.52 = (bf16[64,2048]{1,0:T(8,128)(2,1)}, bf16[64,2048]{1,0:T(8,128)(2,1)S(1)}, u32[]{:S(2)}) copy-start(bf16[64,2048]{1,0:T(8,128)(2,1)S(1)} %fusion.189) | copy-start | bytes 786436
  210.4 6.1 copy-start.51
  210.5 8.1 copy-start.49
  213.5 7.3 copy-start.47
  216.5 6.3 copy-start.45
  218.6 6.3 copy-start.43
  220.7 6.3 copy-start.41
  222.8 6.3 copy-start.39
  224.9 6.3 copy-start.37
  227.0 6.3 copy-start.35
  229.2 6.2 copy-start.33
  1482.6 3.2 copy-start.31
  1482.6 4.7 copy-start.30
  1487.2 2.9 copy-start.28
  1488.7 2.9 copy-start.27
  1490.2 2.9 copy-start.26
  1491.6 2.9 copy-start.25
  1493.1 2.9 copy-start.24
  1494.5 2.9 copy-start.23
  1497.5 2.9 copy-start.21
  1676.4 62.6 %copy-start.15 = (bf16[1,2048,512]{2,1,0:T(8,128)(2,1)S(1)}, bf16[1,2048,512]{2,1,0:T(8,128)(2,1)}, u32[]{:S(2)}) copy-start(bf16[1,2048,512]{2,1,0:T(8,128)(2,1)} %get-tuple-element.29) | copy-start | bytes 6291460
  1739.0 3.8 copy-start.13
  1741.4 3.0 copy-start.12
  1742.8 3.0 copy-start.11
  1744.3 3.0 copy-start.10
  1745.8 3.0 copy-start.9
  1750.2 2.9 copy-start.6
  1751.7 3.0 copy-start.5
  1753.2 3.0 copy-start.4
  1754.7 3.0 copy-start.3
  1756.2 3.0 copy-start.2
  1757.7 3.0 copy-start.1
  1762.1 105.4 %copy-start.55 = (bf16[64,512]{1,0:T(8,128)(2,1)S(1)}, bf16[64,512]{1,0:T(8,128)(2,1)}, u32[]{:S(2)}) copy-start(bf16[64,512]{1,0:T(8,128)(2,1)} %param.14) | copy-start | bytes 196612
  1914.4 3.4 copy-start.56
  (10 other events, 28.6 us)
Sparse Core Ops, SparseCore 0:
  246.4 1236.1 all-reduce.2
where the time goes:
time: 1940 us; the launch traced here: 1930 us
  waiting for transfers between devices  1110 us (57%)
  local copies, waits for them, and re-layouts  300 us (15%)
  other arithmetic  276 us (14%)
  matrix products  228 us (12%)
    psum x1, waiting for transfers between devices, local_steps(): lax.psum((grad_in, grad_out), 'data')  1110 us
    unnamed x148, local copies, waits for them, and re-layouts  297 us
    another operation x4, other arithmetic  275 us
    dot_general x32, matrix products, forward_stack(): h_cur = h_cur + jnp.dot(act_bf, w_out_l, preferred_element_type=jnp.float32)  89 us
  transfers between devices with their start and end apart: 1, of which 1 were waited for; matrix products, arithmetic and copies ran while one was open for 6% of the time, Pallas kernels for 0%

commit v1 on v0

v1 whole, which is shorter than its diff:
```python
import functools

import jax
import jax.numpy as jnp
from jax import lax
from jax.experimental import pallas as pl
from jax.experimental.pallas import tpu as pltpu
from jax.sharding import PartitionSpec as P

LR_SCALE = 1.0
MOMENTUM = 0.9
F32 = jnp.float32
BF16 = jnp.bfloat16
MESH = pl.DeviceIdType.MESH
GELU_C = 0.7978845608028654
GELU_K = 0.044715
SLOTS = 4
PIECES = 4
VMEM_LIMIT = 62 * 1024 * 1024

NN = (((1,), (0,)), ((), ()))
NT = (((1,), (1,)), ((), ()))
TN = (((0,), (0,)), ((), ()))


def mm(a, b, dims=NN):
    return lax.dot_general(a, b, dims, preferred_element_type=F32)


def gelu(z):
    t = jnp.tanh(GELU_C * (z + GELU_K * (z * z * z)))
    return z * (0.5 * (1.0 + t))


def gelu_grad(z):
    zz = z * z
    t = jnp.tanh(GELU_C * (z + GELU_K * (zz * z)))
    cdf = 0.5 * (1.0 + t)
    slope = cdf + (0.5 * z) * (1.0 - t * t) * (GELU_C * (1.0 + (3.0 * GELU_K) * zz))
    return z * cdf, slope


def grads_kernel(dims, w1_hbm, w2_hbm, x_ref, y_ref, *rest):
    n_dev, layers, rows, d, hid = dims
    chips = n_dev // 2
    hc = hid // 2
    piece = hc // PIECES
    g_refs = rest[:PIECES]
    (wb1, wb2, z_all, hb, eb, hcur, rh, re, ow1, ow2, zq, aa, ss, acc1, acc2,
     w1_sem, w2_sem, hs_sem, hr_sem, es_sem, er_sem, px_send, px_recv) = rest[PIECES:]

    me = lax.axis_index("data")
    chip = me // 2
    core = me % 2
    partner = chip * 2 + (1 - core)

    def greet(c, carry):
        @pl.when(c != chip)
        def _():
            pl.semaphore_signal(barrier, inc=1, device_id=(2 * c + core,), device_id_type=MESH)
        return carry

    barrier = pltpu.get_barrier_semaphore()
    lax.fori_loop(0, chips, greet, 0)
    pl.semaphore_signal(barrier, inc=1, device_id=(partner,), device_id_type=MESH)

    def w1_copy(l, j, slot):
        return pltpu.make_async_copy(w1_hbm.at[l, :, pl.ds(pl.multiple_of(j * hc, 128), hc)], wb1.at[slot], w1_sem.at[slot])

    def w2_copy(l, j, slot):
        return pltpu.make_async_copy(w2_hbm.at[l, pl.ds(pl.multiple_of(j * hc, 128), hc), :], wb2.at[slot], w2_sem.at[slot])

    def fetch(l, j, slot):
        w1_copy(l, j, slot).start()
        w2_copy(l, j, slot).start()

    def arrived(l, j, slot):
        w1_copy(l, j, slot).wait()
        w2_copy(l, j, slot).wait()

    for i in range(SLOTS):
        fetch(i // 2, i % 2, i)
    pl.semaphore_wait(barrier, chips)

    def h_copy(l):
        return pltpu.make_async_remote_copy(
            src_ref=hb.at[l], dst_ref=rh.at[core * chips + chip], send_sem=hs_sem.at[l], recv_sem=hr_sem.at[chip],
            device_id=(2 * l + core,), device_id_type=MESH)

    def e_copy(l):
        return pltpu.make_async_remote_copy(
            src_ref=eb.at[l], dst_ref=re.at[core * chips + chip], send_sem=es_sem.at[l], recv_sem=er_sem.at[chip],
            device_id=(2 * l + core,), device_id_type=MESH)

    def h_arrival(c):
        return pltpu.make_async_remote_copy(
            src_ref=hb.at[0], dst_ref=rh.at[core * chips + c], send_sem=hs_sem.at[0], recv_sem=hr_sem.at[c],
            device_id=(me,), device_id_type=MESH)

    def e_arrival(c):
        return pltpu.make_async_remote_copy(
            src_ref=eb.at[0], dst_ref=re.at[core * chips + c], send_sem=es_sem.at[0], recv_sem=er_sem.at[c],
            device_id=(me,), device_id_type=MESH)

    def send_h(l):
        @pl.when(l != chip)
        def _():
            h_copy(l).start()

        @pl.when(l == chip)
        def _():
            rh[core * chips + chip] = hb[l]

    def send_e(l):
        @pl.when(l != chip)
        def _():
            e_copy(l).start()

        @pl.when(l == chip)
        def _():
            re[core * chips + chip] = eb[l]

    n_fwd = 2 * layers
    n_bwd = 2 * (layers - 1)
    hcur[...] = x_ref[...].astype(F32)

    def forward(i, carry):
        l, j, slot = i // 2, i % 2, i % SLOTS
        arrived(l, j, slot)

        @pl.when(j == 0)
        def _():
            hb[l] = hcur[...].astype(BF16)

        z = mm(hb[l], wb1[slot].astype(BF16))
        z_all[i] = z
        hcur[...] += mm(gelu(z).astype(BF16), wb2[slot].astype(BF16))

        nxt = i + SLOTS

        @pl.when(nxt < n_fwd)
        def _():
            fetch(nxt // 2, nxt % 2, slot)

        @pl.when(nxt >= n_fwd)
        def _():
            fetch(layers - 1 - (nxt - n_fwd) // 2, nxt % 2, slot)

        @pl.when(j == 1)
        def _():
            send_h(l)
        return carry

    lax.fori_loop(0, n_fwd, forward, 0)

    scale = 1.0 / (rows * n_dev * d)
    hcur[...] = (hcur[...] - y_ref[...].astype(F32)) * scale

    h_swap = pltpu.make_async_remote_copy(
        src_ref=rh.at[pl.ds(core * chips, chips)], dst_ref=rh.at[pl.ds(core * chips, chips)],
        send_sem=px_send.at[0], recv_sem=px_recv.at[0], device_id=(partner,), device_id_type=MESH)
    e_swap = pltpu.make_async_remote_copy(
        src_ref=re.at[pl.ds(core * chips, chips)], dst_ref=re.at[pl.ds(core * chips, chips)],
        send_sem=px_send.at[1], recv_sem=px_recv.at[1], device_id=(partner,), device_id_type=MESH)

    def backward(i, carry):
        l, j, slot = layers - 1 - i // 2, i % 2, i % SLOTS
        arrived(l, j, slot)

        @pl.when(j == 0)
        def _():
            eb[l] = hcur[...].astype(BF16)

        q = mm(eb[l], wb2[slot].astype(BF16), NT)
        slope = gelu_grad(z_all[2 * l + j])[1]
        hcur[...] += mm((slope * q).astype(BF16), wb1[slot].astype(BF16), NT)

        nxt = i + SLOTS

        @pl.when(nxt < n_bwd)
        def _():
            fetch(layers - 1 - nxt // 2, nxt % 2, slot)

        @pl.when(nxt == n_bwd)
        def _():
            fetch(chip, core, slot)

        @pl.when(j == 1)
        def _():
            send_e(l)
        return carry

    lax.fori_loop(0, n_bwd, backward, 0)
    eb[0] = hcur[...].astype(BF16)

    own_slot = n_bwd % SLOTS
    arrived(chip, core, own_slot)
    ow1[...] = wb1[own_slot].astype(BF16)
    ow2[...] = wb2[own_slot].astype(BF16)
    acc1[...] = jnp.zeros_like(acc1)
    acc2[...] = jnp.zeros_like(acc2)
    send_e(0)

    def h_in(c, carry):
        @pl.when(c != chip)
        def _():
            h_arrival(c).wait_recv()
        return carry

    def e_in(c, carry):
        @pl.when(c != chip)
        def _():
            e_arrival(c).wait_recv()
        return carry

    lax.fori_loop(0, chips, h_in, 0)
    h_swap.start()
    lax.fori_loop(0, chips, e_in, 0)
    e_swap.start()

    group = 4
    half_groups = chips // group
    nb = hc // piece

    def owner(gi, carry):
        half = (core + gi // half_groups) % 2

        @pl.when(gi == half_groups)
        def _():
            h_swap.wait_recv()
            e_swap.wait_recv()

        base = half * chips + (gi % half_groups) * group
        hg = rh[pl.ds(base, group)].reshape(group * rows, d)
        eg = re[pl.ds(base, group)].reshape(group * rows, d)
        for n in range(nb):
            cols = slice(n * piece, (n + 1) * piece)
            z = mm(hg, ow1[:, cols])
            q = mm(eg, ow2[cols, :], NT)
            a, slope = gelu_grad(z)
            aa[n] = a.astype(BF16).reshape(group, rows, piece)
            ss[n] = (slope * q).astype(BF16).reshape(group, rows, piece)

        def products(n, c2):
            for b in range(group):
                h_b = rh[base + b]
                e_b = re[base + b]
                acc1[n] += mm(h_b, ss[n, b], TN).astype(BF16).astype(F32)
                acc2[n] += mm(aa[n, b], e_b, TN).astype(BF16).astype(F32)
            return c2

        lax.fori_loop(0, nb, products, 0)
        return carry

    lax.fori_loop(0, 2 * half_groups, owner, 0)

    for n in range(PIECES):
        for cb in range(piece // 128):
            g_refs[n][cb * d:(cb + 1) * d, :] = acc1[n, :, cb * 128:(cb + 1) * 128].astype(BF16)
        off = (piece // 128) * d
        for lb in range(d // 128):
            g_refs[n][off + lb * piece:off + (lb + 1) * piece, :] = acc2[n, :, lb * 128:(lb + 1) * 128].astype(BF16)

    def sent(l, carry):
        @pl.when(l != chip)
        def _():
            h_copy(l).wait_send()
            e_copy(l).wait_send()
        return carry

    lax.fori_loop(0, layers, sent, 0)
    h_swap.wait_send()
    e_swap.wait_send()


def local_grads(w_in, w_out, x, y, n_dev):
    layers, d, hid = w_in.shape
    rows = x.shape[0]
    hc = hid // 2
    piece = hc // PIECES
    g_rows = (piece // 128) * d + (d // 128) * piece
    dims = (n_dev, layers, rows, d, hid)
    flops = 2 * rows * d * hid * layers * 4 + 2 * rows * n_dev * d * hc * 4
    return pl.pallas_call(
        functools.partial(grads_kernel, dims),
        out_shape=[jax.ShapeDtypeStruct((g_rows, 128), BF16)] * PIECES,
        in_specs=[pl.BlockSpec(memory_space=pl.ANY)] * 2 + [pl.BlockSpec(memory_space=pltpu.VMEM)] * 2,
        out_specs=[pl.BlockSpec(memory_space=pltpu.VMEM)] * PIECES,
        scratch_shapes=[
            pltpu.VMEM((SLOTS, d, hc), F32),
            pltpu.VMEM((SLOTS, hc, d), F32),
            pltpu.VMEM((2 * layers, rows, hc), F32),
            pltpu.VMEM((layers, rows, d), BF16),
            pltpu.VMEM((layers, rows, d), BF16),
            pltpu.VMEM((rows, d), F32),
            pltpu.VMEM((n_dev, rows, d), BF16),
            pltpu.VMEM((n_dev, rows, d), BF16),
            pltpu.VMEM((d, hc), BF16),
            pltpu.VMEM((hc, d), BF16),
            pltpu.VMEM((8, 128), F32),
            pltpu.VMEM((PIECES, 4, rows, piece), BF16),
            pltpu.VMEM((PIECES, 4, rows, piece), BF16),
            pltpu.VMEM((PIECES, d, piece), F32),
            pltpu.VMEM((PIECES, piece, d), F32),
            pltpu.SemaphoreType.DMA((SLOTS,)),
            pltpu.SemaphoreType.DMA((SLOTS,)),
            pltpu.SemaphoreType.DMA((layers,)),
            pltpu.SemaphoreType.DMA((layers,)),
            pltpu.SemaphoreType.DMA((layers,)),
            pltpu.SemaphoreType.DMA((layers,)),
            pltpu.SemaphoreType.DMA((2,)),
            pltpu.SemaphoreType.DMA((2,)),
        ],
        compiler_params=pltpu.CompilerParams(collective_id=0, has_side_effects=True, vmem_limit_bytes=VMEM_LIMIT),
        cost_estimate=pl.CostEstimate(flops=flops, bytes_accessed=4 * w_in.size * 4, transcendentals=0),
        name="local_grads",
    )(w_in, w_out, x, y)


def update_kernel(first, last, dims, *refs):
    layers, rows, d, hid, piece = dims
    step_size = LR_SCALE / layers
    w1, m1, w2, m2, g = refs[:5]
    refs = refs[5:]
    if not first:
        refs = refs[4:]
    if last:
        side = refs[:2 * (PIECES - 1)]
        x_ref, y_ref = refs[2 * (PIECES - 1):2 * PIECES]
        w1o, w2o, m1o, m2o, loss_ref, h_out, nb1, nb2, h_ref, hb_ref = refs[2 * PIECES:]
    else:
        w1o, w2o, m1o, m2o, nb1, nb2 = refs
    lead = () if last else (0,)

    for cb in range(piece // 128):
        cols = slice(cb * 128, (cb + 1) * 128)
        mn = MOMENTUM * m1[0, :, cols] + g[0, cb * d:(cb + 1) * d, :].astype(F32)
        wn = w1[0, :, cols] - step_size * mn
        m1o[0, :, cols] = mn
        w1o[0, :, cols] = wn
        nb1[(*lead, slice(None), cols)] = wn.astype(BF16)
    off = (piece // 128) * d
    for lb in range(d // 128):
        cols = slice(lb * 128, (lb + 1) * 128)
        mn = MOMENTUM * m2[0, :, cols] + g[0, off + lb * piece:off + (lb + 1) * piece, :].astype(F32)
        wn = w2[0, :, cols] - step_size * mn
        m2o[0, :, cols] = mn
        w2o[0, :, cols] = wn
        nb2[(*lead, slice(None), cols)] = wn.astype(BF16)
    if not last:
        return

    l, c = pl.program_id(0), pl.program_id(1)

    @pl.when(jnp.logical_and(l == 0, c == 0))
    def _():
        h_ref[...] = x_ref[...].astype(F32)

    @pl.when(c == 0)
    def _():
        hb_ref[...] = h_ref[...].astype(BF16)

    total = h_ref[...]
    for p in range(PIECES):
        a1 = side[2 * p][0] if p < PIECES - 1 else nb1[...]
        a2 = side[2 * p + 1][0] if p < PIECES - 1 else nb2[...]
        z = mm(hb_ref[...], a1)
        total += mm(gelu(z).astype(BF16), a2)
    h_ref[...] = total

    @pl.when(jnp.logical_and(l == layers - 1, c == 1))
    def _():
        h_out[...] = h_ref[...]
        diff = h_ref[...] - y_ref[...].astype(F32)
        loss_ref[...] = jnp.sum(diff * diff, axis=-1, keepdims=True) / (2 * d)


def update(p, w_in, m_in, w_out, m_out, g_all, prev, side, x, y):
    layers, d, hid = w_in.shape
    rows = x.shape[0]
    piece = hid // 2 // PIECES
    first, last = p == 0, p == PIECES - 1
    in_spec = pl.BlockSpec((1, d, piece), lambda l, c: (l, 0, c * PIECES + p))
    out_spec = pl.BlockSpec((1, piece, d), lambda l, c: (l, c * PIECES + p, 0))
    g_spec = pl.BlockSpec((1, g_all.shape[1], 128), lambda l, c: (2 * l + c, 0, 0))
    any_spec = pl.BlockSpec(memory_space=pl.ANY)
    s1_spec = pl.BlockSpec((1, d, piece), lambda l, c: (2 * l + c, 0, 0))
    s2_spec = pl.BlockSpec((1, piece, d), lambda l, c: (2 * l + c, 0, 0))
    whole = pl.BlockSpec((rows, d), lambda l, c: (0, 0))
    in_specs = [in_spec, in_spec, out_spec, out_spec, g_spec]
    args = [w_in, m_in, w_out, m_out, g_all]
    out_specs = [in_spec, out_spec, in_spec, out_spec]
    out_shape = [jax.ShapeDtypeStruct(a.shape, F32) for a in (w_in, w_out, m_in, m_out)]
    aliases = {}
    scratch = []
    if not first:
        aliases = {5 + i: i for i in range(4)}
        in_specs += [any_spec] * 4
        args += prev
    if last:
        in_specs += [s1_spec, s2_spec] * (PIECES - 1) + [whole, whole]
        args += side + [x, y]
        out_specs += [pl.BlockSpec((rows, 1), lambda l, c: (0, 0)), whole]
        out_shape += [jax.ShapeDtypeStruct((rows, 1), F32), jax.ShapeDtypeStruct((rows, d), F32)]
        scratch = [pltpu.VMEM((d, piece), BF16), pltpu.VMEM((piece, d), BF16), pltpu.VMEM((rows, d), F32), pltpu.VMEM((rows, d), BF16)]
    else:
        out_specs += [s1_spec, s2_spec]
        out_shape += [jax.ShapeDtypeStruct((2 * layers, d, piece), BF16), jax.ShapeDtypeStruct((2 * layers, piece, d), BF16)]
    n_el = 2 * w_in.size // PIECES
    return pl.pallas_call(
        functools.partial(update_kernel, first, last, (layers, rows, d, hid, piece)),
        grid=(layers, 2),
        in_specs=in_specs,
        out_specs=out_specs,
        out_shape=out_shape,
        scratch_shapes=scratch,
        input_output_aliases=aliases,
        compiler_params=pltpu.CompilerParams(dimension_semantics=("arbitrary", "arbitrary"), vmem_limit_bytes=VMEM_LIMIT),
        cost_estimate=pl.CostEstimate(flops=400 * n_el, bytes_accessed=20 * n_el, transcendentals=0),
        name=f"update_{p}",
    )(*args)


def solution(mesh):
    n_dev = mesh.shape["data"]
    rows_spec = P("data", None)

    def local_steps(w_in, w_out, mom_in, mom_out, x_first, y_first, x_second, y_second):
        pieces = local_grads(w_in, w_out, x_first, y_first, n_dev)
        gathered = [lax.all_gather(g, "data", axis=0) for g in pieces]
        prev, side = [], []
        for p in range(PIECES):
            outs = update(p, w_in, mom_in, w_out, mom_out, gathered[p], prev, side, x_second, y_second)
            prev = list(outs[:4])
            side = side + list(outs[4:])
        loss, h_final = outs[4:]
        w_in_new, w_out_new, mom_in_new, mom_out_new = prev
        return w_in_new, w_out_new, mom_in_new, mom_out_new, loss.reshape(-1), h_final

    return jax.shard_map(
        local_steps, mesh=mesh,
        in_specs=(P(), P(), P(), P(), rows_spec, rows_spec, rows_spec, rows_spec),
        out_specs=(P(), P(), P(), P(), P("data"), rows_spec), check_vma=False)
```

time: 1940 us -> 682 us (0.35)
  waiting for transfers between devices: 1110 us -> 268 us
  Pallas kernels: 0 us -> 398 us
  local copies, waits for them, and re-layouts: 300 us -> 0 us
  other arithmetic: 276 us -> 1.39 us
  matrix products: 228 us -> 0 us
    psum x1 -> x0, waiting for transfers between devices: 1110 us -> none  [local_steps(): lax.psum((grad_in, grad_out), 'data')]
    pallas_call x0 -> x5, Pallas kernels: none -> 398 us  [the longest x4 265 us: update(): pl.pallas_call(functools.partial(update_kernel, first, last, (layers, row...]
    unnamed x148 -> x0, local copies, waits for them, and re-layouts: 297 us -> none
    another operation x4 -> x0, other arithmetic: 275 us -> none
    all_gather x0 -> x4, waiting for transfers between devices: none -> 266 us  [local_steps(): gathered = [lax.all_gather(g, 'data', axis=0) for g in pieces]]
    dot_general x110 -> x0, matrix products: 228 us -> none  [the longest x32 89 us: forward_stack(): h_cur = h_cur + jnp.dot(act_bf, w_out_l, preferred_element_type=jnp.float32)]
  transfers between devices with their start and end apart: 1 -> 4, of which waited for: 1 -> 4; matrix products, arithmetic and copies ran while one was open for 6% -> 0% of each run, Pallas kernels for 0% -> 28%
where the time goes in v1:
time: 682 us; the launch traced here: 681 us
  Pallas kernels  398 us (58%)
  waiting for transfers between devices  268 us (39%)
  between operations  13.8 us (2%)
    all_gather x4, waiting for transfers between devices, local_steps(): gathered = [lax.all_gather(g, 'data', axis=0) for g in pieces]  266 us
    pallas_call x4, Pallas kernels, update(): pl.pallas_call(functools.partial(update_kernel, first, last, (layers, row...  265 us
    pallas_call x1, Pallas kernels, local_grads(): pl.pallas_call(functools.partial(grads_kernel, dims), out_shape=[jax.Shap...  133 us
  transfers between devices with their start and end apart: 4, of which 4 were waited for; matrix products, arithmetic and copies ran while one was open for 0% of the time, Pallas kernels for 28%

profile of v1, /device:TPU:0, one launch (start us, length us, event | category | flops | bytes accessed | tf_op | source)
XLA Modules:
  0.0 681.0 jit_solution(5688847475437951388)
XLA Ops:
  7.2 0.0 all-gather.15.cloned.1.call-start
  7.2 132.8 %local_grads.1 = (bf16[2048,128]{1,0:T(8,128)(2,1)}, bf16[2048,128]{1,0:T(8,128)(2,1)}, bf16[2048,128]{1,0:T(8,128)(2,1)}, bf16[2048,128]{1,0:T(8,128)(2,1)}) custom-call(f32[16,512,2048]{2,1,0:T(8,128)} %refs_0_.7, f32[16,2048,512]{2,1,0:T(8,128)} %refs_2_.7, bf16[64,512]{1,0:T(8,128)(2,1)} %x_ref.1, bf16[64,512]{1,0:T(8,128)(2,1)} %y_ref.1), custom_call_target="tpu_custom_call" | custom-call | flops 17179869184 | bytes 268435456 | tf_op jit(solution)/shard_map/local_grads/pallas_call | solution.py:284
  140.1 0.0 all-gather.15.cloned.1.call-update
  140.1 0.0 all-gather.13.cloned.1.call-start
  140.1 0.7 all-gather.13.cloned.1.call-update
  140.8 0.0 all-gather.11.cloned.1.call-start
  140.9 0.7 all-gather.11.cloned.1.call-update
  141.6 0.0 all-gather.9.cloned.1.call-start
  141.6 0.5 all-gather.9.cloned.1.call-update
  142.2 108.1 %all-gather.15.cloned.1.call-done = bf16[65536,128]{1,0:T(8,128)(2,1)} async-done(((bf16[2048,128]{1,0:T(8,128)(2,1)}), bf16[65536,128]{1,0:T(8,128)(2,1)}) %all-gather.15.cloned.1.call-update) | async-done | bytes 16777232 | tf_op jit(solution)/shard_map/all_gather | solution.py:430
  250.3 62.6 %update_0.1 = (f32[16,512,2048]{2,1,0:T(8,128)}, f32[16,2048,512]{2,1,0:T(8,128)}, f32[16,512,2048]{2,1,0:T(8,128)}, f32[16,2048,512]{2,1,0:T(8,128)}, bf16[32,5...) custom-call(f32[16,512,2048]{2,1,0:T(8,128)} %refs_0_.7, f32[16,512,2048]{2,1,0:T(8,128)} %refs_1_.7, ...), custom_call_target="tpu_custom_call" | custom-call | flops 3355443200 | bytes 167772160 | tf_op jit(solution)/shard_map/update_0/pallas_call | solution.py:410
  312.9 52.8 %all-gather.13.cloned.1.call-done = bf16[65536,128]{1,0:T(8,128)(2,1)} async-done(((bf16[2048,128]{1,0:T(8,128)(2,1)}), bf16[65536,128]{1,0:T(8,128)(2,1)}) %all-gather.13.cloned.1.call-update) | async-done | bytes 16777232 | tf_op jit(solution)/shard_map/all_gather | solution.py:430
  365.6 62.6 %update_1.1 = (f32[16,512,2048]{2,1,0:T(8,128)}, f32[16,2048,512]{2,1,0:T(8,128)}, f32[16,512,2048]{2,1,0:T(8,128)}, f32[16,2048,512]{2,1,0:T(8,128)}, bf16[32,5...) custom-call(f32[16,512,2048]{2,1,0:T(8,128)} %refs_0_.7, ...), custom_call_target="tpu_custom_call", output_to_operand_aliasing={{0}: (5, {}), {1}: (6, {}), {2}: (7, {}), {3}: (8, {})} | custom-call | flops 3355443200 | bytes 167772160 | tf_op jit(solution)/shard_map/update_1/pallas_call | solution.py:410
  428.3 52.8 %all-gather.11.cloned.1.call-done = bf16[65536,128]{1,0:T(8,128)(2,1)} async-done(((bf16[2048,128]{1,0:T(8,128)(2,1)}), bf16[65536,128]{1,0:T(8,128)(2,1)}) %all-gather.11.cloned.1.call-update) | async-done | bytes 16777232 | tf_op jit(solution)/shard_map/all_gather | solution.py:430
  481.0 62.6 %update_2.1 = (f32[16,512,2048]{2,1,0:T(8,128)}, f32[16,2048,512]{2,1,0:T(8,128)}, f32[16,512,2048]{2,1,0:T(8,128)}, f32[16,2048,512]{2,1,0:T(8,128)}, bf16[32,5...) custom-call(f32[16,512,2048]{2,1,0:T(8,128)} %refs_0_.7, ...), custom_call_target="tpu_custom_call", output_to_operand_aliasing={{0}: (5, {}), {1}: (6, {}), {2}: (7, {}), {3}: (8, {})} | custom-call | flops 3355443200 | bytes 167772160 | tf_op jit(solution)/shard_map/update_2/pallas_call | solution.py:410
  543.7 52.6 %all-gather.9.cloned.1.call-done = bf16[65536,128]{1,0:T(8,128)(2,1)} async-done(((bf16[2048,128]{1,0:T(8,128)(2,1)}), bf16[65536,128]{1,0:T(8,128)(2,1)}) %all-gather.9.cloned.1.call-update) | async-done | bytes 16777232 | tf_op jit(solution)/shard_map/all_gather | solution.py:430
  596.3 76.8 %update_3.1 = (f32[16,512,2048]{2,1,0:T(8,128)}, f32[16,2048,512]{2,1,0:T(8,128)}, f32[16,512,2048]{2,1,0:T(8,128)}, f32[16,2048,512]{2,1,0:T(8,128)}, f32[64,1]{1,0:T(8,128)}, /*index=5*/f32[64,512]{1,0:T(8,128)}) custom-call(f32[16,512,2048]{2,1,0:T(8,128)} %refs_0_.7, ...), custom_call_target="tpu_custom_call", output_to_operand_aliasing={{0}: (5, {}), {1}: (6, {}), {2}: (7, {}), {3}: (8, {})} | custom-call | flops 3355443200 | bytes 167772160 | tf_op jit(solution)/shard_map/update_3/pallas_call | solution.py:410
  673.1 1.4 reduce
Async XLA Ops:
  7.2 243.1 %all-gather.15.cloned.1.call-start = ((), (), s32[]{:S(2)}) async-start(), calls=%async_computation.3 | async-start | bytes 17301504 | tf_op jit(solution)/shard_map/all_gather | solution.py:430
  140.1 225.6 %all-gather.13.cloned.1.call-start = ((), (), s32[]{:S(2)}) async-start(), calls=%async_computation.2 | async-start | bytes 17301504 | tf_op jit(solution)/shard_map/all_gather | solution.py:430
  140.8 340.2 %all-gather.11.cloned.1.call-start = ((), (), s32[]{:S(2)}) async-start(), calls=%async_computation.1 | async-start | bytes 17301504 | tf_op jit(solution)/shard_map/all_gather | solution.py:430
  141.6 454.7 %all-gather.9.cloned.1.call-start = ((), (), s32[]{:S(2)}) async-start(), calls=%async_computation | async-start | bytes 17301504 | tf_op jit(solution)/shard_map/all_gather | solution.py:430
Sparse Core Ops, SparseCore 0:
  140.2 109.9 all-gather.14
  253.1 112.4 all-gather.12
  368.5 112.4 all-gather.10
  483.8 112.4 all-gather.8

commit v2 on v1

--- a/solution.py
+++ b/solution.py
@@ -15,7 +15,8 @@
 GELU_C = 0.7978845608028654
 GELU_K = 0.044715
 SLOTS = 4
-PIECES = 4
+QUARTERS = 4
+ROUTES = ((0, 2, 1), (1, 2, 0), (2, 0, 1), (2, 1, 0))
 VMEM_LIMIT = 62 * 1024 * 1024
 
 NN = (((1,), (0,)), ((), ()))
@@ -44,15 +45,17 @@
     n_dev, layers, rows, d, hid = dims
     chips = n_dev // 2
     hc = hid // 2
-    piece = hc // PIECES
-    g_refs = rest[:PIECES]
-    (wb1, wb2, z_all, hb, eb, hcur, rh, re, ow1, ow2, zq, aa, ss, acc1, acc2,
-     w1_sem, w2_sem, hs_sem, hr_sem, es_sem, er_sem, px_send, px_recv) = rest[PIECES:]
+    piece = hc // QUARTERS
+    (g_all, wb1, wb2, z_all, hb, eb, hcur, rh, re, ow1, ow2, aa, ss, acc1, acc2, own,
+     w1_sem, w2_sem, hs_sem, hr_sem, es_sem, er_sem, px_send, px_recv,
+     sp_send, sp_recv, tw_send, tw_recv, own_sem) = rest
 
     me = lax.axis_index("data")
     chip = me // 2
     core = me % 2
     partner = chip * 2 + (1 - core)
+
+    cx, cy, cz = chip % 2, (chip // 2) % 2, chip // 4
 
     def greet(c, carry):
         @pl.when(c != chip)
@@ -220,7 +223,6 @@
 
     group = 4
     half_groups = chips // group
-    nb = hc // piece
 
     def owner(gi, carry):
         half = (core + gi // half_groups) % 2
@@ -233,33 +235,108 @@
         base = half * chips + (gi % half_groups) * group
         hg = rh[pl.ds(base, group)].reshape(group * rows, d)
         eg = re[pl.ds(base, group)].reshape(group * rows, d)
-        for n in range(nb):
+        for n in range(QUARTERS):
             cols = slice(n * piece, (n + 1) * piece)
             z = mm(hg, ow1[:, cols])
             q = mm(eg, ow2[cols, :], NT)
             a, slope = gelu_grad(z)
-            aa[n] = a.astype(BF16).reshape(group, rows, piece)
-            ss[n] = (slope * q).astype(BF16).reshape(group, rows, piece)
-
-        def products(n, c2):
+            aa[n, pl.ds(base, group)] = a.astype(BF16).reshape(group, rows, piece)
+            ss[n, pl.ds(base, group)] = (slope * q).astype(BF16).reshape(group, rows, piece)
+        return carry
+
+    lax.fori_loop(0, 2 * half_groups, owner, 0)
+
+    def place(src, n):
+        return g_all.at[2 * src + core, n]
+
+    hops = {"x": chip + 1 - 2 * cx, "y": chip + 2 - 4 * cy, "up": chip + 4, "down": chip - 4}
+    exists = {"x": None, "y": None, "up": cz < 3, "down": cz > 0}
+    kinds = ("x", "y", "up", "down")
+
+    def sends(n, rel):
+        order = ROUTES[n]
+        last = max([i for i in range(3) if rel[order[i]]], default=-1)
+        out = []
+        if last >= 0 and order[last] == 2:
+            out.append("down" if rel[2] > 0 else "up")
+        for i in range(last + 1, 3):
+            out += {0: ["x"], 1: ["y"], 2: ["up", "down"]}[order[i]]
+        return out
+
+    def source(rel):
+        sx = 1 - cx if rel[0] else cx
+        sy = 1 - cy if rel[1] else cy
+        return (cz + rel[2]) * 4 + sy * 2 + sx
+
+    def hop_copy(n, rel, kind):
+        src = source(rel)
+        block = place(src, n) if any(rel) else own.at[n]
+        return pltpu.make_async_remote_copy(
+            src_ref=block, dst_ref=place(src, n), send_sem=sp_send.at[n, kinds.index(kind), src],
+            recv_sem=sp_recv.at[n, src], device_id=(2 * hops[kind] + core,), device_id_type=MESH)
+
+    def twin_copy(n, rel):
+        src = source(rel)
+        block = place(src, n) if any(rel) else own.at[n]
+        return pltpu.make_async_remote_copy(
+            src_ref=block, dst_ref=place(src, n), send_sem=tw_send.at[n, src], recv_sem=tw_recv.at[n, src],
+            device_id=(partner,), device_id_type=MESH)
+
+    def guarded(cond, fn):
+        if cond is None:
+            fn()
+        else:
+            pl.when(cond)(fn)
+
+    def valid(rel):
+        if rel[2] > 0:
+            return cz <= 3 - rel[2]
+        return cz >= -rel[2] if rel[2] < 0 else None
+
+    def forward_block(n, rel):
+        def act():
+            if any(rel):
+                hop_copy(n, rel, "x").wait_recv()
+            for kind in sends(n, rel):
+                guarded(exists[kind], hop_copy(n, rel, kind).start)
+            twin_copy(n, rel).start()
+        guarded(valid(rel), act)
+
+    def drain_block(n, rel):
+        def act():
+            for kind in sends(n, rel):
+                guarded(exists[kind], hop_copy(n, rel, kind).wait_send)
+            twin_copy(n, rel).wait_send()
+        guarded(valid(rel), act)
+
+    rels = [(rx, ry, dz) for rx in (0, 1) for ry in (0, 1) for dz in (-3, -2, -1, 0, 1, 2, 3)]
+    steps = sorted(((n, rel) for n in range(QUARTERS) for rel in rels),
+                   key=lambda t: (t[1][0] + t[1][1] + abs(t[1][2]), t[0]))
+    steps = [t for t in steps if any(t[1])]
+    here = (0, 0, 0)
+
+    for n in range(QUARTERS):
+        acc1[...] = jnp.zeros_like(acc1)
+        acc2[...] = jnp.zeros_like(acc2)
+
+        def products(gi, carry):
             for b in range(group):
-                h_b = rh[base + b]
-                e_b = re[base + b]
-                acc1[n] += mm(h_b, ss[n, b], TN).astype(BF16).astype(F32)
-                acc2[n] += mm(aa[n, b], e_b, TN).astype(BF16).astype(F32)
-            return c2
-
-        lax.fori_loop(0, nb, products, 0)
-        return carry
-
-    lax.fori_loop(0, 2 * half_groups, owner, 0)
-
-    for n in range(PIECES):
+                k = gi * group + b
+                acc1[...] += mm(rh[k], ss[n, k], TN).astype(BF16).astype(F32)
+                acc2[...] += mm(aa[n, k], re[k], TN).astype(BF16).astype(F32)
+            return carry
+
+        lax.fori_loop(0, 2 * half_groups, products, 0)
         for cb in range(piece // 128):
-            g_refs[n][cb * d:(cb + 1) * d, :] = acc1[n, :, cb * 128:(cb + 1) * 128].astype(BF16)
+            own[n, cb * d:(cb + 1) * d, :] = acc1[:, cb * 128:(cb + 1) * 128].astype(BF16)
         off = (piece // 128) * d
         for lb in range(d // 128):
-            g_refs[n][off + lb * piece:off + (lb + 1) * piece, :] = acc2[n, :, lb * 128:(lb + 1) * 128].astype(BF16)
+            own[n, off + lb * piece:off + (lb + 1) * piece, :] = acc2[:, lb * 128:(lb + 1) * 128].astype(BF16)
+        pltpu.make_async_copy(own.at[n], g_all.at[me, n], own_sem.at[n]).start()
+        forward_block(n, here)
+
+    for n, rel in steps:
+        forward_block(n, rel)
 
     def sent(l, carry):
         @pl.when(l != chip)
@@ -271,21 +348,35 @@
     lax.fori_loop(0, layers, sent, 0)
     h_swap.wait_send()
     e_swap.wait_send()
+    for n in range(QUARTERS):
+        pltpu.make_async_copy(own.at[n], g_all.at[me, n], own_sem.at[n]).wait()
+        drain_block(n, here)
+    for n, rel in steps:
+        drain_block(n, rel)
+
+    def twin_in(i, carry):
+        n, src = i // chips, i % chips
+        pltpu.make_async_remote_copy(
+            src_ref=place(src, n), dst_ref=g_all.at[2 * src + 1 - core, n], send_sem=tw_send.at[n, src],
+            recv_sem=tw_recv.at[n, src], device_id=(me,), device_id_type=MESH).wait_recv()
+        return carry
+
+    lax.fori_loop(0, QUARTERS * chips, twin_in, 0)
 
 
 def local_grads(w_in, w_out, x, y, n_dev):
     layers, d, hid = w_in.shape
     rows = x.shape[0]
     hc = hid // 2
-    piece = hc // PIECES
+    piece = hc // QUARTERS
     g_rows = (piece // 128) * d + (d // 128) * piece
     dims = (n_dev, layers, rows, d, hid)
     flops = 2 * rows * d * hid * layers * 4 + 2 * rows * n_dev * d * hc * 4
     return pl.pallas_call(
         functools.partial(grads_kernel, dims),
-        out_shape=[jax.ShapeDtypeStruct((g_rows, 128), BF16)] * PIECES,
+        out_shape=jax.ShapeDtypeStruct((n_dev, QUARTERS, g_rows, 128), BF16),
         in_specs=[pl.BlockSpec(memory_space=pl.ANY)] * 2 + [pl.BlockSpec(memory_space=pltpu.VMEM)] * 2,
-        out_specs=[pl.BlockSpec(memory_space=pltpu.VMEM)] * PIECES,
+        out_specs=pl.BlockSpec(memory_space=pl.ANY),
         scratch_shapes=[
             pltpu.VMEM((SLOTS, d, hc), F32),
             pltpu.VMEM((SLOTS, hc, d), F32),
@@ -297,11 +388,11 @@
             pltpu.VMEM((n_dev, rows, d), BF16),
             pltpu.VMEM((d, hc), BF16),
             pltpu.VMEM((hc, d), BF16),
-            pltpu.VMEM((8, 128), F32),
-            pltpu.VMEM((PIECES, 4, rows, piece), BF16),
-            pltpu.VMEM((PIECES, 4, rows, piece), BF16),
-            pltpu.VMEM((PIECES, d, piece), F32),
-            pltpu.VMEM((PIECES, piece, d), F32),
+            pltpu.VMEM((QUARTERS, n_dev, rows, piece), BF16),
+            pltpu.VMEM((QUARTERS, n_dev, rows, piece), BF16),
+            pltpu.VMEM((d, piece), F32),
+            pltpu.VMEM((piece, d), F32),
+            pltpu.VMEM((QUARTERS, g_rows, 128), BF16),
             pltpu.SemaphoreType.DMA((SLOTS,)),
             pltpu.SemaphoreType.DMA((SLOTS,)),
             pltpu.SemaphoreType.DMA((layers,)),
@@ -310,6 +401,11 @@
             pltpu.SemaphoreType.DMA((layers,)),
             pltpu.SemaphoreType.DMA((2,)),
             pltpu.SemaphoreType.DMA((2,)),
+            pltpu.SemaphoreType.DMA((QUARTERS, 4, n_dev // 2)),
+            pltpu.SemaphoreType.DMA((QUARTERS, n_dev // 2)),
+            pltpu.SemaphoreType.DMA((QUARTERS, n_dev // 2)),
+            pltpu.SemaphoreType.DMA((QUARTERS, n_dev // 2)),
+            pltpu.SemaphoreType.DMA((QUARTERS,)),
         ],
         compiler_params=pltpu.CompilerParams(collective_id=0, has_side_effects=True, vmem_limit_bytes=VMEM_LIMIT),
         cost_estimate=pl.CostEstimate(flops=flops, bytes_accessed=4 * w_in.size * 4, transcendentals=0),
@@ -317,38 +413,27 @@
     )(w_in, w_out, x, y)
 
 
-def update_kernel(first, last, dims, *refs):
-    layers, rows, d, hid, piece = dims
+def update_kernel(dims, w1, m1, w2, m2, g, x_ref, y_ref, w1o, w2o, m1o, m2o, loss_ref, h_out, nb1, nb2, h_ref, hb_ref):
+    layers, rows, d, hid = dims
+    piece = hid // 2 // QUARTERS
     step_size = LR_SCALE / layers
-    w1, m1, w2, m2, g = refs[:5]
-    refs = refs[5:]
-    if not first:
-        refs = refs[4:]
-    if last:
-        side = refs[:2 * (PIECES - 1)]
-        x_ref, y_ref = refs[2 * (PIECES - 1):2 * PIECES]
-        w1o, w2o, m1o, m2o, loss_ref, h_out, nb1, nb2, h_ref, hb_ref = refs[2 * PIECES:]
-    else:
-        w1o, w2o, m1o, m2o, nb1, nb2 = refs
-    lead = () if last else (0,)
-
-    for cb in range(piece // 128):
-        cols = slice(cb * 128, (cb + 1) * 128)
-        mn = MOMENTUM * m1[0, :, cols] + g[0, cb * d:(cb + 1) * d, :].astype(F32)
-        wn = w1[0, :, cols] - step_size * mn
-        m1o[0, :, cols] = mn
-        w1o[0, :, cols] = wn
-        nb1[(*lead, slice(None), cols)] = wn.astype(BF16)
     off = (piece // 128) * d
-    for lb in range(d // 128):
-        cols = slice(lb * 128, (lb + 1) * 128)
-        mn = MOMENTUM * m2[0, :, cols] + g[0, off + lb * piece:off + (lb + 1) * piece, :].astype(F32)
-        wn = w2[0, :, cols] - step_size * mn
-        m2o[0, :, cols] = mn
-        w2o[0, :, cols] = wn
-        nb2[(*lead, slice(None), cols)] = wn.astype(BF16)
-    if not last:
-        return
+    for n in range(QUARTERS):
+        for cb in range(piece // 128):
+            cols = slice(n * piece + cb * 128, n * piece + (cb + 1) * 128)
+            mn = MOMENTUM * m1[0, :, cols] + g[0, n, cb * d:(cb + 1) * d, :].astype(F32)
+            wn = w1[0, :, cols] - step_size * mn
+            m1o[0, :, cols] = mn
+            w1o[0, :, cols] = wn
+            nb1[:, cols] = wn.astype(BF16)
+        hid_rows = slice(n * piece, (n + 1) * piece)
+        for lb in range(d // 128):
+            cols = slice(lb * 128, (lb + 1) * 128)
+            mn = MOMENTUM * m2[0, hid_rows, cols] + g[0, n, off + lb * piece:off + (lb + 1) * piece, :].astype(F32)
+            wn = w2[0, hid_rows, cols] - step_size * mn
+            m2o[0, hid_rows, cols] = mn
+            w2o[0, hid_rows, cols] = wn
+            nb2[hid_rows, cols] = wn.astype(BF16)
 
     l, c = pl.program_id(0), pl.program_id(1)
 
@@ -360,13 +445,8 @@
     def _():
         hb_ref[...] = h_ref[...].astype(BF16)
 
-    total = h_ref[...]
-    for p in range(PIECES):
-        a1 = side[2 * p][0] if p < PIECES - 1 else nb1[...]
-        a2 = side[2 * p + 1][0] if p < PIECES - 1 else nb2[...]
-        z = mm(hb_ref[...], a1)
-        total += mm(gelu(z).astype(BF16), a2)
-    h_ref[...] = total
+    z = mm(hb_ref[...], nb1[...])
+    h_ref[...] += mm(gelu(z).astype(BF16), nb2[...])
 
     @pl.when(jnp.logical_and(l == layers - 1, c == 1))
     def _():
@@ -375,50 +455,27 @@
         loss_ref[...] = jnp.sum(diff * diff, axis=-1, keepdims=True) / (2 * d)
 
 
-def update(p, w_in, m_in, w_out, m_out, g_all, prev, side, x, y):
+def update(w_in, m_in, w_out, m_out, g_all, x, y):
     layers, d, hid = w_in.shape
     rows = x.shape[0]
-    piece = hid // 2 // PIECES
-    first, last = p == 0, p == PIECES - 1
-    in_spec = pl.BlockSpec((1, d, piece), lambda l, c: (l, 0, c * PIECES + p))
-    out_spec = pl.BlockSpec((1, piece, d), lambda l, c: (l, c * PIECES + p, 0))
-    g_spec = pl.BlockSpec((1, g_all.shape[1], 128), lambda l, c: (2 * l + c, 0, 0))
-    any_spec = pl.BlockSpec(memory_space=pl.ANY)
-    s1_spec = pl.BlockSpec((1, d, piece), lambda l, c: (2 * l + c, 0, 0))
-    s2_spec = pl.BlockSpec((1, piece, d), lambda l, c: (2 * l + c, 0, 0))
+    hc = hid // 2
+    in_spec = pl.BlockSpec((1, d, hc), lambda l, c: (l, 0, c))
+    out_spec = pl.BlockSpec((1, hc, d), lambda l, c: (l, c, 0))
+    g_spec = pl.BlockSpec((1, *g_all.shape[1:]), lambda l, c: (2 * l + c, 0, 0, 0))
     whole = pl.BlockSpec((rows, d), lambda l, c: (0, 0))
-    in_specs = [in_spec, in_spec, out_spec, out_spec, g_spec]
-    args = [w_in, m_in, w_out, m_out, g_all]
-    out_specs = [in_spec, out_spec, in_spec, out_spec]
-    out_shape = [jax.ShapeDtypeStruct(a.shape, F32) for a in (w_in, w_out, m_in, m_out)]
-    aliases = {}
-    scratch = []
-    if not first:
-        aliases = {5 + i: i for i in range(4)}
-        in_specs += [any_spec] * 4
-        args += prev
-    if last:
-        in_specs += [s1_spec, s2_spec] * (PIECES - 1) + [whole, whole]
-        args += side + [x, y]
-        out_specs += [pl.BlockSpec((rows, 1), lambda l, c: (0, 0)), whole]
-        out_shape += [jax.ShapeDtypeStruct((rows, 1), F32), jax.ShapeDtypeStruct((rows, d), F32)]
-        scratch = [pltpu.VMEM((d, piece), BF16), pltpu.VMEM((piece, d), BF16), pltpu.VMEM((rows, d), F32), pltpu.VMEM((rows, d), BF16)]
-    else:
-        out_specs += [s1_spec, s2_spec]
-        out_shape += [jax.ShapeDtypeStruct((2 * layers, d, piece), BF16), jax.ShapeDtypeStruct((2 * layers, piece, d), BF16)]
-    n_el = 2 * w_in.size // PIECES
+    n_el = 2 * w_in.size
     return pl.pallas_call(
-        functools.partial(update_kernel, first, last, (layers, rows, d, hid, piece)),
+        functools.partial(update_kernel, (layers, rows, d, hid)),
         grid=(layers, 2),
-        in_specs=in_specs,
-        out_specs=out_specs,
-        out_shape=out_shape,
-        scratch_shapes=scratch,
-        input_output_aliases=aliases,
+        in_specs=[in_spec, in_spec, out_spec, out_spec, g_spec, whole, whole],
+        out_specs=[in_spec, out_spec, in_spec, out_spec, pl.BlockSpec((rows, 1), lambda l, c: (0, 0)), whole],
+        out_shape=[jax.ShapeDtypeStruct(a.shape, F32) for a in (w_in, w_out, m_in, m_out)]
+        + [jax.ShapeDtypeStruct((rows, 1), F32), jax.ShapeDtypeStruct((rows, d), F32)],
+        scratch_shapes=[pltpu.VMEM((d, hc), BF16), pltpu.VMEM((hc, d), BF16), pltpu.VMEM((rows, d), F32), pltpu.VMEM((rows, d), BF16)],
         compiler_params=pltpu.CompilerParams(dimension_semantics=("arbitrary", "arbitrary"), vmem_limit_bytes=VMEM_LIMIT),
-        cost_estimate=pl.CostEstimate(flops=400 * n_el, bytes_accessed=20 * n_el, transcendentals=0),
-        name=f"update_{p}",
-    )(*args)
+        cost_estimate=pl.CostEstimate(flops=4 * rows * d * hid * layers, bytes_accessed=18 * n_el, transcendentals=0),
+        name="update",
+    )(w_in, m_in, w_out, m_out, g_all, x, y)
 
 
 def solution(mesh):
@@ -426,15 +483,8 @@
     rows_spec = P("data", None)
 
     def local_steps(w_in, w_out, mom_in, mom_out, x_first, y_first, x_second, y_second):
-        pieces = local_grads(w_in, w_out, x_first, y_first, n_dev)
-        gathered = [lax.all_gather(g, "data", axis=0) for g in pieces]
-        prev, side = [], []
-        for p in range(PIECES):
-            outs = update(p, w_in, mom_in, w_out, mom_out, gathered[p], prev, side, x_second, y_second)
-            prev = list(outs[:4])
-            side = side + list(outs[4:])
-        loss, h_final = outs[4:]
-        w_in_new, w_out_new, mom_in_new, mom_out_new = prev
+        g_all = local_grads(w_in, w_out, x_first, y_first, n_dev)
+        w_in_new, w_out_new, mom_in_new, mom_out_new, loss, h_final = update(w_in, mom_in, w_out, mom_out, g_all, x_second, y_second)
         return w_in_new, w_out_new, mom_in_new, mom_out_new, loss.reshape(-1), h_final
 
     return jax.shard_map(

time: 682 us -> 558 us (0.82)
  waiting for transfers between devices: 268 us -> 0 us
  Pallas kernels: 398 us -> 555 us
  between operations: 13.8 us -> 0.64 us
    all_gather x4 -> x0, waiting for transfers between devices: 266 us -> none  [local_steps(): gathered = [lax.all_gather(g, 'data', axis=0) for g in pieces]]
    pallas_call x5 -> x2, Pallas kernels: 398 us -> 555 us  [the longest x1 355 us: local_grads(): pl.pallas_call(functools.partial(grads_kernel, dims), out_shape=jax.Shape...]
  transfers between devices with their start and end apart: 4 -> 0, of which waited for: 4 -> 0; matrix products, arithmetic and copies ran while one was open for 0% -> 0% of each run, Pallas kernels for 28% -> 0%
where the time goes in v2:
time: 558 us; the launch traced here: 557 us
  Pallas kernels  555 us (99%)
    pallas_call x1, Pallas kernels, local_grads(): pl.pallas_call(functools.partial(grads_kernel, dims), out_shape=jax.Shape...  355 us
    pallas_call x1, Pallas kernels, update(): pl.pallas_call(functools.partial(update_kernel, (layers, rows, d, hid)),...  201 us

profile of v2, /device:TPU:0, one launch (start us, length us, event | category | flops | bytes accessed | tf_op | source)
XLA Modules:
  0.0 557.2 jit_solution(8366659348869246569)
XLA Ops:
  0.6 354.5 %local_grads.1.g = bf16[32,4,2048,128]{3,2,1,0:T(8,128)(2,1)} custom-call(f32[16,512,2048]{2,1,0:T(8,128)} %w1.1, f32[16,2048,512]{2,1,0:T(8,128)} %w2.1, bf16[64,512]{1,0:T(8,128)(2,1)} %x_ref.2, bf16[64,512]{1,0:T(8,128)(2,1)} %y_ref.2), custom_call_target="tpu_custom_call" | custom-call | flops 17179869184 | bytes 268435456 | tf_op jit(solution)/shard_map/local_grads/pallas_call | solution.py:375
  355.1 200.7 %update.1 = (f32[16,512,2048]{2,1,0:T(8,128)}, f32[16,2048,512]{2,1,0:T(8,128)}, f32[16,512,2048]{2,1,0:T(8,128)}, f32[16,2048,512]{2,1,0:T(8,128)}, f32[64,1]{1,0:T(8,128)}, /*index=5*/f32[64,512]{1,0:T(8,128)}) custom-call(f32[16,512,2048]{2,1,0:T(8,128)} %w1.1, f32[16,512,2048]{2,1,0:T(8,128)} %m1.1, f32[16,2048,512]{2,1,0:T(8,128)} %w2.1, ...), custom_call_target="tpu_custom_call" | custom-call | flops 4294967296 | bytes 603979776 | tf_op jit(solution)/shard_map/update/pallas_call | solution.py:467
  555.8 1.4 reduce

commit v3 on v2

v3 whole, which is shorter than its diff:
```python
import functools

import jax
import jax.numpy as jnp
from jax import lax
from jax.experimental import pallas as pl
from jax.experimental.pallas import tpu as pltpu
from jax.sharding import PartitionSpec as P


LR_SCALE = 1.0
MOMENTUM = 0.9
F32 = jnp.float32
BF16 = jnp.bfloat16
MESH = pl.DeviceIdType.MESH
GELU_C = 0.7978845608028654
GELU_K = 0.044715
SLOTS = 4
QUARTERS = 4
AHEAD = 4
CACHED = 4
FIRST = 1
RELAYS = (
    (100, 10, 1, 1100, 1010, 1001, 2100, 2010, 2001, 10001, 21001, 3100, 3010, 3001, 12001, 23001, 101, 1011, 2,
     10002, 20100, 2101, 3011, 1002, 11010, 21002, 102, 110, 3, 10003, 22100, 1110, 1012, 1003, 13010, 21003, 103,
     2110, 2003, 12003, 3110, 1013, 3003, 23003, 2103, 2002, 12002, 3013, 3002, 23002, 2102, 3012),
    (0, 101, 2, 10000, 1011, 20000, 1000, 2101, 1002, 10002, 3011, 21000, 2000, 100, 2002, 30000, 40002, 11000, 10,
     21002, 3000, 102, 3002, 31000, 41002, 12000, 1010, 22000, 1100, 3, 32000, 40003, 10003, 1012, 2100, 1003,
     21003, 33000, 41003, 12002, 2010, 20100, 103, 2003, 42003, 12003, 1013, 2102, 3003, 23003, 43003, 13000, 110,
     23000, 2103, 42002, 11010, 3013, 23002, 3100, 43002, 3010, 13010, 22100, 1110, 3012, 3110, 2110),
    (1, 102, 3, 10001, 1012, 1001, 2102, 1003, 21001, 10003, 3012, 21003, 2001, 101, 2003, 30001, 40003, 12001,
     1011, 3001, 103, 3003, 23001, 31001, 41003, 12003, 1013, 0, 2101, 20000, 30000, 42003, 10000, 3011, 1000,
     2103, 21000, 31000, 43003, 11000, 10, 2000, 100, 22000, 32000, 12000, 1010, 20100, 3000, 1100, 33000, 11010,
     2010, 23000, 2100, 32001, 13000, 110, 22100, 1110, 33001, 3010, 13010, 23003, 3100, 2110, 3110, 3013),
    (2, 103, 10002, 1013, 1002, 2103, 21002, 3013, 2002, 102, 12002, 1012, 3002, 23002, 2102, 1, 10001, 3012, 1001,
     21001, 101, 0, 10000, 20000, 1011, 1000, 21000, 11000, 100, 10, 20100, 2000, 12000, 1100, 1010, 22000, 11010,
     3000, 2100, 110, 13000, 23000, 2001, 1110, 2010, 22100, 12001, 3001, 3100, 3010, 23001, 13010, 2110, 2101,
     3011, 3110),
)
VMEM_LIMIT = 62 * 1024 * 1024

NN = (((1,), (0,)), ((), ()))
NT = (((1,), (1,)), ((), ()))
TN = (((0,), (0,)), ((), ()))


def mm(a, b, dims=NN):
    return lax.dot_general(a, b, dims, preferred_element_type=F32)


def gelu(z):
    t = jnp.tanh(GELU_C * (z + GELU_K * (z * z * z)))
    return z * (0.5 * (1.0 + t))


def gelu_grad(z):
    zz = z * z
    t = jnp.tanh(GELU_C * (z + GELU_K * (zz * z)))
    cdf = 0.5 * (1.0 + t)
    slope = cdf + (0.5 * z) * (1.0 - t * t) * (GELU_C * (1.0 + (3.0 * GELU_K) * zz))
    return z * cdf, slope


def grads_kernel(dims, w1_hbm, w2_hbm, x_ref, y_ref, *rest):
    n_dev, layers, rows, d, hid = dims
    chips = n_dev // 2
    hc = hid // 2
    piece = hc // QUARTERS
    chips_z = chips // 4
    n_out = 4 * chips_z + 4 * FIRST
    outs, rest = rest[:n_out], rest[n_out:]
    (wb1, wb2, cw1, cw2, z_all, hb, eb, hcur, rh, re, ow1, ow2, aa, ss, acc1, acc2, own,
     w1_sem, w2_sem, hs_sem, hr_sem, es_sem, er_sem, px_send, px_recv,
     sp_send, sp_recv, tw_send, tw_recv, own_sem) = rest

    me = lax.axis_index("data")
    chip = me // 2
    core = me % 2
    partner = chip * 2 + (1 - core)

    cx, cy, cz = chip % 2, (chip // 2) % 2, chip // 4

    def greet(c, carry):
        @pl.when(c != chip)
        def _():
            pl.semaphore_signal(barrier, inc=1, device_id=(2 * c + core,), device_id_type=MESH)

        return carry

    barrier = pltpu.get_barrier_semaphore()
    lax.fori_loop(0, chips, greet, 0)
    pl.semaphore_signal(barrier, inc=1, device_id=(partner,), device_id_type=MESH)

    def w1_copy(l, j, slot):
        return pltpu.make_async_copy(w1_hbm.at[l, :, pl.ds(pl.multiple_of(j * hc, 128), hc)], wb1.at[slot], w1_sem.at[slot])

    def w2_copy(l, j, slot):
        return pltpu.make_async_copy(w2_hbm.at[l, pl.ds(pl.multiple_of(j * hc, 128), hc), :], wb2.at[slot], w2_sem.at[slot])

    def fetch(l, j, slot):
        w1_copy(l, j, slot).start()
        w2_copy(l, j, slot).start()

    def arrived(l, j, slot):
        w1_copy(l, j, slot).wait()
        w2_copy(l, j, slot).wait()

    for i in range(SLOTS):
        fetch(i // 2, i % 2, i)
    pl.semaphore_wait(barrier, chips)

    def h_copy(l):
        return pltpu.make_async_remote_copy(
            src_ref=hb.at[l], dst_ref=rh.at[core * chips + chip], send_sem=hs_sem.at[l], recv_sem=hr_sem.at[chip],
            device_id=(2 * l + core,), device_id_type=MESH)

    def e_copy(l):
        return pltpu.make_async_remote_copy(
            src_ref=eb.at[l], dst_ref=re.at[core * chips + chip], send_sem=es_sem.at[l], recv_sem=er_sem.at[chip],
            device_id=(2 * l + core,), device_id_type=MESH)

    def h_arrival(c):
        return pltpu.make_async_remote_copy(
            src_ref=hb.at[0], dst_ref=rh.at[core * chips + c], send_sem=hs_sem.at[0], recv_sem=hr_sem.at[c],
            device_id=(me,), device_id_type=MESH)

    def e_arrival(c):
        return pltpu.make_async_remote_copy(
            src_ref=eb.at[0], dst_ref=re.at[core * chips + c], send_sem=es_sem.at[0], recv_sem=er_sem.at[c],
            device_id=(me,), device_id_type=MESH)

    def send_h(l):
        @pl.when(l != chip)
        def _():
            h_copy(l).start()

        @pl.when(l == chip)
        def _():
            rh[core * chips + chip] = hb[l]

    def send_e(l):
        @pl.when(l != chip)
        def _():
            e_copy(l).start()

        @pl.when(l == chip)
        def _():
            re[core * chips + chip] = eb[l]

    n_fwd = 2 * layers
    n_bwd = 2 * (layers - 1 - CACHED)
    hcur[...] = x_ref[...].astype(F32)

    def forward(i, carry):
        l, j, slot = i // 2, i % 2, i % SLOTS
        arrived(l, j, slot)

        @pl.when(j == 0)
        def _():
            hb[l] = hcur[...].astype(BF16)

        z = mm(hb[l], wb1[slot].astype(BF16))
        z_all[i] = z
        hcur[...] += mm(gelu(z).astype(BF16), wb2[slot].astype(BF16))

        @pl.when(l >= layers - CACHED)
        def _():
            cw1[i - (n_fwd - 2 * CACHED)] = wb1[slot].astype(BF16)
            cw2[i - (n_fwd - 2 * CACHED)] = wb2[slot].astype(BF16)

        nxt = i + SLOTS

        @pl.when(nxt < n_fwd)
        def _():
            fetch(nxt // 2, nxt % 2, slot)

        @pl.when(nxt >= n_fwd)
        def _():
            fetch(layers - 1 - CACHED - (nxt - n_fwd) // 2, nxt % 2, slot)

        @pl.when(j == 1)
        def _():
            send_h(l)

        return carry

    lax.fori_loop(0, n_fwd, forward, 0)

    scale = 1.0 / (rows * n_dev * d)
    hcur[...] = (hcur[...] - y_ref[...].astype(F32)) * scale

    h_swap = pltpu.make_async_remote_copy(
        src_ref=rh.at[pl.ds(core * chips, chips)], dst_ref=rh.at[pl.ds(core * chips, chips)],
        send_sem=px_send.at[0], recv_sem=px_recv.at[0], device_id=(partner,), device_id_type=MESH)
    e_swap = pltpu.make_async_remote_copy(
        src_ref=re.at[pl.ds(core * chips, chips)], dst_ref=re.at[pl.ds(core * chips, chips)],
        send_sem=px_send.at[1], recv_sem=px_recv.at[1], device_id=(partner,), device_id_type=MESH)

    def error_step(l, j, w1, w2):
        @pl.when(j == 0)
        def _():
            eb[l] = hcur[...].astype(BF16)

        q = mm(eb[l], w2, NT)
        slope = gelu_grad(z_all[2 * l + j])[1]
        hcur[...] += mm((slope * q).astype(BF16), w1, NT)

    def backward_cached(i, carry):
        l, j = layers - 1 - i // 2, i % 2
        kept = 2 * (l - (layers - CACHED)) + j
        error_step(l, j, cw1[kept], cw2[kept])

        @pl.when(j == 1)
        def _():
            send_e(l)

        return carry

    def backward(i, carry):
        l, j, slot = layers - 1 - CACHED - i // 2, i % 2, i % SLOTS
        arrived(l, j, slot)
        error_step(l, j, wb1[slot].astype(BF16), wb2[slot].astype(BF16))
        nxt = i + SLOTS

        @pl.when(nxt < n_bwd)
        def _():
            fetch(layers - 1 - CACHED - nxt // 2, nxt % 2, slot)

        @pl.when(nxt == n_bwd)
        def _():
            fetch(chip, core, slot)

        @pl.when(j == 1)
        def _():
            send_e(l)

        return carry

    lax.fori_loop(0, 2 * CACHED, backward_cached, 0)
    lax.fori_loop(0, n_bwd, backward, 0)
    eb[0] = hcur[...].astype(BF16)

    own_slot = n_bwd % SLOTS
    arrived(chip, core, own_slot)
    ow1[...] = wb1[own_slot].astype(BF16)
    ow2[...] = wb2[own_slot].astype(BF16)
    send_e(0)

    def h_in(c, carry):
        @pl.when(c != chip)
        def _():
            h_arrival(c).wait_recv()

        return carry

    def e_in(c, carry):
        @pl.when(c != chip)
        def _():
            e_arrival(c).wait_recv()

        return carry

    lax.fori_loop(0, chips, h_in, 0)
    h_swap.start()
    lax.fori_loop(0, chips, e_in, 0)
    e_swap.start()

    group = 4
    half_groups = chips // group

    def owner(gi, carry):
        half = (core + gi // half_groups) % 2

        @pl.when(gi == half_groups)
        def _():
            h_swap.wait_recv()
            e_swap.wait_recv()

        base = half * chips + (gi % half_groups) * group
        hg = rh[pl.ds(base, group)].reshape(group * rows, d)
        eg = re[pl.ds(base, group)].reshape(group * rows, d)
        for n in range(QUARTERS):
            cols = slice(n * piece, (n + 1) * piece)
            z = mm(hg, ow1[:, cols])
            q = mm(eg, ow2[cols, :], NT)
            a, slope = gelu_grad(z)
            aa[n, pl.ds(base, group)] = a.astype(BF16).reshape(group, rows, piece)
            ss[n, pl.ds(base, group)] = (slope * q).astype(BF16).reshape(group, rows, piece)
        return carry

    lax.fori_loop(0, 2 * half_groups, owner, 0)

    def place(n, rx, ry, sz, twin):
        sx = 1 - cx if rx else cx
        sy = 1 - cy if ry else cy
        inner, far = (sx, ry) if n % 2 == 0 else (sy, rx)
        at = 4 * chips_z + 4 * sz + 2 * (n % 2) + twin if far else 4 * sz + 2 * (n % 2) + twin
        return outs[at].at[inner, n // 2]

    def source(rx, ry, sz):
        sx = 1 - cx if rx else cx
        sy = 1 - cy if ry else cy
        return sz * 4 + sy * 2 + sx

    hops = (chip + 1 - 2 * cx, chip + 2 - 4 * cy, chip + 4, chip - 4)

    def hop_copy(kind, n, rx, ry, sz, mine):
        src = source(rx, ry, sz)
        there = (n, 1 - rx if kind == 0 else rx, 1 - ry if kind == 1 else ry, sz, 0)
        tx, ty = there[1], there[2]
        inner = (1 - cx if rx else cx) if n % 2 == 0 else (1 - cy if ry else cy)
        far = ty if n % 2 == 0 else tx
        at = 4 * chips_z + 4 * sz + 2 * (n % 2) if far else 4 * sz + 2 * (n % 2)
        return pltpu.make_async_remote_copy(
            src_ref=own.at[n] if mine else place(n, rx, ry, sz, 0), dst_ref=outs[at].at[inner, n // 2],
            send_sem=sp_send.at[n, kind, src], recv_sem=sp_recv.at[n, src],
            device_id=(2 * hops[kind] + core,), device_id_type=MESH)

    def arrival(n, rx, ry, sz):
        return pltpu.make_async_remote_copy(
            src_ref=own.at[n], dst_ref=place(n, rx, ry, sz, 0), send_sem=sp_send.at[n, 0, source(rx, ry, sz)],
            recv_sem=sp_recv.at[n, source(rx, ry, sz)], device_id=(me,), device_id_type=MESH)

    def twin_copy(n, rx, ry, sz, mine):
        src = source(rx, ry, sz)
        return pltpu.make_async_remote_copy(
            src_ref=own.at[n] if mine else place(n, rx, ry, sz, 0), dst_ref=place(n, rx, ry, sz, 1),
            send_sem=tw_send.at[n, src], recv_sem=tw_recv.at[n, src], device_id=(partner,), device_id_type=MESH)

    def own_sends(n, z):
        kinds = [0 if n % 2 == 0 else 1]
        if z < FIRST:
            kinds.append(1 if n % 2 == 0 else 0)
        return kinds + ([2] if z < chips_z - 1 else []) + ([3] if z > 0 else [])

    def at_z(fn):
        for z in range(chips_z):
            pl.when(cz == z)(functools.partial(fn, z))

    def split(code):
        return code // 10000, (code // 1000 % 10, code // 100 % 10, code // 10 % 10, code % 10)

    for n in range(QUARTERS):
        acc1[...] = jnp.zeros_like(acc1)
        acc2[...] = jnp.zeros_like(acc2)

        def products(gi, carry):
            for b in range(group):
                k = gi * group + b
                acc1[...] += mm(rh[k], ss[n, k], TN).astype(BF16).astype(F32)
                acc2[...] += mm(aa[n, k], re[k], TN).astype(BF16).astype(F32)
            return carry

        lax.fori_loop(0, 2 * half_groups, products, 0)
        for cb in range(piece // 128):
            own[n, cb * d:(cb + 1) * d, :] = acc1[:, cb * 128:(cb + 1) * 128].astype(BF16)
        off = (piece // 128) * d
        for lb in range(d // 128):
            own[n, off + lb * piece:off + (lb + 1) * piece, :] = acc2[:, lb * 128:(lb + 1) * 128].astype(BF16)

        def start_own(z, n=n):
            for kind in own_sends(n, z):
                hop_copy(kind, n, 0, 0, z, True).start()
            twin_copy(n, 0, 0, z, True).start()
            pltpu.make_async_copy(own.at[n], place(n, 0, 0, z, 0), own_sem.at[n]).start()

        at_z(start_own)

    def relay(z):
        for code in RELAYS[z]:
            kind, (n, rx, ry, sz) = split(code)
            if kind == 0:
                arrival(n, rx, ry, sz).wait_recv()
                twin_copy(n, rx, ry, sz, False).start()
            else:
                hop_copy(kind - 1, n, rx, ry, sz, False).start()

    at_z(relay)

    def sent(l, carry):
        @pl.when(l != chip)
        def _():
            h_copy(l).wait_send()
            e_copy(l).wait_send()

        return carry

    lax.fori_loop(0, layers, sent, 0)
    h_swap.wait_send()
    e_swap.wait_send()

    def drain(z):
        for n in range(QUARTERS):
            for kind in own_sends(n, z):
                hop_copy(kind, n, 0, 0, z, True).wait_send()
            twin_copy(n, 0, 0, z, True).wait_send()
            pltpu.make_async_copy(own.at[n], place(n, 0, 0, z, 0), own_sem.at[n]).wait()
            twin_copy(n, 0, 0, z, True).wait_recv()
        for code in RELAYS[z]:
            kind, (n, rx, ry, sz) = split(code)
            if kind == 0:
                twin_copy(n, rx, ry, sz, False).wait()
            else:
                hop_copy(kind - 1, n, rx, ry, sz, False).wait_send()

    at_z(drain)


def local_grads(w_in, w_out, x, y, n_dev):
    layers, d, hid = w_in.shape
    rows = x.shape[0]
    hc = hid // 2
    piece = hc // QUARTERS
    g_rows = (piece // 128) * d + (d // 128) * piece
    dims = (n_dev, layers, rows, d, hid)
    n_out = n_dev // 2 + 4 * FIRST
    flops = 2 * rows * d * hid * layers * 4 + 2 * rows * n_dev * d * hc * 4
    return pl.pallas_call(
        functools.partial(grads_kernel, dims),
        out_shape=[jax.ShapeDtypeStruct((2, QUARTERS // 2, g_rows, 128), BF16)] * n_out,
        in_specs=[pl.BlockSpec(memory_space=pl.ANY)] * 2 + [pl.BlockSpec(memory_space=pltpu.VMEM)] * 2,
        out_specs=[pl.BlockSpec(memory_space=pl.ANY)] * n_out,
        scratch_shapes=[
            pltpu.VMEM((SLOTS, d, hc), F32),
            pltpu.VMEM((SLOTS, hc, d), F32),
            pltpu.VMEM((2 * CACHED, d, hc), BF16),
            pltpu.VMEM((2 * CACHED, hc, d), BF16),
            pltpu.VMEM((2 * layers, rows, hc), F32),
            pltpu.VMEM((layers, rows, d), BF16),
            pltpu.VMEM((layers, rows, d), BF16),
            pltpu.VMEM((rows, d), F32),
            pltpu.VMEM((n_dev, rows, d), BF16),
            pltpu.VMEM((n_dev, rows, d), BF16),
            pltpu.VMEM((d, hc), BF16),
            pltpu.VMEM((hc, d), BF16),
            pltpu.VMEM((QUARTERS, n_dev, rows, piece), BF16),
            pltpu.VMEM((QUARTERS, n_dev, rows, piece), BF16),
            pltpu.VMEM((d, piece), F32),
            pltpu.VMEM((piece, d), F32),
            pltpu.VMEM((QUARTERS, g_rows, 128), BF16),
            pltpu.SemaphoreType.DMA((SLOTS,)),
            pltpu.SemaphoreType.DMA((SLOTS,)),
            pltpu.SemaphoreType.DMA((layers,)),
            pltpu.SemaphoreType.DMA((layers,)),
            pltpu.SemaphoreType.DMA((layers,)),
            pltpu.SemaphoreType.DMA((layers,)),
            pltpu.SemaphoreType.DMA((2,)),
            pltpu.SemaphoreType.DMA((2,)),
            pltpu.SemaphoreType.DMA((QUARTERS, 4, n_dev // 2)),
            pltpu.SemaphoreType.DMA((QUARTERS, n_dev // 2)),
            pltpu.SemaphoreType.DMA((QUARTERS, n_dev // 2)),
            pltpu.SemaphoreType.DMA((QUARTERS, n_dev // 2)),
            pltpu.SemaphoreType.DMA((QUARTERS,)),
        ],
        compiler_params=pltpu.CompilerParams(collective_id=0, has_side_effects=True, vmem_limit_bytes=VMEM_LIMIT),
        cost_estimate=pl.CostEstimate(flops=flops, bytes_accessed=4 * w_in.size * 4, transcendentals=0),
        name="local_grads",
    )(w_in, w_out, x, y)


def update_kernel(dims, group, last, *refs):
    layers, _, d, piece = dims
    step_size = LR_SCALE / layers
    chunk = 2 * piece
    steps = 16
    w1, m1, w2, m2, h_in = refs[:5]
    sums = refs[5:13]
    refs = refs[13:]
    if group:
        refs = refs[4:]
    if last:
        y_ref, refs = refs[0], refs[1:]
    w1o, w2o, m1o, m2o, h_out = refs[:5]
    if last:
        loss_ref = refs[5]
    bw1, bm1, bw2, bm2, gbuf, in_sem, out_sem, gsem, nb1, nb2, hb_ref = refs[-11:]
    slots = bw1.shape[0]

    me = lax.axis_index("data")
    chip, core = me // 2, me % 2
    cx, cy = chip % 2, (chip // 2) % 2

    def tile1(ref, t):
        return ref.at[4 * group + t // 4, :, pl.ds(pl.multiple_of((t % 4) * chunk, 128), chunk)]

    def tile2(ref, t):
        return ref.at[4 * group + t // 4, pl.ds(pl.multiple_of((t % 4) * chunk, 8), chunk), :]

    def reads(t, slot):
        return [pltpu.make_async_copy(src, buf.at[slot], in_sem.at[i, slot]) for i, (src, buf) in enumerate(
            ((tile1(w1, t), bw1), (tile1(m1, t), bm1), (tile2(w2, t), bw2), (tile2(m2, t), bm2)))]

    def writes(t, slot):
        return [pltpu.make_async_copy(buf.at[slot], dst, out_sem.at[i, slot]) for i, (dst, buf) in enumerate(
            ((tile1(w1o, t), bw1), (tile1(m1o, t), bm1), (tile2(w2o, t), bw2), (tile2(m2o, t), bm2)))]

    def fetch(t, slot):
        for copy in reads(t, slot):
            copy.start()
        layer, part = t // 4, t % 4
        sx, sy, half, q = layer % 2, layer // 2, part // 2, part % 2
        for par, inner, far in ((0, sx, sy != cy), (1, sy, sx != cx)):
            for is_far in (0, 1):
                for twin in (0, 1):
                    hit = jnp.logical_and(far == bool(is_far), (half != core) == bool(twin))

                    @pl.when(hit)
                    def _(par=par, inner=inner, is_far=is_far, twin=twin):
                        pltpu.make_async_copy(sums[4 * is_far + 2 * par + twin].at[inner, q], gbuf.at[slot, par], gsem.at[par, slot]).start()

    for t in range(AHEAD):
        fetch(t, t)
    h_out[...] = h_in[...].astype(F32)
    off = (piece // 128) * d

    def body(t, carry):
        slot = t % slots

        @pl.when(t % 4 == 0)
        def _():
            hb_ref[...] = h_out[...].astype(BF16)

        for copy in reads(t, slot):
            copy.wait()
        for par in range(2):
            pltpu.make_async_copy(sums[0].at[0, 0], gbuf.at[slot, par], gsem.at[par, slot]).wait()
            for cb in range(piece // 128):
                cols = slice(par * piece + cb * 128, par * piece + (cb + 1) * 128)
                mn = MOMENTUM * bm1[slot, :, cols] + gbuf[slot, par, cb * d:(cb + 1) * d, :].astype(F32)
                wn = bw1[slot, :, cols] - step_size * mn
                bm1[slot, :, cols] = mn
                bw1[slot, :, cols] = wn
                nb1[:, cols] = wn.astype(BF16)
            hid_rows = slice(par * piece, (par + 1) * piece)
            for lb in range(d // 128):
                cols = slice(lb * 128, (lb + 1) * 128)
                mn = MOMENTUM * bm2[slot, hid_rows, cols] + gbuf[slot, par, off + lb * piece:off + (lb + 1) * piece, :].astype(F32)
                wn = bw2[slot, hid_rows, cols] - step_size * mn
                bm2[slot, hid_rows, cols] = mn
                bw2[slot, hid_rows, cols] = wn
                nb2[hid_rows, cols] = wn.astype(BF16)
        for copy in writes(t, slot):
            copy.start()

        @pl.when(t + AHEAD < steps)
        def _():
            nslot = (t + AHEAD) % slots

            @pl.when(t + AHEAD >= slots)
            def _():
                for copy in writes(t + AHEAD - slots, nslot):
                    copy.wait()

            fetch(t + AHEAD, nslot)

        z = mm(hb_ref[...], nb1[...])
        h_out[...] += mm(gelu(z).astype(BF16), nb2[...])
        return carry

    lax.fori_loop(0, steps, body, 0)
    for t in range(steps - slots, steps):
        for copy in writes(t, t % slots):
            copy.wait()
    if last:
        diff = h_out[...] - y_ref[...].astype(F32)
        loss_ref[...] = jnp.sum(diff * diff, axis=-1) / (2 * d)


def update(group, w_in, m_in, w_out, m_out, h, sums, prev, y):
    layers, d, hid = w_in.shape
    rows = h.shape[0]
    piece = hid // 2 // QUARTERS
    chunk = 2 * piece
    last = group == layers // 4 - 1
    whole = pl.BlockSpec(memory_space=pltpu.VMEM)
    any_spec = pl.BlockSpec(memory_space=pl.ANY)
    args = [w_in, m_in, w_out, m_out, h, *sums, *prev] + ([y] if last else [])
    in_specs = [any_spec] * 4 + [whole] + [any_spec] * (8 + len(prev)) + ([whole] if last else [])
    out_specs = [any_spec] * 4 + [whole]
    out_shape = [jax.ShapeDtypeStruct(a.shape, F32) for a in (w_in, w_out, m_in, m_out, h)]
    if last:
        out_specs.append(whole)
        out_shape.append(jax.ShapeDtypeStruct((rows,), F32))
    n_el = 2 * w_in.size // 4
    slots = 7
    return pl.pallas_call(
        functools.partial(update_kernel, (layers, rows, d, piece), group, last),
        in_specs=in_specs,
        out_specs=out_specs,
        out_shape=out_shape,
        scratch_shapes=[
            pltpu.VMEM((slots, d, chunk), F32),
            pltpu.VMEM((slots, d, chunk), F32),
            pltpu.VMEM((slots, chunk, d), F32),
            pltpu.VMEM((slots, chunk, d), F32),
            pltpu.VMEM((slots, 2, *sums[0].shape[2:]), BF16),
            pltpu.SemaphoreType.DMA((4, slots)),
            pltpu.SemaphoreType.DMA((4, slots)),
            pltpu.SemaphoreType.DMA((2, slots)),
            pltpu.VMEM((d, chunk), BF16),
            pltpu.VMEM((chunk, d), BF16),
            pltpu.VMEM((rows, d), BF16),
        ],
        input_output_aliases={13 + i: i for i in range(len(prev))},
        compiler_params=pltpu.CompilerParams(vmem_limit_bytes=VMEM_LIMIT),
        cost_estimate=pl.CostEstimate(flops=5 * 10**10, bytes_accessed=18 * n_el, transcendentals=0),
    )(*args)


def solution(mesh):
    n_dev = mesh.shape["data"]
    rows_spec = P("data", None)
    swap = {axis: [(i, i ^ bit) for i in range(n_dev)] for axis, bit in (("core", 1), ("x", 2), ("y", 4))}

    def send(array, axis):
        return lax.ppermute(array, "data", swap[axis])

    def local_steps(w_in, w_out, mom_in, mom_out, x_first, y_first, x_second, y_second):
        groups = w_in.shape[0] // 4
        sums = local_grads(w_in, w_out, x_first, y_first, n_dev)
        near = [list(sums[4 * g:4 * g + 4]) for g in range(groups)]
        far = [list(sums[4 * (groups + g):4 * (groups + g) + 4]) for g in range(FIRST)]
        for g in range(FIRST, groups):
            from_y = send(near[g][0], "y")
            from_x = send(near[g][2], "x")
            far.append([from_y, send(from_y, "core"), from_x, send(from_x, "core")])
        prev, h = [], x_second
        for g in range(groups):
            outs = update(g, w_in, mom_in, w_out, mom_out, h, near[g] + far[g], prev, y_second)
            prev, h = list(outs[:4]), outs[4]
        w_in_new, w_out_new, mom_in_new, mom_out_new = prev
        return w_in_new, w_out_new, mom_in_new, mom_out_new, outs[5], h

    return jax.shard_map(
        local_steps, mesh=mesh,
        in_specs=(P(), P(), P(), P(), rows_spec, rows_spec, rows_spec, rows_spec),
        out_specs=(P(), P(), P(), P(), P("data"), rows_spec), check_vma=False)
```

time: 558 us -> 556 us (level); the launches traced: 557 us -> 548 us
  Pallas kernels: 555 us -> 450 us
  waiting for transfers between devices: 0 us -> 87.6 us
  starting transfers between devices: 0 us -> 9.48 us
    pallas_call x2 -> x5, Pallas kernels: 555 us -> 450 us  [the longest x1 250 us: local_grads(): pl.pallas_call(functools.partial(grads_kernel, dims), out_shape=[jax.Shap...]
    ppermute x0 -> x12, waiting for transfers between devices: none -> 87.6 us  [send(): return lax.ppermute(array, 'data', swap[axis])]
    ppermute x0 -> x12, starting transfers between devices: none -> 9.48 us  [send(): return lax.ppermute(array, 'data', swap[axis])]
  transfers between devices with their start and end apart: 0 -> 12, of which waited for: 0 -> 2; matrix products, arithmetic and copies ran while one was open for 0% -> 0% of each run, Pallas kernels for 0% -> 27%
where the time goes in v3:
time: 556 us; the launch traced here: 548 us
  Pallas kernels  450 us (81%)
  waiting for transfers between devices  87.6 us (16%)
  starting transfers between devices  9.48 us (2%)
    pallas_call x1, Pallas kernels, local_grads(): pl.pallas_call(functools.partial(grads_kernel, dims), out_shape=[jax.Shap...  250 us
    pallas_call x4, Pallas kernels, update(): pl.pallas_call(functools.partial(update_kernel, (layers, rows, d, piece),...  200 us
    ppermute x12, waiting for transfers between devices, send(): return lax.ppermute(array, 'data', swap[axis])  87.6 us
  transfers between devices with their start and end apart: 12, of which 2 were waited for; matrix products, arithmetic and copies ran while one was open for 0% of the time, Pallas kernels for 27%

profile of v3, /device:TPU:0, one launch (start us, length us, event | category | flops | bytes accessed | tf_op | source)
XLA Modules:
  0.0 547.8 jit_solution(16676968407958754004)
XLA Ops:
  0.6 250.0 %local_grads.1 = (bf16[2,2,2048,128]{3,2,1,0:T(8,128)(2,1)}, bf16[2,2,2048,128]{3,2,1,0:T(8,128)(2,1)}, bf16[2,2,2048,128]{3,2,1,0:T(8,128)(2,1)}, bf16[2,2,2048...) custom-call(f32[16,512,2048]{2,1,0:T(8,128)} %refs_0_.7, ...), custom_call_target="tpu_custom_call" | custom-call | flops 17179869184 | bytes 268435456 | tf_op jit(solution)/shard_map/local_grads/pallas_call | solution.py:418
  250.7 4.0 collective-permute-start
  254.6 0.1 collective-permute-start.2
  254.7 0.1 collective-permute-start.4
  254.8 1.9 collective-permute-start.6
  256.7 0.1 collective-permute-start.10
  256.8 44.6 %collective-permute-done.refs_9_ = bf16[2,2,2048,128]{3,2,1,0:T(8,128)(2,1)} collective-permute-done((bf16[2,2,2048,128]{3,2,1,0:T(8,128)(2,1)}, bf16[2,2,2048,128]{3,2,1,0:T(8,128)(2,1)}, u32[]{:S(2)}, u32[]{:S(2)}) %collective-permute-start) | collective-permute-done | bytes 2097184 | tf_op jit(solution)/shard_map/ppermute | solution.py:616
  301.4 2.0 collective-permute-start.8
  303.4 0.0 collective-permute-done.2.refs_11_
  303.4 0.0 collective-permute-start.1
  303.4 42.9 %collective-permute-done.4.refs_9_ = bf16[2,2,2048,128]{3,2,1,0:T(8,128)(2,1)} collective-permute-done((bf16[2,2,2048,128]{3,2,1,0:T(8,128)(2,1)}, bf16[2,2,2048,128]{3,2,1,0:T(8,128)(2,1)}, u32[]{:S(2)}, u32[]{:S(2)}) %collective-permute-start.4) | collective-permute-done | bytes 2097184 | tf_op jit(solution)/shard_map/ppermute | solution.py:616
  346.4 0.0 collective-permute-start.3
  346.4 49.9 %shard_map.127 = (f32[16,512,2048]{2,1,0:T(8,128)}, f32[16,2048,512]{2,1,0:T(8,128)}, f32[16,512,2048]{2,1,0:T(8,128)}, f32[16,2048,512]{2,1,0:T(8,128)}, f32[64,512]{1,0:T(8,128)}) custom-call(f32[16,512,2048]{2,1,0:T(8,128)} %refs_0_.7, f32[16,512,2048]{2,1,0:T(8,128)} %refs_1_.7, f32[16,2048,512]{2,1,0:T(8,128)} %refs_2_.7, f32[16,2048,512]{2,1,0:T(8,128)} %refs_3_.7, ...), custom_call_target="tpu_custom_call" | custom-call | flops 49999998976 | bytes 150994944 | tf_op jit(solution)/shard_map/pallas_call | solution.py:586
  396.3 0.0 collective-permute-done.6.refs_11_
  396.3 0.7 collective-permute-start.5
  397.0 0.0 collective-permute-done.10.refs_11_
  397.0 0.1 collective-permute-start.7
  397.1 0.0 collective-permute-done.8.refs_9_
  397.1 0.4 collective-permute-start.11
  397.5 0.0 collective-permute-done.1.refs_10_
  397.5 0.1 collective-permute-start.9
  397.6 0.0 collective-permute-done.3.refs_12_
  397.6 50.0 %shard_map.128 = (f32[16,512,2048]{2,1,0:T(8,128)}, f32[16,2048,512]{2,1,0:T(8,128)}, f32[16,512,2048]{2,1,0:T(8,128)}, f32[16,2048,512]{2,1,0:T(8,128)}, f32[64,512]{1,0:T(8,128)}) custom-call(f32[16,512,2048]{2,1,0:T(8,128)} %refs_0_.7, f32[16,512,2048]{2,1,0:T(8,128)} %refs_1_.7, ...), custom_call_target="tpu_custom_call", output_to_operand_aliasing={{0}: (13, {}), {1}: (14, {}), {2}: (15, {}), {3}: (16, {})} | custom-call | flops 49999998976 | bytes 150994944 | tf_op jit(solution)/shard_map/pallas_call | solution.py:586
  447.6 0.0 collective-permute-done.5.refs_10_
  447.6 0.0 collective-permute-done.7.refs_12_
  447.6 50.0 %shard_map.129 = (f32[16,512,2048]{2,1,0:T(8,128)}, f32[16,2048,512]{2,1,0:T(8,128)}, f32[16,512,2048]{2,1,0:T(8,128)}, f32[16,2048,512]{2,1,0:T(8,128)}, f32[64,512]{1,0:T(8,128)}) custom-call(f32[16,512,2048]{2,1,0:T(8,128)} %refs_0_.7, f32[16,512,2048]{2,1,0:T(8,128)} %refs_1_.7, ...), custom_call_target="tpu_custom_call", output_to_operand_aliasing={{0}: (13, {}), {1}: (14, {}), {2}: (15, {}), {3}: (16, {})} | custom-call | flops 49999998976 | bytes 150994944 | tf_op jit(solution)/shard_map/pallas_call | solution.py:586
  497.6 0.0 collective-permute-done.11.refs_12_
  497.6 0.0 collective-permute-done.9.refs_10_
  497.6 50.0 %shard_map.130 = (f32[16,512,2048]{2,1,0:T(8,128)}, f32[16,2048,512]{2,1,0:T(8,128)}, f32[16,512,2048]{2,1,0:T(8,128)}, f32[16,2048,512]{2,1,0:T(8,128)}, f32[64,512]{1,0:T(8,128)}, /*index=5*/f32[64]{0:T(128)}) custom-call(f32[16,512,2048]{2,1,0:T(8,128)} %refs_0_.7, ...), custom_call_target="tpu_custom_call", output_to_operand_aliasing={{0}: (13, {}), {1}: (14, {}), {2}: (15, {}), {3}: (16, {})} | custom-call | flops 49999998976 | bytes 150994944 | tf_op jit(solution)/shard_map/pallas_call | solution.py:586
Async XLA Ops:
  250.7 50.8 %collective-permute-start = (bf16[2,2,2048,128]{3,2,1,0:T(8,128)(2,1)}, bf16[2,2,2048,128]{3,2,1,0:T(8,128)(2,1)}, u32[]{:S(2)}, u32[]{:S(2)}) collective-permute-start(bf16[2,2,2048,128]{3,2,1,0:T(8,128)(2,1)} %get-tuple-element.56.refs_5_), channel_id=1, source_target_pairs={{0,4},{1,5},{2,6},{3,7},{4,0},{5,1},{6,2},{7,3},{8,12},{9,13},{10,... | collective-permute-start | bytes 6291464 | tf_op jit(solution)/shard_map/ppermute | solution.py:616
  254.6 48.8 %collective-permute-start.2 = (bf16[2,2,2048,128]{3,2,1,0:T(8,128)(2,1)}, bf16[2,2,2048,128]{3,2,1,0:T(8,128)(2,1)}, u32[]{:S(2)}, u32[]{:S(2)}) collective-permute-start(bf16[2,2,2048,128]{3,2,1,0:T(8,128)(2,1)} %get-tuple-element.58.refs_7_), channel_id=1, source_target_pairs={{0,2},{1,3},{2,0},{3,1},{4,6},{5,7},{6,4},{7,5},{8,10},{9,11},{10,... | collective-permute-start | bytes 6291464 | tf_op jit(solution)/shard_map/ppermute | solution.py:616
  254.7 91.7 %collective-permute-start.4 = (bf16[2,2,2048,128]{3,2,1,0:T(8,128)(2,1)}, bf16[2,2,2048,128]{3,2,1,0:T(8,128)(2,1)}, u32[]{:S(2)}, u32[]{:S(2)}) collective-permute-start(bf16[2,2,2048,128]{3,2,1,0:T(8,128)(2,1)} %get-tuple-element.65.refs_5_), channel_id=1, source_target_pairs={{0,4},{1,5},{2,6},{3,7},{4,0},{5,1},{6,2},{7,3},{8,12},{9,13},{10,... | collective-permute-start | bytes 6291464 | tf_op jit(solution)/shard_map/ppermute | solution.py:616
  254.8 141.5 %collective-permute-start.6 = (bf16[2,2,2048,128]{3,2,1,0:T(8,128)(2,1)}, bf16[2,2,2048,128]{3,2,1,0:T(8,128)(2,1)}, u32[]{:S(2)}, u32[]{:S(2)}) collective-permute-start(bf16[2,2,2048,128]{3,2,1,0:T(8,128)(2,1)} %get-tuple-element.67.refs_7_), channel_id=1, source_target_pairs={{0,2},{1,3},{2,0},{3,1},{4,6},{5,7},{6,4},{7,5},{8,10},{9,11},{10,... | collective-permute-start | bytes 6291464 | tf_op jit(solution)/shard_map/ppermute | solution.py:616
  256.7 140.3 %collective-permute-start.10 = (bf16[2,2,2048,128]{3,2,1,0:T(8,128)(2,1)}, bf16[2,2,2048,128]{3,2,1,0:T(8,128)(2,1)}, u32[]{:S(2)}, u32[]{:S(2)}) collective-permute-start(bf16[2,2,2048,128]{3,2,1,0:T(8,128)(2,1)} %get-tuple-element.76.refs_7_), channel_id=1, source_target_pairs={{0,2},{1,3},{2,0},{3,1},{4,6},{5,7},{6,4},{7,5},{8,10},{9,11},{10,... | collective-permute-start | bytes 6291464 | tf_op jit(solution)/shard_map/ppermute | solution.py:616
  301.4 95.7 %collective-permute-start.8 = (bf16[2,2,2048,128]{3,2,1,0:T(8,128)(2,1)}, bf16[2,2,2048,128]{3,2,1,0:T(8,128)(2,1)}, u32[]{:S(2)}, u32[]{:S(2)}) collective-permute-start(bf16[2,2,2048,128]{3,2,1,0:T(8,128)(2,1)} %get-tuple-element.74.refs_5_), channel_id=1, source_target_pairs={{0,4},{1,5},{2,6},{3,7},{4,0},{5,1},{6,2},{7,3},{8,12},{9,13},{10,... | collective-permute-start | bytes 6291464 | tf_op jit(solution)/shard_map/ppermute | solution.py:616
  303.4 94.1 %collective-permute-start.1 = (bf16[2,2,2048,128]{3,2,1,0:T(8,128)(2,1)}, bf16[2,2,2048,128]{3,2,1,0:T(8,128)(2,1)}, u32[]{:S(2)}, u32[]{:S(2)}) collective-permute-start(bf16[2,2,2048,128]{3,2,1,0:T(8,128)(2,1)} %collective-permute-done.refs_9_), channel_id=1, source_target_pairs={{0,1},{1,0},{2,3},{3,2},{4,5},{5,4},{6,7},{7,6},{8,9},{9,8},{10,11... | collective-permute-start | bytes 6291464 | tf_op jit(solution)/shard_map/ppermute | solution.py:616
  346.4 51.3 %collective-permute-start.3 = (bf16[2,2,2048,128]{3,2,1,0:T(8,128)(2,1)}, bf16[2,2,2048,128]{3,2,1,0:T(8,128)(2,1)}, u32[]{:S(2)}, u32[]{:S(2)}) collective-permute-start(bf16[2,2,2048,128]{3,2,1,0:T(8,128)(2,1)} %collective-permute-done.2.refs_11_), channel_id=1, source_target_pairs={{0,1},{1,0},{2,3},{3,2},{4,5},{5,4},{6,7},{7,6},{8,9},{9,8},{10,11... | collective-permute-start | bytes 6291464 | tf_op jit(solution)/shard_map/ppermute | solution.py:616
  396.3 51.3 %collective-permute-start.5 = (bf16[2,2,2048,128]{3,2,1,0:T(8,128)(2,1)}, bf16[2,2,2048,128]{3,2,1,0:T(8,128)(2,1)}, u32[]{:S(2)}, u32[]{:S(2)}) collective-permute-start(bf16[2,2,2048,128]{3,2,1,0:T(8,128)(2,1)} %collective-permute-done.4.refs_9_), channel_id=1, source_target_pairs={{0,1},{1,0},{2,3},{3,2},{4,5},{5,4},{6,7},{7,6},{8,9},{9,8},{10,11... | collective-permute-start | bytes 6291464 | tf_op jit(solution)/shard_map/ppermute | solution.py:616
  397.0 50.6 %collective-permute-start.7 = (bf16[2,2,2048,128]{3,2,1,0:T(8,128)(2,1)}, bf16[2,2,2048,128]{3,2,1,0:T(8,128)(2,1)}, u32[]{:S(2)}, u32[]{:S(2)}) collective-permute-start(bf16[2,2,2048,128]{3,2,1,0:T(8,128)(2,1)} %collective-permute-done.6.refs_11_), channel_id=1, source_target_pairs={{0,1},{1,0},{2,3},{3,2},{4,5},{5,4},{6,7},{7,6},{8,9},{9,8},{10,11... | collective-permute-start | bytes 6291464 | tf_op jit(solution)/shard_map/ppermute | solution.py:616
  397.1 100.5 %collective-permute-start.11 = (bf16[2,2,2048,128]{3,2,1,0:T(8,128)(2,1)}, bf16[2,2,2048,128]{3,2,1,0:T(8,128)(2,1)}, u32[]{:S(2)}, u32[]{:S(2)}) collective-permute-start(bf16[2,2,2048,128]{3,2,1,0:T(8,128)(2,1)} %collective-permute-done.10.refs_11_), channel_id=1, source_target_pairs={{0,1},{1,0},{2,3},{3,2},{4,5},{5,4},{6,7},{7,6},{8,9},{9,8},{10,11... | collective-permute-start | bytes 6291464 | tf_op jit(solution)/shard_map/ppermute | solution.py:616
  397.5 100.1 %collective-permute-start.9 = (bf16[2,2,2048,128]{3,2,1,0:T(8,128)(2,1)}, bf16[2,2,2048,128]{3,2,1,0:T(8,128)(2,1)}, u32[]{:S(2)}, u32[]{:S(2)}) collective-permute-start(bf16[2,2,2048,128]{3,2,1,0:T(8,128)(2,1)} %collective-permute-done.8.refs_9_), channel_id=1, source_target_pairs={{0,1},{1,0},{2,3},{3,2},{4,5},{5,4},{6,7},{7,6},{8,9},{9,8},{10,11... | collective-permute-start | bytes 6291464 | tf_op jit(solution)/shard_map/ppermute | solution.py:616

commit v4 on v3

--- a/solution.py
+++ b/solution.py
@@ -18,26 +18,53 @@
 SLOTS = 4
 QUARTERS = 4
 AHEAD = 4
-CACHED = 4
+CACHED = 6
 FIRST = 1
 RELAYS = (
-    (100, 10, 1, 1100, 1010, 1001, 2100, 2010, 2001, 10001, 21001, 3100, 3010, 3001, 12001, 23001, 101, 1011, 2,
-     10002, 20100, 2101, 3011, 1002, 11010, 21002, 102, 110, 3, 10003, 22100, 1110, 1012, 1003, 13010, 21003, 103,
-     2110, 2003, 12003, 3110, 1013, 3003, 23003, 2103, 2002, 12002, 3013, 3002, 23002, 2102, 3012),
-    (0, 101, 2, 10000, 1011, 20000, 1000, 2101, 1002, 10002, 3011, 21000, 2000, 100, 2002, 30000, 40002, 11000, 10,
-     21002, 3000, 102, 3002, 31000, 41002, 12000, 1010, 22000, 1100, 3, 32000, 40003, 10003, 1012, 2100, 1003,
-     21003, 33000, 41003, 12002, 2010, 20100, 103, 2003, 42003, 12003, 1013, 2102, 3003, 23003, 43003, 13000, 110,
-     23000, 2103, 42002, 11010, 3013, 23002, 3100, 43002, 3010, 13010, 22100, 1110, 3012, 3110, 2110),
-    (1, 102, 3, 10001, 1012, 1001, 2102, 1003, 21001, 10003, 3012, 21003, 2001, 101, 2003, 30001, 40003, 12001,
-     1011, 3001, 103, 3003, 23001, 31001, 41003, 12003, 1013, 0, 2101, 20000, 30000, 42003, 10000, 3011, 1000,
-     2103, 21000, 31000, 43003, 11000, 10, 2000, 100, 22000, 32000, 12000, 1010, 20100, 3000, 1100, 33000, 11010,
-     2010, 23000, 2100, 32001, 13000, 110, 22100, 1110, 33001, 3010, 13010, 23003, 3100, 2110, 3110, 3013),
-    (2, 103, 10002, 1013, 1002, 2103, 21002, 3013, 2002, 102, 12002, 1012, 3002, 23002, 2102, 1, 10001, 3012, 1001,
-     21001, 101, 0, 10000, 20000, 1011, 1000, 21000, 11000, 100, 10, 20100, 2000, 12000, 1100, 1010, 22000, 11010,
-     3000, 2100, 110, 13000, 23000, 2001, 1110, 2010, 22100, 12001, 3001, 3100, 3010, 23001, 13010, 2110, 2101,
-     3011, 3110),
+    (
+        (30000, 10000, 20000),
+        (31000, 11000, 21000),
+        (32000,),
+        (),
+        (100, 10, 1, 10001, 20100, 1100, 1010, 1001, 33000, 12000, 21001, 101, 110, 2, 10002, 22000, 2100, 1011, 1002,
+         13000, 21002, 102, 2010, 3, 10003, 23000, 3100, 1012, 1003, 11010, 21003, 103, 3010, 2003, 12003, 22100, 1110,
+         1013, 3003, 13010, 23003, 2103, 2110, 2002, 12002, 3110, 3013, 3002, 23002, 2102, 2001, 12001, 3012, 3001,
+         23001, 2101, 3011),
+    ),
+    (
+        (30001, 40001, 10001),
+        (21001, 31001, 41001),
+        (),
+        (),
+        (0, 101, 2, 10000, 20000, 30000, 40002, 10002, 1011, 1000, 1002, 21000, 100, 31000, 41002, 11000, 10, 21002,
+         2000, 3, 102, 32000, 40003, 10003, 1010, 3000, 1003, 21003, 1100, 33000, 41003, 1012, 20100, 2003, 12003, 103,
+         32001, 42003, 12000, 1013, 3003, 23003, 2103, 33001, 43003, 11010, 110, 22000, 2002, 2100, 42002, 13000, 3013,
+         23000, 3002, 1110, 43002, 12002, 2010, 22100, 3100, 42001, 3010, 13010, 23002, 2102, 43001, 12001, 2110,
+         23001, 3110, 3012, 2101, 3011),
+    ),
+    (
+        (30002, 40002, 10002),
+        (21002, 31002, 41002),
+        (),
+        (),
+        (1, 102, 3, 10001, 30001, 40003, 10003, 1012, 23002, 1001, 1003, 21001, 101, 31001, 41003, 3012, 0, 2003,
+         10000, 20000, 103, 30000, 42003, 1011, 1000, 3003, 11000, 21000, 100, 31000, 43003, 10, 2000, 12000, 20100,
+         1100, 32000, 42002, 1010, 11010, 3000, 22000, 2100, 33000, 43002, 13000, 110, 2001, 23000, 1110, 32001, 12003,
+         2010, 3001, 22100, 3100, 33001, 3010, 13010, 21003, 2103, 32002, 12001, 2110, 23003, 3110, 33002, 12002, 1013,
+         23001, 2101, 3013, 2102, 3011),
+    ),
+    (
+        (40003, 10003),
+        (21003, 41003),
+        (42003, 12003),
+        (),
+        (2, 103, 10002, 1013, 23003, 1002, 21002, 102, 43003, 3013, 1, 10001, 2103, 1012, 1001, 21001, 101, 0, 10000,
+         20000, 1011, 1000, 21000, 11000, 100, 10, 20100, 2000, 12000, 1100, 1010, 22000, 11010, 3000, 2100, 110,
+         13000, 23000, 2001, 1110, 2010, 22100, 12001, 3001, 3100, 3010, 13010, 23001, 2002, 2110, 2101, 12002, 3002,
+         23002, 3110, 3011, 3012, 2102),
+    ),
 )
-VMEM_LIMIT = 62 * 1024 * 1024
+VMEM_LIMIT = 67043328
 
 NN = (((1,), (0,)), ((), ()))
 NT = (((1,), (1,)), ((), ()))
@@ -69,7 +96,7 @@
     chips_z = chips // 4
     n_out = 4 * chips_z + 4 * FIRST
     outs, rest = rest[:n_out], rest[n_out:]
-    (wb1, wb2, cw1, cw2, z_all, hb, eb, hcur, rh, re, ow1, ow2, aa, ss, acc1, acc2, own,
+    (wb1, wb2, cw1, cw2, z_all, hb, eb, hcur, rh, re, ow1, ow2, acc1, acc2, own,
      w1_sem, w2_sem, hs_sem, hr_sem, es_sem, er_sem, px_send, px_recv,
      sp_send, sp_recv, tw_send, tw_recv, own_sem) = rest
 
@@ -264,31 +291,6 @@
     h_swap.start()
     lax.fori_loop(0, chips, e_in, 0)
     e_swap.start()
-
-    group = 4
-    half_groups = chips // group
-
-    def owner(gi, carry):
-        half = (core + gi // half_groups) % 2
-
-        @pl.when(gi == half_groups)
-        def _():
-            h_swap.wait_recv()
-            e_swap.wait_recv()
-
-        base = half * chips + (gi % half_groups) * group
-        hg = rh[pl.ds(base, group)].reshape(group * rows, d)
-        eg = re[pl.ds(base, group)].reshape(group * rows, d)
-        for n in range(QUARTERS):
-            cols = slice(n * piece, (n + 1) * piece)
-            z = mm(hg, ow1[:, cols])
-            q = mm(eg, ow2[cols, :], NT)
-            a, slope = gelu_grad(z)
-            aa[n, pl.ds(base, group)] = a.astype(BF16).reshape(group, rows, piece)
-            ss[n, pl.ds(base, group)] = (slope * q).astype(BF16).reshape(group, rows, piece)
-        return carry
-
-    lax.fori_loop(0, 2 * half_groups, owner, 0)
 
     def place(n, rx, ry, sz, twin):
         sx = 1 - cx if rx else cx
@@ -327,12 +329,6 @@
             src_ref=own.at[n] if mine else place(n, rx, ry, sz, 0), dst_ref=place(n, rx, ry, sz, 1),
             send_sem=tw_send.at[n, src], recv_sem=tw_recv.at[n, src], device_id=(partner,), device_id_type=MESH)
 
-    def own_sends(n, z):
-        kinds = [0 if n % 2 == 0 else 1]
-        if z < FIRST:
-            kinds.append(1 if n % 2 == 0 else 0)
-        return kinds + ([2] if z < chips_z - 1 else []) + ([3] if z > 0 else [])
-
     def at_z(fn):
         for z in range(chips_z):
             pl.when(cz == z)(functools.partial(fn, z))
@@ -340,18 +336,46 @@
     def split(code):
         return code // 10000, (code // 1000 % 10, code // 100 % 10, code // 10 % 10, code % 10)
 
+    def act(z, code):
+        kind, block = split(code)
+        mine = block[1:] == (0, 0, z)
+        if kind:
+            hop_copy(kind - 1, *block, mine).start()
+        else:
+            arrival(*block).wait_recv()
+            twin_copy(*block, False).start()
+
+    group = 4
+    half_groups = chips // group
+
     for n in range(QUARTERS):
+        cols = slice(n * piece, (n + 1) * piece)
         acc1[...] = jnp.zeros_like(acc1)
         acc2[...] = jnp.zeros_like(acc2)
 
-        def products(gi, carry):
+        def owner(gi, carry, n=n, cols=cols):
+            half = (core + gi // half_groups) % 2
+            if n == 0:
+                @pl.when(gi == half_groups)
+                def _():
+                    h_swap.wait_recv()
+                    e_swap.wait_recv()
+
+            base = half * chips + (gi % half_groups) * group
+            hg = rh[pl.ds(base, group)].reshape(group * rows, d)
+            eg = re[pl.ds(base, group)].reshape(group * rows, d)
+            z = mm(hg, ow1[:, cols])
+            q = mm(eg, ow2[cols, :], NT)
+            a, slope = gelu_grad(z)
+            a = a.astype(BF16)
+            s = (slope * q).astype(BF16)
             for b in range(group):
-                k = gi * group + b
-                acc1[...] += mm(rh[k], ss[n, k], TN).astype(BF16).astype(F32)
-                acc2[...] += mm(aa[n, k], re[k], TN).astype(BF16).astype(F32)
+                own_rows = slice(b * rows, (b + 1) * rows)
+                acc1[...] += mm(rh[base + b], s[own_rows], TN).astype(BF16).astype(F32)
+                acc2[...] += mm(a[own_rows], re[base + b], TN).astype(BF16).astype(F32)
             return carry
 
-        lax.fori_loop(0, 2 * half_groups, products, 0)
+        lax.fori_loop(0, 2 * half_groups, owner, 0)
         for cb in range(piece // 128):
             own[n, cb * d:(cb + 1) * d, :] = acc1[:, cb * 128:(cb + 1) * 128].astype(BF16)
         off = (piece // 128) * d
@@ -359,21 +383,16 @@
             own[n, off + lb * piece:off + (lb + 1) * piece, :] = acc2[:, lb * 128:(lb + 1) * 128].astype(BF16)
 
         def start_own(z, n=n):
-            for kind in own_sends(n, z):
-                hop_copy(kind, n, 0, 0, z, True).start()
+            for code in RELAYS[z][n]:
+                act(z, code)
             twin_copy(n, 0, 0, z, True).start()
             pltpu.make_async_copy(own.at[n], place(n, 0, 0, z, 0), own_sem.at[n]).start()
 
         at_z(start_own)
 
     def relay(z):
-        for code in RELAYS[z]:
-            kind, (n, rx, ry, sz) = split(code)
-            if kind == 0:
-                arrival(n, rx, ry, sz).wait_recv()
-                twin_copy(n, rx, ry, sz, False).start()
-            else:
-                hop_copy(kind - 1, n, rx, ry, sz, False).start()
+        for code in RELAYS[z][QUARTERS]:
+            act(z, code)
 
     at_z(relay)
 
@@ -391,17 +410,14 @@
 
     def drain(z):
         for n in range(QUARTERS):
-            for kind in own_sends(n, z):
-                hop_copy(kind, n, 0, 0, z, True).wait_send()
-            twin_copy(n, 0, 0, z, True).wait_send()
+            twin_copy(n, 0, 0, z, True).wait()
             pltpu.make_async_copy(own.at[n], place(n, 0, 0, z, 0), own_sem.at[n]).wait()
-            twin_copy(n, 0, 0, z, True).wait_recv()
-        for code in RELAYS[z]:
-            kind, (n, rx, ry, sz) = split(code)
-            if kind == 0:
-                twin_copy(n, rx, ry, sz, False).wait()
+        for code in sum(RELAYS[z], ()):
+            kind, block = split(code)
+            if kind:
+                hop_copy(kind - 1, *block, block[1:] == (0, 0, z)).wait_send()
             else:
-                hop_copy(kind - 1, n, rx, ry, sz, False).wait_send()
+                twin_copy(*block, False).wait()
 
     at_z(drain)
 
@@ -433,8 +449,6 @@
             pltpu.VMEM((n_dev, rows, d), BF16),
             pltpu.VMEM((d, hc), BF16),
             pltpu.VMEM((hc, d), BF16),
-            pltpu.VMEM((QUARTERS, n_dev, rows, piece), BF16),
-            pltpu.VMEM((QUARTERS, n_dev, rows, piece), BF16),
             pltpu.VMEM((d, piece), F32),
             pltpu.VMEM((piece, d), F32),
             pltpu.VMEM((QUARTERS, g_rows, 128), BF16),

time: 556 us -> 548 us (0.986); the launches traced: 548 us -> 546 us
  no operation moved by 1% of the time
where the time goes in v4:
time: 548 us; the launch traced here: 546 us
  Pallas kernels  449 us (82%)
  waiting for transfers between devices  85.6 us (16%)
  starting transfers between devices  10.6 us (2%)
    pallas_call x1, Pallas kernels, local_grads(): pl.pallas_call(functools.partial(grads_kernel, dims), out_shape=[jax.Shap...  249 us
    pallas_call x4, Pallas kernels, update(): pl.pallas_call(functools.partial(update_kernel, (layers, rows, d, piece),...  200 us
    ppermute x12, waiting for transfers between devices, send(): return lax.ppermute(array, 'data', swap[axis])  85.6 us
  transfers between devices with their start and end apart: 12, of which 2 were waited for; matrix products, arithmetic and copies ran while one was open for 0% of the time, Pallas kernels for 27%

profile of v4, /device:TPU:0, one launch (start us, length us, event | category | flops | bytes accessed | tf_op | source)
XLA Modules:
  0.0 545.7 jit_solution(2565548699707472631)
XLA Ops:
  0.6 248.8 %local_grads.1 = (bf16[2,2,2048,128]{3,2,1,0:T(8,128)(2,1)}, bf16[2,2,2048,128]{3,2,1,0:T(8,128)(2,1)}, bf16[2,2,2048,128]{3,2,1,0:T(8,128)(2,1)}, bf16[2,2,2048...) custom-call(f32[16,512,2048]{2,1,0:T(8,128)} %refs_0_.7, ...), custom_call_target="tpu_custom_call" | custom-call | flops 17179869184 | bytes 268435456 | tf_op jit(solution)/shard_map/local_grads/pallas_call | solution.py:434
  249.5 3.1 collective-permute-start
  252.5 2.0 collective-permute-start.2
  254.6 0.1 collective-permute-start.4
  254.6 0.1 collective-permute-start.6
  254.7 1.9 collective-permute-start.10
  256.7 42.7 %collective-permute-done.refs_9_ = bf16[2,2,2048,128]{3,2,1,0:T(8,128)(2,1)} collective-permute-done((bf16[2,2,2048,128]{3,2,1,0:T(8,128)(2,1)}, bf16[2,2,2048,128]{3,2,1,0:T(8,128)(2,1)}, u32[]{:S(2)}, u32[]{:S(2)}) %collective-permute-start) | collective-permute-done | bytes 2097184 | tf_op jit(solution)/shard_map/ppermute | solution.py:630
  299.3 2.0 collective-permute-start.8
  301.4 0.0 collective-permute-done.2.refs_11_
  301.4 0.0 collective-permute-start.1
  301.4 42.9 %collective-permute-done.4.refs_9_ = bf16[2,2,2048,128]{3,2,1,0:T(8,128)(2,1)} collective-permute-done((bf16[2,2,2048,128]{3,2,1,0:T(8,128)(2,1)}, bf16[2,2,2048,128]{3,2,1,0:T(8,128)(2,1)}, u32[]{:S(2)}, u32[]{:S(2)}) %collective-permute-start.4) | collective-permute-done | bytes 2097184 | tf_op jit(solution)/shard_map/ppermute | solution.py:630
  344.3 0.0 collective-permute-start.3
  344.3 49.9 %shard_map.127 = (f32[16,512,2048]{2,1,0:T(8,128)}, f32[16,2048,512]{2,1,0:T(8,128)}, f32[16,512,2048]{2,1,0:T(8,128)}, f32[16,2048,512]{2,1,0:T(8,128)}, f32[64,512]{1,0:T(8,128)}) custom-call(f32[16,512,2048]{2,1,0:T(8,128)} %refs_0_.7, f32[16,512,2048]{2,1,0:T(8,128)} %refs_1_.7, f32[16,2048,512]{2,1,0:T(8,128)} %refs_2_.7, f32[16,2048,512]{2,1,0:T(8,128)} %refs_3_.7, ...), custom_call_target="tpu_custom_call" | custom-call | flops 49999998976 | bytes 150994944 | tf_op jit(solution)/shard_map/pallas_call | solution.py:600
  394.2 0.0 collective-permute-done.6.refs_11_
  394.2 0.7 collective-permute-start.5
  394.9 0.0 collective-permute-done.10.refs_11_
  394.9 0.1 collective-permute-start.7
  395.0 0.0 collective-permute-done.8.refs_9_
  395.0 0.4 collective-permute-start.11
  395.4 0.0 collective-permute-done.1.refs_10_
  395.4 0.1 collective-permute-start.9
  395.5 0.0 collective-permute-done.3.refs_12_
  395.5 50.0 %shard_map.128 = (f32[16,512,2048]{2,1,0:T(8,128)}, f32[16,2048,512]{2,1,0:T(8,128)}, f32[16,512,2048]{2,1,0:T(8,128)}, f32[16,2048,512]{2,1,0:T(8,128)}, f32[64,512]{1,0:T(8,128)}) custom-call(f32[16,512,2048]{2,1,0:T(8,128)} %refs_0_.7, f32[16,512,2048]{2,1,0:T(8,128)} %refs_1_.7, ...), custom_call_target="tpu_custom_call", output_to_operand_aliasing={{0}: (13, {}), {1}: (14, {}), {2}: (15, {}), {3}: (16, {})} | custom-call | flops 49999998976 | bytes 150994944 | tf_op jit(solution)/shard_map/pallas_call | solution.py:600
  445.5 0.0 collective-permute-done.5.refs_10_
  445.5 0.0 collective-permute-done.7.refs_12_
  445.5 50.0 %shard_map.129 = (f32[16,512,2048]{2,1,0:T(8,128)}, f32[16,2048,512]{2,1,0:T(8,128)}, f32[16,512,2048]{2,1,0:T(8,128)}, f32[16,2048,512]{2,1,0:T(8,128)}, f32[64,512]{1,0:T(8,128)}) custom-call(f32[16,512,2048]{2,1,0:T(8,128)} %refs_0_.7, f32[16,512,2048]{2,1,0:T(8,128)} %refs_1_.7, ...), custom_call_target="tpu_custom_call", output_to_operand_aliasing={{0}: (13, {}), {1}: (14, {}), {2}: (15, {}), {3}: (16, {})} | custom-call | flops 49999998976 | bytes 150994944 | tf_op jit(solution)/shard_map/pallas_call | solution.py:600
  495.5 0.0 collective-permute-done.11.refs_12_
  495.5 0.0 collective-permute-done.9.refs_10_
  495.5 50.0 %shard_map.130 = (f32[16,512,2048]{2,1,0:T(8,128)}, f32[16,2048,512]{2,1,0:T(8,128)}, f32[16,512,2048]{2,1,0:T(8,128)}, f32[16,2048,512]{2,1,0:T(8,128)}, f32[64,512]{1,0:T(8,128)}, /*index=5*/f32[64]{0:T(128)}) custom-call(f32[16,512,2048]{2,1,0:T(8,128)} %refs_0_.7, ...), custom_call_target="tpu_custom_call", output_to_operand_aliasing={{0}: (13, {}), {1}: (14, {}), {2}: (15, {}), {3}: (16, {})} | custom-call | flops 49999998976 | bytes 150994944 | tf_op jit(solution)/shard_map/pallas_call | solution.py:600
Async XLA Ops:
  249.5 49.9 %collective-permute-start = (bf16[2,2,2048,128]{3,2,1,0:T(8,128)(2,1)}, bf16[2,2,2048,128]{3,2,1,0:T(8,128)(2,1)}, u32[]{:S(2)}, u32[]{:S(2)}) collective-permute-start(bf16[2,2,2048,128]{3,2,1,0:T(8,128)(2,1)} %get-tuple-element.56.refs_5_), channel_id=1, source_target_pairs={{0,4},{1,5},{2,6},{3,7},{4,0},{5,1},{6,2},{7,3},{8,12},{9,13},{10,... | collective-permute-start | bytes 6291464 | tf_op jit(solution)/shard_map/ppermute | solution.py:630
  252.5 48.8 %collective-permute-start.2 = (bf16[2,2,2048,128]{3,2,1,0:T(8,128)(2,1)}, bf16[2,2,2048,128]{3,2,1,0:T(8,128)(2,1)}, u32[]{:S(2)}, u32[]{:S(2)}) collective-permute-start(bf16[2,2,2048,128]{3,2,1,0:T(8,128)(2,1)} %get-tuple-element.58.refs_7_), channel_id=1, source_target_pairs={{0,2},{1,3},{2,0},{3,1},{4,6},{5,7},{6,4},{7,5},{8,10},{9,11},{10,... | collective-permute-start | bytes 6291464 | tf_op jit(solution)/shard_map/ppermute | solution.py:630
  254.6 89.7 %collective-permute-start.4 = (bf16[2,2,2048,128]{3,2,1,0:T(8,128)(2,1)}, bf16[2,2,2048,128]{3,2,1,0:T(8,128)(2,1)}, u32[]{:S(2)}, u32[]{:S(2)}) collective-permute-start(bf16[2,2,2048,128]{3,2,1,0:T(8,128)(2,1)} %get-tuple-element.65.refs_5_), channel_id=1, source_target_pairs={{0,4},{1,5},{2,6},{3,7},{4,0},{5,1},{6,2},{7,3},{8,12},{9,13},{10,... | collective-permute-start | bytes 6291464 | tf_op jit(solution)/shard_map/ppermute | solution.py:630
  254.6 139.5 %collective-permute-start.6 = (bf16[2,2,2048,128]{3,2,1,0:T(8,128)(2,1)}, bf16[2,2,2048,128]{3,2,1,0:T(8,128)(2,1)}, u32[]{:S(2)}, u32[]{:S(2)}) collective-permute-start(bf16[2,2,2048,128]{3,2,1,0:T(8,128)(2,1)} %get-tuple-element.67.refs_7_), channel_id=1, source_target_pairs={{0,2},{1,3},{2,0},{3,1},{4,6},{5,7},{6,4},{7,5},{8,10},{9,11},{10,... | collective-permute-start | bytes 6291464 | tf_op jit(solution)/shard_map/ppermute | solution.py:630
  254.7 140.2 %collective-permute-start.10 = (bf16[2,2,2048,128]{3,2,1,0:T(8,128)(2,1)}, bf16[2,2,2048,128]{3,2,1,0:T(8,128)(2,1)}, u32[]{:S(2)}, u32[]{:S(2)}) collective-permute-start(bf16[2,2,2048,128]{3,2,1,0:T(8,128)(2,1)} %get-tuple-element.76.refs_7_), channel_id=1, source_target_pairs={{0,2},{1,3},{2,0},{3,1},{4,6},{5,7},{6,4},{7,5},{8,10},{9,11},{10,... | collective-permute-start | bytes 6291464 | tf_op jit(solution)/shard_map/ppermute | solution.py:630
  299.3 95.7 %collective-permute-start.8 = (bf16[2,2,2048,128]{3,2,1,0:T(8,128)(2,1)}, bf16[2,2,2048,128]{3,2,1,0:T(8,128)(2,1)}, u32[]{:S(2)}, u32[]{:S(2)}) collective-permute-start(bf16[2,2,2048,128]{3,2,1,0:T(8,128)(2,1)} %get-tuple-element.74.refs_5_), channel_id=1, source_target_pairs={{0,4},{1,5},{2,6},{3,7},{4,0},{5,1},{6,2},{7,3},{8,12},{9,13},{10,... | collective-permute-start | bytes 6291464 | tf_op jit(solution)/shard_map/ppermute | solution.py:630
  301.4 94.1 %collective-permute-start.1 = (bf16[2,2,2048,128]{3,2,1,0:T(8,128)(2,1)}, bf16[2,2,2048,128]{3,2,1,0:T(8,128)(2,1)}, u32[]{:S(2)}, u32[]{:S(2)}) collective-permute-start(bf16[2,2,2048,128]{3,2,1,0:T(8,128)(2,1)} %collective-permute-done.refs_9_), channel_id=1, source_target_pairs={{0,1},{1,0},{2,3},{3,2},{4,5},{5,4},{6,7},{7,6},{8,9},{9,8},{10,11... | collective-permute-start | bytes 6291464 | tf_op jit(solution)/shard_map/ppermute | solution.py:630
  344.3 51.3 %collective-permute-start.3 = (bf16[2,2,2048,128]{3,2,1,0:T(8,128)(2,1)}, bf16[2,2,2048,128]{3,2,1,0:T(8,128)(2,1)}, u32[]{:S(2)}, u32[]{:S(2)}) collective-permute-start(bf16[2,2,2048,128]{3,2,1,0:T(8,128)(2,1)} %collective-permute-done.2.refs_11_), channel_id=1, source_target_pairs={{0,1},{1,0},{2,3},{3,2},{4,5},{5,4},{6,7},{7,6},{8,9},{9,8},{10,11... | collective-permute-start | bytes 6291464 | tf_op jit(solution)/shard_map/ppermute | solution.py:630
  394.2 51.3 %collective-permute-start.5 = (bf16[2,2,2048,128]{3,2,1,0:T(8,128)(2,1)}, bf16[2,2,2048,128]{3,2,1,0:T(8,128)(2,1)}, u32[]{:S(2)}, u32[]{:S(2)}) collective-permute-start(bf16[2,2,2048,128]{3,2,1,0:T(8,128)(2,1)} %collective-permute-done.4.refs_9_), channel_id=1, source_target_pairs={{0,1},{1,0},{2,3},{3,2},{4,5},{5,4},{6,7},{7,6},{8,9},{9,8},{10,11... | collective-permute-start | bytes 6291464 | tf_op jit(solution)/shard_map/ppermute | solution.py:630
  394.9 50.6 %collective-permute-start.7 = (bf16[2,2,2048,128]{3,2,1,0:T(8,128)(2,1)}, bf16[2,2,2048,128]{3,2,1,0:T(8,128)(2,1)}, u32[]{:S(2)}, u32[]{:S(2)}) collective-permute-start(bf16[2,2,2048,128]{3,2,1,0:T(8,128)(2,1)} %collective-permute-done.6.refs_11_), channel_id=1, source_target_pairs={{0,1},{1,0},{2,3},{3,2},{4,5},{5,4},{6,7},{7,6},{8,9},{9,8},{10,11... | collective-permute-start | bytes 6291464 | tf_op jit(solution)/shard_map/ppermute | solution.py:630
  395.0 100.5 %collective-permute-start.11 = (bf16[2,2,2048,128]{3,2,1,0:T(8,128)(2,1)}, bf16[2,2,2048,128]{3,2,1,0:T(8,128)(2,1)}, u32[]{:S(2)}, u32[]{:S(2)}) collective-permute-start(bf16[2,2,2048,128]{3,2,1,0:T(8,128)(2,1)} %collective-permute-done.10.refs_11_), channel_id=1, source_target_pairs={{0,1},{1,0},{2,3},{3,2},{4,5},{5,4},{6,7},{7,6},{8,9},{9,8},{10,11... | collective-permute-start | bytes 6291464 | tf_op jit(solution)/shard_map/ppermute | solution.py:630
  395.4 100.1 %collective-permute-start.9 = (bf16[2,2,2048,128]{3,2,1,0:T(8,128)(2,1)}, bf16[2,2,2048,128]{3,2,1,0:T(8,128)(2,1)}, u32[]{:S(2)}, u32[]{:S(2)}) collective-permute-start(bf16[2,2,2048,128]{3,2,1,0:T(8,128)(2,1)} %collective-permute-done.8.refs_9_), channel_id=1, source_target_pairs={{0,1},{1,0},{2,3},{3,2},{4,5},{5,4},{6,7},{7,6},{8,9},{9,8},{10,11... | collective-permute-start | bytes 6291464 | tf_op jit(solution)/shard_map/ppermute | solution.py:630

commit v5 on v4

--- a/solution.py
+++ b/solution.py
@@ -18,47 +18,49 @@
 SLOTS = 4
 QUARTERS = 4
 AHEAD = 4
+TILES = 16
+HEAD = 15
 CACHED = 6
 FIRST = 1
 RELAYS = (
     (
         (30000, 10000, 20000),
         (31000, 11000, 21000),
-        (32000,),
+        (32000, 22000),
         (),
-        (100, 10, 1, 10001, 20100, 1100, 1010, 1001, 33000, 12000, 21001, 101, 110, 2, 10002, 22000, 2100, 1011, 1002,
-         13000, 21002, 102, 2010, 3, 10003, 23000, 3100, 1012, 1003, 11010, 21003, 103, 3010, 2003, 12003, 22100, 1110,
-         1013, 3003, 13010, 23003, 2103, 2110, 2002, 12002, 3110, 3013, 3002, 23002, 2102, 2001, 12001, 3012, 3001,
-         23001, 2101, 3011),
+        (100, 10, 1, 10001, 1100, 1010, 1001, 33000, 21001, 12000, 101, 2010, 2, 20100, 10002, 2100, 1011, 1002, 21002,
+         13000, 102, 110, 3, 23000, 10003, 3100, 1012, 1003, 21003, 11010, 103, 3010, 2003, 22100, 12003, 1110, 1013,
+         3003, 23003, 13010, 2103, 2110, 2002, 12002, 3110, 3013, 3002, 23002, 2102, 2001, 12001, 3012, 3001, 23001,
+         2101, 3011),
     ),
     (
         (30001, 40001, 10001),
         (21001, 31001, 41001),
+        (12001,),
         (),
-        (),
-        (0, 101, 2, 10000, 20000, 30000, 40002, 10002, 1011, 1000, 1002, 21000, 100, 31000, 41002, 11000, 10, 21002,
-         2000, 3, 102, 32000, 40003, 10003, 1010, 3000, 1003, 21003, 1100, 33000, 41003, 1012, 20100, 2003, 12003, 103,
-         32001, 42003, 12000, 1013, 3003, 23003, 2103, 33001, 43003, 11010, 110, 22000, 2002, 2100, 42002, 13000, 3013,
-         23000, 3002, 1110, 43002, 12002, 2010, 22100, 3100, 42001, 3010, 13010, 23002, 2102, 43001, 12001, 2110,
-         23001, 3110, 3012, 2101, 3011),
+        (0, 101, 2, 20000, 30000, 40002, 10000, 1011, 1000, 1002, 21000, 31000, 41002, 2101, 10002, 10, 21002, 2000, 3,
+         32000, 40003, 100, 10003, 1010, 3000, 1003, 21003, 33000, 41003, 102, 11000, 1012, 22000, 2003, 32001, 42003,
+         103, 12003, 1013, 3003, 23003, 33001, 43003, 1100, 12000, 2010, 20100, 2002, 42002, 2103, 11010, 3013, 23000,
+         3002, 43002, 2100, 13000, 110, 23002, 42001, 1110, 12002, 3010, 22100, 43001, 3100, 13010, 3012, 23001, 2102,
+         2110, 3110, 3011),
     ),
     (
         (30002, 40002, 10002),
         (21002, 31002, 41002),
+        (12002,),
         (),
-        (),
-        (1, 102, 3, 10001, 30001, 40003, 10003, 1012, 23002, 1001, 1003, 21001, 101, 31001, 41003, 3012, 0, 2003,
-         10000, 20000, 103, 30000, 42003, 1011, 1000, 3003, 11000, 21000, 100, 31000, 43003, 10, 2000, 12000, 20100,
-         1100, 32000, 42002, 1010, 11010, 3000, 22000, 2100, 33000, 43002, 13000, 110, 2001, 23000, 1110, 32001, 12003,
-         2010, 3001, 22100, 3100, 33001, 3010, 13010, 21003, 2103, 32002, 12001, 2110, 23003, 3110, 33002, 12002, 1013,
-         23001, 2101, 3013, 2102, 3011),
+        (1, 102, 3, 30001, 40003, 10001, 23002, 1012, 1001, 1003, 31001, 41003, 21001, 2102, 10003, 0, 3012, 2003,
+         30000, 42003, 20000, 101, 10000, 1000, 1011, 3003, 31000, 43003, 21000, 103, 11000, 2000, 10, 32000, 42002,
+         22000, 100, 12000, 3000, 1010, 33000, 43002, 20100, 1100, 13000, 2001, 2010, 32001, 23000, 2100, 11010, 3001,
+         110, 33001, 22100, 3100, 12003, 3010, 32002, 21003, 1110, 13010, 2110, 33002, 23003, 2103, 12001, 1013, 23001,
+         3110, 3013, 2101, 3011),
     ),
     (
         (40003, 10003),
         (21003, 41003),
-        (42003, 12003),
+        (12003, 42003),
         (),
-        (2, 103, 10002, 1013, 23003, 1002, 21002, 102, 43003, 3013, 1, 10001, 2103, 1012, 1001, 21001, 101, 0, 10000,
+        (2, 103, 10002, 23003, 1013, 1002, 43003, 21002, 2103, 1, 3013, 10001, 102, 1001, 1012, 21001, 101, 0, 10000,
          20000, 1011, 1000, 21000, 11000, 100, 10, 20100, 2000, 12000, 1100, 1010, 22000, 11010, 3000, 2100, 110,
          13000, 23000, 2001, 1110, 2010, 22100, 12001, 3001, 3100, 3010, 13010, 23001, 2002, 2110, 2101, 12002, 3002,
          23002, 3110, 3011, 3012, 2102),
@@ -472,22 +474,21 @@
     )(w_in, w_out, x, y)
 
 
-def update_kernel(dims, group, last, *refs):
+def update_kernel(dims, group, first, stop, last, *refs):
     layers, _, d, piece = dims
     step_size = LR_SCALE / layers
     chunk = 2 * piece
-    steps = 16
-    w1, m1, w2, m2, h_in = refs[:5]
-    sums = refs[5:13]
-    refs = refs[13:]
-    if group:
+    w1, m1, w2, m2, h_in, hb_in = refs[:6]
+    sums = refs[6:14]
+    refs = refs[14:]
+    if group or first:
         refs = refs[4:]
     if last:
         y_ref, refs = refs[0], refs[1:]
-    w1o, w2o, m1o, m2o, h_out = refs[:5]
+    w1o, w2o, m1o, m2o, h_out, hb_ref = refs[:6]
     if last:
-        loss_ref = refs[5]
-    bw1, bm1, bw2, bm2, gbuf, in_sem, out_sem, gsem, nb1, nb2, hb_ref = refs[-11:]
+        loss_ref = refs[6]
+    bw1, bm1, bw2, bm2, gbuf, in_sem, out_sem, gsem, nb1, nb2 = refs[-10:]
     slots = bw1.shape[0]
 
     me = lax.axis_index("data")
@@ -522,9 +523,10 @@
                     def _(par=par, inner=inner, is_far=is_far, twin=twin):
                         pltpu.make_async_copy(sums[4 * is_far + 2 * par + twin].at[inner, q], gbuf.at[slot, par], gsem.at[par, slot]).start()
 
-    for t in range(AHEAD):
-        fetch(t, t)
+    for t in range(first, min(first + AHEAD, stop)):
+        fetch(t, t % slots)
     h_out[...] = h_in[...].astype(F32)
+    hb_ref[...] = hb_in[...]
     off = (piece // 128) * d
 
     def body(t, carry):
@@ -556,11 +558,11 @@
         for copy in writes(t, slot):
             copy.start()
 
-        @pl.when(t + AHEAD < steps)
+        @pl.when(t + AHEAD < stop)
         def _():
             nslot = (t + AHEAD) % slots
 
-            @pl.when(t + AHEAD >= slots)
+            @pl.when(t + AHEAD >= first + slots)
             def _():
                 for copy in writes(t + AHEAD - slots, nslot):
                     copy.wait()
@@ -571,8 +573,8 @@
         h_out[...] += mm(gelu(z).astype(BF16), nb2[...])
         return carry
 
-    lax.fori_loop(0, steps, body, 0)
-    for t in range(steps - slots, steps):
+    lax.fori_loop(first, stop, body, 0)
+    for t in range(max(first, stop - slots), stop):
         for copy in writes(t, t % slots):
             copy.wait()
     if last:
@@ -580,25 +582,26 @@
         loss_ref[...] = jnp.sum(diff * diff, axis=-1) / (2 * d)
 
 
-def update(group, w_in, m_in, w_out, m_out, h, sums, prev, y):
+def update(group, first, stop, w_in, m_in, w_out, m_out, h, hb, sums, prev, y):
     layers, d, hid = w_in.shape
     rows = h.shape[0]
     piece = hid // 2 // QUARTERS
     chunk = 2 * piece
-    last = group == layers // 4 - 1
+    last = group == layers // 4 - 1 and stop == TILES
     whole = pl.BlockSpec(memory_space=pltpu.VMEM)
     any_spec = pl.BlockSpec(memory_space=pl.ANY)
-    args = [w_in, m_in, w_out, m_out, h, *sums, *prev] + ([y] if last else [])
-    in_specs = [any_spec] * 4 + [whole] + [any_spec] * (8 + len(prev)) + ([whole] if last else [])
-    out_specs = [any_spec] * 4 + [whole]
+    args = [w_in, m_in, w_out, m_out, h, hb, *sums, *prev] + ([y] if last else [])
+    in_specs = [any_spec] * 4 + [whole] * 2 + [any_spec] * (8 + len(prev)) + ([whole] if last else [])
+    out_specs = [any_spec] * 4 + [whole] * 2
     out_shape = [jax.ShapeDtypeStruct(a.shape, F32) for a in (w_in, w_out, m_in, m_out, h)]
+    out_shape.append(jax.ShapeDtypeStruct(hb.shape, BF16))
     if last:
         out_specs.append(whole)
         out_shape.append(jax.ShapeDtypeStruct((rows,), F32))
-    n_el = 2 * w_in.size // 4
-    slots = 7
+    n_el = 2 * w_in.size // 4 * (stop - first) // TILES
+    slots = min(7, stop - first)
     return pl.pallas_call(
-        functools.partial(update_kernel, (layers, rows, d, piece), group, last),
+        functools.partial(update_kernel, (layers, rows, d, piece), group, first, stop, last),
         in_specs=in_specs,
         out_specs=out_specs,
         out_shape=out_shape,
@@ -613,11 +616,10 @@
             pltpu.SemaphoreType.DMA((2, slots)),
             pltpu.VMEM((d, chunk), BF16),
             pltpu.VMEM((chunk, d), BF16),
-            pltpu.VMEM((rows, d), BF16),
         ],
-        input_output_aliases={13 + i: i for i in range(len(prev))},
+        input_output_aliases={14 + i: i for i in range(len(prev))},
         compiler_params=pltpu.CompilerParams(vmem_limit_bytes=VMEM_LIMIT),
-        cost_estimate=pl.CostEstimate(flops=5 * 10**10, bytes_accessed=18 * n_el, transcendentals=0),
+        cost_estimate=pl.CostEstimate(flops=3 * 10**9 * (stop - first), bytes_accessed=18 * n_el, transcendentals=0),
     )(*args)
 
 
@@ -638,12 +640,14 @@
             from_y = send(near[g][0], "y")
             from_x = send(near[g][2], "x")
             far.append([from_y, send(from_y, "core"), from_x, send(from_x, "core")])
-        prev, h = [], x_second
+        prev, h, hb = [], x_second, x_second
         for g in range(groups):
-            outs = update(g, w_in, mom_in, w_out, mom_out, h, near[g] + far[g], prev, y_second)
-            prev, h = list(outs[:4]), outs[4]
+            cuts = [0, HEAD, TILES] if g < groups - 1 else [0, TILES]
+            for part in range(len(cuts) - 1):
+                outs = update(g, cuts[part], cuts[part + 1], w_in, mom_in, w_out, mom_out, h, hb, near[g] + far[g], prev, y_second)
+                prev, h, hb = list(outs[:4]), outs[4], outs[5]
         w_in_new, w_out_new, mom_in_new, mom_out_new = prev
-        return w_in_new, w_out_new, mom_in_new, mom_out_new, outs[5], h
+        return w_in_new, w_out_new, mom_in_new, mom_out_new, outs[6], h
 
     return jax.shard_map(
         local_steps, mesh=mesh,

time: 548 us -> 563 us (1.027)
  Pallas kernels: 449 us -> 464 us
    pallas_call x4 -> x7, Pallas kernels: 200 us -> 216 us  [update(): pl.pallas_call(functools.partial(update_kernel, (layers, rows, d, piece),...]
  transfers between devices with their start and end apart: 12 -> 12, of which waited for: 2 -> 2; matrix products, arithmetic and copies ran while one was open for 0% -> 0% of each run, Pallas kernels for 27% -> 29%
where the time goes in v5:
time: 563 us; the launch traced here: 562 us
  Pallas kernels  464 us (82%)
  waiting for transfers between devices  87.6 us (16%)
  starting transfers between devices  9.26 us (2%)
    pallas_call x1, Pallas kernels, local_grads(): pl.pallas_call(functools.partial(grads_kernel, dims), out_shape=[jax.Shap...  249 us
    pallas_call x7, Pallas kernels, update(): pl.pallas_call(functools.partial(update_kernel, (layers, rows, d, piece),...  216 us
    ppermute x12, waiting for transfers between devices, send(): return lax.ppermute(array, 'data', swap[axis])  87.6 us
  transfers between devices with their start and end apart: 12, of which 2 were waited for; matrix products, arithmetic and copies ran while one was open for 0% of the time, Pallas kernels for 29%

profile of v5, /device:TPU:0, one launch (start us, length us, event | category | flops | bytes accessed | tf_op | source)
XLA Modules:
  0.0 562.1 jit_solution(1110302694513022988)
XLA Ops:
  0.6 248.8 %local_grads.1 = (bf16[2,2,2048,128]{3,2,1,0:T(8,128)(2,1)}, bf16[2,2,2048,128]{3,2,1,0:T(8,128)(2,1)}, bf16[2,2,2048,128]{3,2,1,0:T(8,128)(2,1)}, bf16[2,2,2048...) custom-call(f32[16,512,2048]{2,1,0:T(8,128)} %refs_0_.13, ...), custom_call_target="tpu_custom_call" | custom-call | flops 17179869184 | bytes 268435456 | tf_op jit(solution)/shard_map/local_grads/pallas_call | solution.py:436
  249.4 3.4 collective-permute-start
  252.9 0.1 collective-permute-start.2
  253.0 0.1 collective-permute-start.4
  253.0 1.9 collective-permute-start.6
  255.0 0.1 collective-permute-start.10
  255.1 44.6 %collective-permute-done.refs_10_ = bf16[2,2,2048,128]{3,2,1,0:T(8,128)(2,1)} collective-permute-done((bf16[2,2,2048,128]{3,2,1,0:T(8,128)(2,1)}, bf16[2,2,2048,128]{3,2,1,0:T(8,128)(2,1)}, u32[]{:S(2)}, u32[]{:S(2)}) %collective-permute-start) | collective-permute-done | bytes 2097184 | tf_op jit(solution)/shard_map/ppermute | solution.py:632
  299.7 2.0 collective-permute-start.8
  301.7 0.0 collective-permute-done.2.refs_12_
  301.7 0.0 collective-permute-start.1
  301.7 42.9 %collective-permute-done.4.refs_10_ = bf16[2,2,2048,128]{3,2,1,0:T(8,128)(2,1)} collective-permute-done((bf16[2,2,2048,128]{3,2,1,0:T(8,128)(2,1)}, bf16[2,2,2048,128]{3,2,1,0:T(8,128)(2,1)}, u32[]{:S(2)}, u32[]{:S(2)}) %collective-permute-start.4) | collective-permute-done | bytes 2097184 | tf_op jit(solution)/shard_map/ppermute | solution.py:632
  344.6 0.0 collective-permute-start.3
  344.6 48.5 %shard_map.127 = (f32[16,512,2048]{2,1,0:T(8,128)}, f32[16,2048,512]{2,1,0:T(8,128)}, f32[16,512,2048]{2,1,0:T(8,128)}, f32[16,2048,512]{2,1,0:T(8,128)}, f32[64,512]{1,0:T(8,128)}, /*index=5*/bf16[64,512]{1,0:T(8,128)(2,1)}) custom-call(f32[16,512,2048]{2,1,0:T(8,128)} %refs_0_.13, f32[16,512,2048]{2,1,0:T(8,128)} %refs_1_.13, f32[16,2048,512]{2,1,0:T(8,128)} %refs_2_.13, ...), custom_call_target="tpu_custom_call" | custom-call | flops 44999999488 | bytes 141557760 | tf_op jit(solution)/shard_map/pallas_call | solution.py:603
  393.2 6.6 %shard_map.128 = (f32[16,512,2048]{2,1,0:T(8,128)}, f32[16,2048,512]{2,1,0:T(8,128)}, f32[16,512,2048]{2,1,0:T(8,128)}, f32[16,2048,512]{2,1,0:T(8,128)}, f32[64,512]{1,0:T(8,128)}, /*index=5*/bf16[64,512]{1,0:T(8,128)(2,1)}) custom-call(f32[16,512,2048]{2,1,0:T(8,128)} %refs_0_.13, ...), custom_call_target="tpu_custom_call", output_to_operand_aliasing={{0}: (14, {}), {1}: (15, {}), {2}: (16, {}), {3}: (17, {})} | custom-call | flops 3000000000 | bytes 9437184 | tf_op jit(solution)/shard_map/pallas_call | solution.py:603
  399.8 0.0 collective-permute-done.6.refs_12_
  399.8 1.0 collective-permute-start.5
  400.8 0.0 collective-permute-done.10.refs_12_
  400.8 0.1 collective-permute-start.7
  400.9 0.0 collective-permute-done.8.refs_10_
  400.9 0.4 collective-permute-start.11
  401.3 0.0 collective-permute-done.1.refs_11_
  401.3 0.1 collective-permute-start.9
  401.4 0.0 collective-permute-done.3.refs_13_
  401.4 48.5 %shard_map.129 = (f32[16,512,2048]{2,1,0:T(8,128)}, f32[16,2048,512]{2,1,0:T(8,128)}, f32[16,512,2048]{2,1,0:T(8,128)}, f32[16,2048,512]{2,1,0:T(8,128)}, f32[64,512]{1,0:T(8,128)}, /*index=5*/bf16[64,512]{1,0:T(8,128)(2,1)}) custom-call(f32[16,512,2048]{2,1,0:T(8,128)} %refs_0_.13, ...), custom_call_target="tpu_custom_call", output_to_operand_aliasing={{0}: (14, {}), {1}: (15, {}), {2}: (16, {}), {3}: (17, {})} | custom-call | flops 44999999488 | bytes 141557760 | tf_op jit(solution)/shard_map/pallas_call | solution.py:603
  449.9 6.6 %shard_map.130 = (f32[16,512,2048]{2,1,0:T(8,128)}, f32[16,2048,512]{2,1,0:T(8,128)}, f32[16,512,2048]{2,1,0:T(8,128)}, f32[16,2048,512]{2,1,0:T(8,128)}, f32[64,512]{1,0:T(8,128)}, /*index=5*/bf16[64,512]{1,0:T(8,128)(2,1)}) custom-call(f32[16,512,2048]{2,1,0:T(8,128)} %refs_0_.13, ...), custom_call_target="tpu_custom_call", output_to_operand_aliasing={{0}: (14, {}), {1}: (15, {}), {2}: (16, {}), {3}: (17, {})} | custom-call | flops 3000000000 | bytes 9437184 | tf_op jit(solution)/shard_map/pallas_call | solution.py:603
  456.6 0.0 collective-permute-done.5.refs_11_
  456.6 0.0 collective-permute-done.7.refs_13_
  456.6 48.5 %shard_map.131 = (f32[16,512,2048]{2,1,0:T(8,128)}, f32[16,2048,512]{2,1,0:T(8,128)}, f32[16,512,2048]{2,1,0:T(8,128)}, f32[16,2048,512]{2,1,0:T(8,128)}, f32[64,512]{1,0:T(8,128)}, /*index=5*/bf16[64,512]{1,0:T(8,128)(2,1)}) custom-call(f32[16,512,2048]{2,1,0:T(8,128)} %refs_0_.13, ...), custom_call_target="tpu_custom_call", output_to_operand_aliasing={{0}: (14, {}), {1}: (15, {}), {2}: (16, {}), {3}: (17, {})} | custom-call | flops 44999999488 | bytes 141557760 | tf_op jit(solution)/shard_map/pallas_call | solution.py:603
  505.1 6.6 %shard_map.132 = (f32[16,512,2048]{2,1,0:T(8,128)}, f32[16,2048,512]{2,1,0:T(8,128)}, f32[16,512,2048]{2,1,0:T(8,128)}, f32[16,2048,512]{2,1,0:T(8,128)}, f32[64,512]{1,0:T(8,128)}, /*index=5*/bf16[64,512]{1,0:T(8,128)(2,1)}) custom-call(f32[16,512,2048]{2,1,0:T(8,128)} %refs_0_.13, ...), custom_call_target="tpu_custom_call", output_to_operand_aliasing={{0}: (14, {}), {1}: (15, {}), {2}: (16, {}), {3}: (17, {})} | custom-call | flops 3000000000 | bytes 9437184 | tf_op jit(solution)/shard_map/pallas_call | solution.py:603
  511.8 0.0 collective-permute-done.11.refs_13_
  511.8 0.0 collective-permute-done.9.refs_11_
  511.8 50.1 %shard_map.133 = (f32[16,512,2048]{2,1,0:T(8,128)}, f32[16,2048,512]{2,1,0:T(8,128)}, f32[16,512,2048]{2,1,0:T(8,128)}, f32[16,2048,512]{2,1,0:T(8,128)}, f32[64...) custom-call(f32[16,512,2048]{2,1,0:T(8,128)} %refs_0_.13, ...), custom_call_target="tpu_custom_call", output_to_operand_aliasing={{0}: (14, {}), {1}: (15, {}), {2}: (16, {}), {3}: (17, {})} | custom-call | flops 48000000000 | bytes 150994944 | tf_op jit(solution)/shard_map/pallas_call | solution.py:603
Async XLA Ops:
  249.4 50.2 %collective-permute-start = (bf16[2,2,2048,128]{3,2,1,0:T(8,128)(2,1)}, bf16[2,2,2048,128]{3,2,1,0:T(8,128)(2,1)}, u32[]{:S(2)}, u32[]{:S(2)}) collective-permute-start(bf16[2,2,2048,128]{3,2,1,0:T(8,128)(2,1)} %get-tuple-element.84.refs_6_), channel_id=1, source_target_pairs={{0,4},{1,5},{2,6},{3,7},{4,0},{5,1},{6,2},{7,3},{8,12},{9,13},{10,... | collective-permute-start | bytes 6291464 | tf_op jit(solution)/shard_map/ppermute | solution.py:632
  252.9 48.8 %collective-permute-start.2 = (bf16[2,2,2048,128]{3,2,1,0:T(8,128)(2,1)}, bf16[2,2,2048,128]{3,2,1,0:T(8,128)(2,1)}, u32[]{:S(2)}, u32[]{:S(2)}) collective-permute-start(bf16[2,2,2048,128]{3,2,1,0:T(8,128)(2,1)} %get-tuple-element.86.refs_8_), channel_id=1, source_target_pairs={{0,2},{1,3},{2,0},{3,1},{4,6},{5,7},{6,4},{7,5},{8,10},{9,11},{10,... | collective-permute-start | bytes 6291464 | tf_op jit(solution)/shard_map/ppermute | solution.py:632
  253.0 91.7 %collective-permute-start.4 = (bf16[2,2,2048,128]{3,2,1,0:T(8,128)(2,1)}, bf16[2,2,2048,128]{3,2,1,0:T(8,128)(2,1)}, u32[]{:S(2)}, u32[]{:S(2)}) collective-permute-start(bf16[2,2,2048,128]{3,2,1,0:T(8,128)(2,1)} %get-tuple-element.100.refs_6_), channel_id=1, source_target_pairs={{0,4},{1,5},{2,6},{3,7},{4,0},{5,1},{6,2},{7,3},{8,12},{9,13},{10,... | collective-permute-start | bytes 6291464 | tf_op jit(solution)/shard_map/ppermute | solution.py:632
  253.0 146.7 %collective-permute-start.6 = (bf16[2,2,2048,128]{3,2,1,0:T(8,128)(2,1)}, bf16[2,2,2048,128]{3,2,1,0:T(8,128)(2,1)}, u32[]{:S(2)}, u32[]{:S(2)}) collective-permute-start(bf16[2,2,2048,128]{3,2,1,0:T(8,128)(2,1)} %get-tuple-element.102.refs_8_), channel_id=1, source_target_pairs={{0,2},{1,3},{2,0},{3,1},{4,6},{5,7},{6,4},{7,5},{8,10},{9,11},{10,... | collective-permute-start | bytes 6291464 | tf_op jit(solution)/shard_map/ppermute | solution.py:632
  255.0 145.8 %collective-permute-start.10 = (bf16[2,2,2048,128]{3,2,1,0:T(8,128)(2,1)}, bf16[2,2,2048,128]{3,2,1,0:T(8,128)(2,1)}, u32[]{:S(2)}, u32[]{:S(2)}) collective-permute-start(bf16[2,2,2048,128]{3,2,1,0:T(8,128)(2,1)} %get-tuple-element.118.refs_8_), channel_id=1, source_target_pairs={{0,2},{1,3},{2,0},{3,1},{4,6},{5,7},{6,4},{7,5},{8,10},{9,11},{10,... | collective-permute-start | bytes 6291464 | tf_op jit(solution)/shard_map/ppermute | solution.py:632
  299.7 101.2 %collective-permute-start.8 = (bf16[2,2,2048,128]{3,2,1,0:T(8,128)(2,1)}, bf16[2,2,2048,128]{3,2,1,0:T(8,128)(2,1)}, u32[]{:S(2)}, u32[]{:S(2)}) collective-permute-start(bf16[2,2,2048,128]{3,2,1,0:T(8,128)(2,1)} %get-tuple-element.116.refs_6_), channel_id=1, source_target_pairs={{0,4},{1,5},{2,6},{3,7},{4,0},{5,1},{6,2},{7,3},{8,12},{9,13},{10,... | collective-permute-start | bytes 6291464 | tf_op jit(solution)/shard_map/ppermute | solution.py:632
  301.7 99.6 %collective-permute-start.1 = (bf16[2,2,2048,128]{3,2,1,0:T(8,128)(2,1)}, bf16[2,2,2048,128]{3,2,1,0:T(8,128)(2,1)}, u32[]{:S(2)}, u32[]{:S(2)}) collective-permute-start(bf16[2,2,2048,128]{3,2,1,0:T(8,128)(2,1)} %collective-permute-done.refs_10_), channel_id=1, source_target_pairs={{0,1},{1,0},{2,3},{3,2},{4,5},{5,4},{6,7},{7,6},{8,9},{9,8},{10,11... | collective-permute-start | bytes 6291464 | tf_op jit(solution)/shard_map/ppermute | solution.py:632
  344.6 56.8 %collective-permute-start.3 = (bf16[2,2,2048,128]{3,2,1,0:T(8,128)(2,1)}, bf16[2,2,2048,128]{3,2,1,0:T(8,128)(2,1)}, u32[]{:S(2)}, u32[]{:S(2)}) collective-permute-start(bf16[2,2,2048,128]{3,2,1,0:T(8,128)(2,1)} %collective-permute-done.2.refs_12_), channel_id=1, source_target_pairs={{0,1},{1,0},{2,3},{3,2},{4,5},{5,4},{6,7},{7,6},{8,9},{9,8},{10,11... | collective-permute-start | bytes 6291464 | tf_op jit(solution)/shard_map/ppermute | solution.py:632
  399.8 56.8 %collective-permute-start.5 = (bf16[2,2,2048,128]{3,2,1,0:T(8,128)(2,1)}, bf16[2,2,2048,128]{3,2,1,0:T(8,128)(2,1)}, u32[]{:S(2)}, u32[]{:S(2)}) collective-permute-start(bf16[2,2,2048,128]{3,2,1,0:T(8,128)(2,1)} %collective-permute-done.4.refs_10_), channel_id=1, source_target_pairs={{0,1},{1,0},{2,3},{3,2},{4,5},{5,4},{6,7},{7,6},{8,9},{9,8},{10,11... | collective-permute-start | bytes 6291464 | tf_op jit(solution)/shard_map/ppermute | solution.py:632
  400.8 55.8 %collective-permute-start.7 = (bf16[2,2,2048,128]{3,2,1,0:T(8,128)(2,1)}, bf16[2,2,2048,128]{3,2,1,0:T(8,128)(2,1)}, u32[]{:S(2)}, u32[]{:S(2)}) collective-permute-start(bf16[2,2,2048,128]{3,2,1,0:T(8,128)(2,1)} %collective-permute-done.6.refs_12_), channel_id=1, source_target_pairs={{0,1},{1,0},{2,3},{3,2},{4,5},{5,4},{6,7},{7,6},{8,9},{9,8},{10,11... | collective-permute-start | bytes 6291464 | tf_op jit(solution)/shard_map/ppermute | solution.py:632
  400.9 110.9 %collective-permute-start.11 = (bf16[2,2,2048,128]{3,2,1,0:T(8,128)(2,1)}, bf16[2,2,2048,128]{3,2,1,0:T(8,128)(2,1)}, u32[]{:S(2)}, u32[]{:S(2)}) collective-permute-start(bf16[2,2,2048,128]{3,2,1,0:T(8,128)(2,1)} %collective-permute-done.10.refs_12_), channel_id=1, source_target_pairs={{0,1},{1,0},{2,3},{3,2},{4,5},{5,4},{6,7},{7,6},{8,9},{9,8},{10,11... | collective-permute-start | bytes 6291464 | tf_op jit(solution)/shard_map/ppermute | solution.py:632
  401.3 110.5 %collective-permute-start.9 = (bf16[2,2,2048,128]{3,2,1,0:T(8,128)(2,1)}, bf16[2,2,2048,128]{3,2,1,0:T(8,128)(2,1)}, u32[]{:S(2)}, u32[]{:S(2)}) collective-permute-start(bf16[2,2,2048,128]{3,2,1,0:T(8,128)(2,1)} %collective-permute-done.8.refs_10_), channel_id=1, source_target_pairs={{0,1},{1,0},{2,3},{3,2},{4,5},{5,4},{6,7},{7,6},{8,9},{9,8},{10,11... | collective-permute-start | bytes 6291464 | tf_op jit(solution)/shard_map/ppermute | solution.py:632

commit v6 on v4

--- a/solution.py
+++ b/solution.py
@@ -16,6 +16,7 @@
 GELU_C = 0.7978845608028654
 GELU_K = 0.044715
 SLOTS = 4
+RING = 3
 QUARTERS = 4
 AHEAD = 4
 CACHED = 6
@@ -24,41 +25,41 @@
     (
         (30000, 10000, 20000),
         (31000, 11000, 21000),
-        (32000,),
+        (32000, 22000),
         (),
-        (100, 10, 1, 10001, 20100, 1100, 1010, 1001, 33000, 12000, 21001, 101, 110, 2, 10002, 22000, 2100, 1011, 1002,
-         13000, 21002, 102, 2010, 3, 10003, 23000, 3100, 1012, 1003, 11010, 21003, 103, 3010, 2003, 12003, 22100, 1110,
-         1013, 3003, 13010, 23003, 2103, 2110, 2002, 12002, 3110, 3013, 3002, 23002, 2102, 2001, 12001, 3012, 3001,
-         23001, 2101, 3011),
+        (100, 10, 1, 10001, 1100, 1010, 1001, 33000, 12000, 21001, 101, 2010, 2, 10002, 20100, 2100, 1011, 1002, 13000,
+         21002, 102, 110, 3, 10003, 23000, 3100, 1012, 1003, 11010, 21003, 103, 3010, 2003, 12003, 22100, 1110, 1013,
+         3003, 13010, 23003, 2103, 2110, 2002, 12002, 3110, 3013, 3002, 23002, 2102, 2001, 12001, 3012, 3001, 23001,
+         2101, 3011),
     ),
     (
         (30001, 40001, 10001),
         (21001, 31001, 41001),
+        (12001,),
         (),
-        (),
-        (0, 101, 2, 10000, 20000, 30000, 40002, 10002, 1011, 1000, 1002, 21000, 100, 31000, 41002, 11000, 10, 21002,
-         2000, 3, 102, 32000, 40003, 10003, 1010, 3000, 1003, 21003, 1100, 33000, 41003, 1012, 20100, 2003, 12003, 103,
-         32001, 42003, 12000, 1013, 3003, 23003, 2103, 33001, 43003, 11010, 110, 22000, 2002, 2100, 42002, 13000, 3013,
-         23000, 3002, 1110, 43002, 12002, 2010, 22100, 3100, 42001, 3010, 13010, 23002, 2102, 43001, 12001, 2110,
-         23001, 3110, 3012, 2101, 3011),
+        (0, 101, 2, 20000, 30000, 40002, 10000, 1011, 1000, 1002, 21000, 2101, 31000, 41002, 10002, 10, 21002, 2000, 3,
+         100, 32000, 40003, 10003, 1010, 3000, 1003, 21003, 102, 33000, 41003, 11000, 1012, 22000, 2003, 103, 32001,
+         42003, 12003, 1013, 3003, 23003, 1100, 33001, 43003, 12000, 2010, 20100, 2002, 2103, 42002, 11010, 3013,
+         23000, 3002, 2100, 43002, 13000, 110, 23002, 1110, 42001, 12002, 3010, 22100, 3100, 43001, 13010, 3012, 23001,
+         2102, 2110, 3110, 3011),
     ),
     (
         (30002, 40002, 10002),
         (21002, 31002, 41002),
+        (12002,),
         (),
-        (),
-        (1, 102, 3, 10001, 30001, 40003, 10003, 1012, 23002, 1001, 1003, 21001, 101, 31001, 41003, 3012, 0, 2003,
-         10000, 20000, 103, 30000, 42003, 1011, 1000, 3003, 11000, 21000, 100, 31000, 43003, 10, 2000, 12000, 20100,
-         1100, 32000, 42002, 1010, 11010, 3000, 22000, 2100, 33000, 43002, 13000, 110, 2001, 23000, 1110, 32001, 12003,
-         2010, 3001, 22100, 3100, 33001, 3010, 13010, 21003, 2103, 32002, 12001, 2110, 23003, 3110, 33002, 12002, 1013,
-         23001, 2101, 3013, 2102, 3011),
+        (1, 102, 3, 30001, 40003, 10001, 23002, 1012, 1001, 1003, 21001, 2102, 31001, 41003, 10003, 3012, 0, 2003,
+         20000, 101, 30000, 42003, 10000, 1011, 1000, 3003, 21000, 103, 31000, 43003, 11000, 10, 2000, 22000, 100,
+         32000, 42002, 12000, 1010, 20100, 3000, 1100, 33000, 43002, 11010, 2010, 23000, 2001, 2100, 32001, 13000, 110,
+         22100, 3001, 1110, 33001, 3010, 13010, 21003, 3100, 32002, 12003, 2110, 23003, 3110, 33002, 12001, 1013,
+         23001, 2103, 3013, 2101, 3011),
     ),
     (
         (40003, 10003),
         (21003, 41003),
-        (42003, 12003),
+        (12003, 42003),
         (),
-        (2, 103, 10002, 1013, 23003, 1002, 21002, 102, 43003, 3013, 1, 10001, 2103, 1012, 1001, 21001, 101, 0, 10000,
+        (2, 103, 10002, 23003, 1013, 1002, 21002, 2103, 43003, 3013, 1, 10001, 102, 1012, 1001, 21001, 101, 0, 10000,
          20000, 1011, 1000, 21000, 11000, 100, 10, 20100, 2000, 12000, 1100, 1010, 22000, 11010, 3000, 2100, 110,
          13000, 23000, 2001, 1110, 2010, 22100, 12001, 3001, 3100, 3010, 13010, 23001, 2002, 2110, 2101, 12002, 3002,
          23002, 3110, 3011, 3012, 2102),
@@ -96,8 +97,8 @@
     chips_z = chips // 4
     n_out = 4 * chips_z + 4 * FIRST
     outs, rest = rest[:n_out], rest[n_out:]
-    (wb1, wb2, cw1, cw2, z_all, hb, eb, hcur, rh, re, ow1, ow2, acc1, acc2, own,
-     w1_sem, w2_sem, hs_sem, hr_sem, es_sem, er_sem, px_send, px_recv,
+    (wb1, wb2, own2, far2, cw1, cw2, z_all, hb, eb, hcur, rh, re, ow1, ow2, acc1, acc2, own,
+     w1_sem, w2_sem, x_send, x_recv, free_sem, hs_sem, hr_sem, es_sem, er_sem, px_send, px_recv,
      sp_send, sp_recv, tw_send, tw_recv, own_sem) = rest
 
     me = lax.axis_index("data")
@@ -118,23 +119,38 @@
     lax.fori_loop(0, chips, greet, 0)
     pl.semaphore_signal(barrier, inc=1, device_id=(partner,), device_id_type=MESH)
 
+    n_fwd, n_bwd = layers, layers - 1 - CACHED
+    top = layers - 1 - CACHED
+    n_steps = n_fwd + n_bwd
+
     def w1_copy(l, j, slot):
         return pltpu.make_async_copy(w1_hbm.at[l, :, pl.ds(pl.multiple_of(j * hc, 128), hc)], wb1.at[slot], w1_sem.at[slot])
 
-    def w2_copy(l, j, slot):
-        return pltpu.make_async_copy(w2_hbm.at[l, pl.ds(pl.multiple_of(j * hc, 128), hc), :], wb2.at[slot], w2_sem.at[slot])
-
-    def fetch(l, j, slot):
-        w1_copy(l, j, slot).start()
-        w2_copy(l, j, slot).start()
-
-    def arrived(l, j, slot):
-        w1_copy(l, j, slot).wait()
-        w2_copy(l, j, slot).wait()
-
-    for i in range(SLOTS):
-        fetch(i // 2, i % 2, i)
+    def w2_copy(l, slot):
+        return pltpu.make_async_copy(w2_hbm.at[l, pl.ds(pl.multiple_of(core * hc, 128), hc), :], wb2.at[slot], w2_sem.at[slot])
+
+    def pass_copy(step):
+        at = step % RING
+        return pltpu.make_async_remote_copy(
+            src_ref=own2.at[at], dst_ref=far2.at[at], send_sem=x_send.at[at], recv_sem=x_recv.at[at],
+            device_id=(partner,), device_id_type=MESH)
+
+    def take_in(step):
+        own2[step % RING] = wb2[step % 2].astype(BF16)
+
+    def chunk(m):
+        return (core + m) % 2
+
+    for step in range(2):
+        w2_copy(step, step).start()
+        for m in range(2):
+            w1_copy(step, chunk(m), 2 * step + m).start()
     pl.semaphore_wait(barrier, chips)
+    for step in range(2):
+        w2_copy(step, step).wait()
+        take_in(step)
+        pass_copy(step).start()
+        w2_copy(step + 2, step).start()
 
     def h_copy(l):
         return pltpu.make_async_remote_copy(
@@ -174,41 +190,61 @@
         def _():
             re[core * chips + chip] = eb[l]
 
-    n_fwd = 2 * layers
-    n_bwd = 2 * (layers - 1 - CACHED)
     hcur[...] = x_ref[...].astype(F32)
 
-    def forward(i, carry):
-        l, j, slot = i // 2, i % 2, i % SLOTS
-        arrived(l, j, slot)
-
-        @pl.when(j == 0)
-        def _():
-            hb[l] = hcur[...].astype(BF16)
-
-        z = mm(hb[l], wb1[slot].astype(BF16))
-        z_all[i] = z
-        hcur[...] += mm(gelu(z).astype(BF16), wb2[slot].astype(BF16))
-
-        @pl.when(l >= layers - CACHED)
-        def _():
-            cw1[i - (n_fwd - 2 * CACHED)] = wb1[slot].astype(BF16)
-            cw2[i - (n_fwd - 2 * CACHED)] = wb2[slot].astype(BF16)
-
-        nxt = i + SLOTS
-
-        @pl.when(nxt < n_fwd)
-        def _():
-            fetch(nxt // 2, nxt % 2, slot)
-
-        @pl.when(nxt >= n_fwd)
-        def _():
-            fetch(layers - 1 - CACHED - (nxt - n_fwd) // 2, nxt % 2, slot)
-
-        @pl.when(j == 1)
-        def _():
-            send_h(l)
-
+    def ahead(step):
+        @pl.when(step >= 1)
+        def _():
+            pass_copy(step - 1).wait_send()
+            pl.semaphore_wait(free_sem.at[(step + 2) % RING], 1)
+
+        w2_copy(0, step % 2).wait()
+        take_in(step + 2)
+
+    def release(step):
+        @pl.when(step <= n_steps - 1 - RING)
+        def _():
+            pl.semaphore_signal(free_sem.at[step % RING], inc=1, device_id=(partner,), device_id_type=MESH)
+
+    def forward(step, carry):
+        ahead(step)
+
+        @pl.when(step + 4 < n_fwd)
+        def _():
+            w2_copy(step + 4, step % 2).start()
+
+        @pl.when(step + 4 >= n_fwd)
+        def _():
+            w2_copy(top - (step + 4 - n_fwd), step % 2).start()
+
+        hb[step] = hcur[...].astype(BF16)
+        for m in range(2):
+            j, slot = chunk(m), (2 * step + m) % SLOTS
+            w1_copy(0, 0, slot).wait()
+            if m == 1:
+                pass_copy(step).wait_recv()
+            w2 = own2 if m == 0 else far2
+            z = mm(hb[step], wb1[slot].astype(BF16))
+            z_all[2 * step + j] = z
+            hcur[...] += mm(gelu(z).astype(BF16), w2[step % RING])
+            if m == 0:
+                pass_copy(step + 2).start()
+
+            @pl.when(step >= layers - CACHED)
+            def _(m=m, j=j, slot=slot, w2=w2):
+                kept = 2 * (step - (layers - CACHED)) + j
+                cw1[kept] = wb1[slot].astype(BF16)
+                cw2[kept] = w2[step % RING]
+
+            @pl.when(step + 2 < n_fwd)
+            def _(j=j, slot=slot):
+                w1_copy(step + 2, j, slot).start()
+
+            @pl.when(step + 2 >= n_fwd)
+            def _(j=j, slot=slot):
+                w1_copy(top - (step + 2 - n_fwd), j, slot).start()
+        release(step)
+        send_h(step)
         return carry
 
     lax.fori_loop(0, n_fwd, forward, 0)
@@ -224,53 +260,64 @@
         send_sem=px_send.at[1], recv_sem=px_recv.at[1], device_id=(partner,), device_id_type=MESH)
 
     def error_step(l, j, w1, w2):
-        @pl.when(j == 0)
-        def _():
-            eb[l] = hcur[...].astype(BF16)
-
         q = mm(eb[l], w2, NT)
         slope = gelu_grad(z_all[2 * l + j])[1]
         hcur[...] += mm((slope * q).astype(BF16), w1, NT)
 
     def backward_cached(i, carry):
-        l, j = layers - 1 - i // 2, i % 2
-        kept = 2 * (l - (layers - CACHED)) + j
-        error_step(l, j, cw1[kept], cw2[kept])
-
-        @pl.when(j == 1)
-        def _():
-            send_e(l)
-
+        l = layers - 1 - i
+        eb[l] = hcur[...].astype(BF16)
+        for j in range(2):
+            kept = 2 * (l - (layers - CACHED)) + j
+            error_step(l, j, cw1[kept], cw2[kept])
+        send_e(l)
         return carry
 
     def backward(i, carry):
-        l, j, slot = layers - 1 - CACHED - i // 2, i % 2, i % SLOTS
-        arrived(l, j, slot)
-        error_step(l, j, wb1[slot].astype(BF16), wb2[slot].astype(BF16))
-        nxt = i + SLOTS
-
-        @pl.when(nxt < n_bwd)
-        def _():
-            fetch(layers - 1 - CACHED - nxt // 2, nxt % 2, slot)
-
-        @pl.when(nxt == n_bwd)
-        def _():
-            fetch(chip, core, slot)
-
-        @pl.when(j == 1)
-        def _():
-            send_e(l)
-
+        l, step = top - i, n_fwd + i
+
+        @pl.when(step + 2 < n_steps)
+        def _():
+            ahead(step)
+
+        @pl.when(step + 4 < n_steps)
+        def _():
+            w2_copy(l - 4, step % 2).start()
+
+        @pl.when(step + 4 == n_steps)
+        def _():
+            w2_copy(chip, step % 2).start()
+
+        eb[l] = hcur[...].astype(BF16)
+        for m in range(2):
+            j, slot = chunk(m), (2 * step + m) % SLOTS
+            w1_copy(0, 0, slot).wait()
+            if m == 1:
+                pass_copy(step).wait_recv()
+            error_step(l, j, wb1[slot].astype(BF16), (own2 if m == 0 else far2)[step % RING])
+
+            @pl.when(step + 2 < n_steps)
+            def _(m=m, j=j, slot=slot):
+                if m == 0:
+                    pass_copy(step + 2).start()
+                w1_copy(l - 2, j, slot).start()
+
+            if m == 0:
+                @pl.when(step + 2 == n_steps)
+                def _(j=j, slot=slot):
+                    w1_copy(chip, j, slot).start()
+        release(step)
+        send_e(l)
         return carry
 
-    lax.fori_loop(0, 2 * CACHED, backward_cached, 0)
+    lax.fori_loop(0, CACHED, backward_cached, 0)
     lax.fori_loop(0, n_bwd, backward, 0)
     eb[0] = hcur[...].astype(BF16)
 
-    own_slot = n_bwd % SLOTS
-    arrived(chip, core, own_slot)
-    ow1[...] = wb1[own_slot].astype(BF16)
-    ow2[...] = wb2[own_slot].astype(BF16)
+    w1_copy(0, 0, (2 * n_steps) % SLOTS).wait()
+    w2_copy(0, n_steps % 2).wait()
+    ow1[...] = wb1[(2 * n_steps) % SLOTS].astype(BF16)
+    ow2[...] = wb2[n_steps % 2].astype(BF16)
     send_e(0)
 
     def h_in(c, carry):
@@ -306,16 +353,18 @@
 
     hops = (chip + 1 - 2 * cx, chip + 2 - 4 * cy, chip + 4, chip - 4)
 
-    def hop_copy(kind, n, rx, ry, sz, mine):
+    def hop_copy(kind, n, rx, ry, sz, mine, part=None):
         src = source(rx, ry, sz)
         there = (n, 1 - rx if kind == 0 else rx, 1 - ry if kind == 1 else ry, sz, 0)
         tx, ty = there[1], there[2]
         inner = (1 - cx if rx else cx) if n % 2 == 0 else (1 - cy if ry else cy)
         far = ty if n % 2 == 0 else tx
         at = 4 * chips_z + 4 * sz + 2 * (n % 2) if far else 4 * sz + 2 * (n % 2)
+        src_ref, dst_ref = own.at[n] if mine else place(n, rx, ry, sz, 0), outs[at].at[inner, n // 2]
+        if part is not None:
+            src_ref, dst_ref = src_ref.at[part], dst_ref.at[part]
         return pltpu.make_async_remote_copy(
-            src_ref=own.at[n] if mine else place(n, rx, ry, sz, 0), dst_ref=outs[at].at[inner, n // 2],
-            send_sem=sp_send.at[n, kind, src], recv_sem=sp_recv.at[n, src],
+            src_ref=src_ref, dst_ref=dst_ref, send_sem=sp_send.at[n, kind, src], recv_sem=sp_recv.at[n, src],
             device_id=(2 * hops[kind] + core,), device_id_type=MESH)
 
     def arrival(n, rx, ry, sz):
@@ -348,47 +397,93 @@
     group = 4
     half_groups = chips // group
 
-    for n in range(QUARTERS):
-        cols = slice(n * piece, (n + 1) * piece)
-        acc1[...] = jnp.zeros_like(acc1)
-        acc2[...] = jnp.zeros_like(acc2)
-
-        def owner(gi, carry, n=n, cols=cols):
-            half = (core + gi // half_groups) % 2
-            if n == 0:
+    def row_groups(body, wait=False):
+        def step(gi, carry):
+            if wait:
                 @pl.when(gi == half_groups)
                 def _():
                     h_swap.wait_recv()
                     e_swap.wait_recv()
 
+            half = (core + gi // half_groups) % 2
             base = half * chips + (gi % half_groups) * group
-            hg = rh[pl.ds(base, group)].reshape(group * rows, d)
-            eg = re[pl.ds(base, group)].reshape(group * rows, d)
-            z = mm(hg, ow1[:, cols])
+            body(base, rh[pl.ds(base, group)].reshape(group * rows, d), re[pl.ds(base, group)].reshape(group * rows, d))
+            return carry
+
+        lax.fori_loop(0, 2 * half_groups, step, 0)
+
+    def add_in(base, s):
+        for b in range(group):
+            acc1[...] += mm(rh[base + b], s[b * rows:(b + 1) * rows], TN).astype(BF16).astype(F32)
+
+    def add_out(base, a):
+        for b in range(group):
+            acc2[...] += mm(a[b * rows:(b + 1) * rows], re[base + b], TN).astype(BF16).astype(F32)
+
+    def store_in(n):
+        for cb in range(piece // 128):
+            own[n, 0, cb * d:(cb + 1) * d, :] = acc1[:, cb * 128:(cb + 1) * 128].astype(BF16)
+
+    def store_out(n):
+        for lb in range(d // 128):
+            own[n, 1, lb * piece:(lb + 1) * piece, :] = acc2[:, lb * 128:(lb + 1) * 128].astype(BF16)
+
+    def send_part(part):
+        def start(z):
+            for code in RELAYS[z][0]:
+                kind, block = split(code)
+                hop_copy(kind - 1, *block, True, part).start()
+
+        at_z(start)
+
+    acc1[...] = jnp.zeros_like(acc1)
+    acc2[...] = jnp.zeros_like(acc2)
+
+    def first_out(base, hg, eg):
+        a, slope = gelu_grad(mm(hg, ow1[:, :piece]))
+        z_all[pl.ds(base, group), :, :piece] = slope.reshape(group, rows, piece)
+        add_out(base, a.astype(BF16))
+
+    def first_in(base, hg, eg):
+        q = mm(eg, ow2[:piece, :], NT)
+        add_in(base, (z_all[pl.ds(base, group), :, :piece].reshape(group * rows, piece) * q).astype(BF16))
+
+    row_groups(first_out, wait=True)
+    store_out(0)
+    send_part(1)
+    row_groups(first_in)
+    store_in(0)
+    send_part(0)
+
+    def start_rest(n):
+        def start(z):
+            for code in RELAYS[z][n] if n else ():
+                act(z, code)
+            twin_copy(n, 0, 0, z, True).start()
+            pltpu.make_async_copy(own.at[n], place(n, 0, 0, z, 0), own_sem.at[n]).start()
+
+        at_z(start)
+
+    start_rest(0)
+    for n in range(1, QUARTERS):
+        cols = slice(n * piece, (n + 1) * piece)
+        acc1[...] = jnp.zeros_like(acc1)
+        acc2[...] = jnp.zeros_like(acc2)
+
+        def both(base, hg, eg, cols=cols):
+            a, slope = gelu_grad(mm(hg, ow1[:, cols]))
             q = mm(eg, ow2[cols, :], NT)
-            a, slope = gelu_grad(z)
             a = a.astype(BF16)
             s = (slope * q).astype(BF16)
             for b in range(group):
                 own_rows = slice(b * rows, (b + 1) * rows)
                 acc1[...] += mm(rh[base + b], s[own_rows], TN).astype(BF16).astype(F32)
                 acc2[...] += mm(a[own_rows], re[base + b], TN).astype(BF16).astype(F32)
-            return carry
-
-        lax.fori_loop(0, 2 * half_groups, owner, 0)
-        for cb in range(piece // 128):
-            own[n, cb * d:(cb + 1) * d, :] = acc1[:, cb * 128:(cb + 1) * 128].astype(BF16)
-        off = (piece // 128) * d
-        for lb in range(d // 128):
-            own[n, off + lb * piece:off + (lb + 1) * piece, :] = acc2[:, lb * 128:(lb + 1) * 128].astype(BF16)
-
-        def start_own(z, n=n):
-            for code in RELAYS[z][n]:
-                act(z, code)
-            twin_copy(n, 0, 0, z, True).start()
-            pltpu.make_async_copy(own.at[n], place(n, 0, 0, z, 0), own_sem.at[n]).start()
-
-        at_z(start_own)
+
+        row_groups(both)
+        store_in(n)
+        store_out(n)
+        start_rest(n)
 
     def relay(z):
         for code in RELAYS[z][QUARTERS]:
@@ -407,6 +502,8 @@
     lax.fori_loop(0, layers, sent, 0)
     h_swap.wait_send()
     e_swap.wait_send()
+    for step in range(n_steps - RING, n_steps):
+        pass_copy(step).wait_send()
 
     def drain(z):
         for n in range(QUARTERS):
@@ -427,18 +524,20 @@
     rows = x.shape[0]
     hc = hid // 2
     piece = hc // QUARTERS
-    g_rows = (piece // 128) * d + (d // 128) * piece
+    part_rows = piece * d // 128
     dims = (n_dev, layers, rows, d, hid)
     n_out = n_dev // 2 + 4 * FIRST
     flops = 2 * rows * d * hid * layers * 4 + 2 * rows * n_dev * d * hc * 4
     return pl.pallas_call(
         functools.partial(grads_kernel, dims),
-        out_shape=[jax.ShapeDtypeStruct((2, QUARTERS // 2, g_rows, 128), BF16)] * n_out,
+        out_shape=[jax.ShapeDtypeStruct((2, QUARTERS // 2, 2, part_rows, 128), BF16)] * n_out,
         in_specs=[pl.BlockSpec(memory_space=pl.ANY)] * 2 + [pl.BlockSpec(memory_space=pltpu.VMEM)] * 2,
         out_specs=[pl.BlockSpec(memory_space=pl.ANY)] * n_out,
         scratch_shapes=[
             pltpu.VMEM((SLOTS, d, hc), F32),
-            pltpu.VMEM((SLOTS, hc, d), F32),
+            pltpu.VMEM((2, hc, d), F32),
+            pltpu.VMEM((RING, hc, d), BF16),
+            pltpu.VMEM((RING, hc, d), BF16),
             pltpu.VMEM((2 * CACHED, d, hc), BF16),
             pltpu.VMEM((2 * CACHED, hc, d), BF16),
             pltpu.VMEM((2 * layers, rows, hc), F32),
@@ -451,9 +550,12 @@
             pltpu.VMEM((hc, d), BF16),
             pltpu.VMEM((d, piece), F32),
             pltpu.VMEM((piece, d), F32),
-            pltpu.VMEM((QUARTERS, g_rows, 128), BF16),
+            pltpu.VMEM((QUARTERS, 2, part_rows, 128), BF16),
             pltpu.SemaphoreType.DMA((SLOTS,)),
-            pltpu.SemaphoreType.DMA((SLOTS,)),
+            pltpu.SemaphoreType.DMA((2,)),
+            pltpu.SemaphoreType.DMA((RING,)),
+            pltpu.SemaphoreType.DMA((RING,)),
+            pltpu.SemaphoreType.REGULAR((RING,)),
             pltpu.SemaphoreType.DMA((layers,)),
             pltpu.SemaphoreType.DMA((layers,)),
             pltpu.SemaphoreType.DMA((layers,)),
@@ -525,7 +627,6 @@
     for t in range(AHEAD):
         fetch(t, t)
     h_out[...] = h_in[...].astype(F32)
-    off = (piece // 128) * d
 
     def body(t, carry):
         slot = t % slots
@@ -540,7 +641,7 @@
             pltpu.make_async_copy(sums[0].at[0, 0], gbuf.at[slot, par], gsem.at[par, slot]).wait()
             for cb in range(piece // 128):
                 cols = slice(par * piece + cb * 128, par * piece + (cb + 1) * 128)
-                mn = MOMENTUM * bm1[slot, :, cols] + gbuf[slot, par, cb * d:(cb + 1) * d, :].astype(F32)
+                mn = MOMENTUM * bm1[slot, :, cols] + gbuf[slot, par, 0, cb * d:(cb + 1) * d, :].astype(F32)
                 wn = bw1[slot, :, cols] - step_size * mn
                 bm1[slot, :, cols] = mn
                 bw1[slot, :, cols] = wn
@@ -548,7 +649,7 @@
             hid_rows = slice(par * piece, (par + 1) * piece)
             for lb in range(d // 128):
                 cols = slice(lb * 128, (lb + 1) * 128)
-                mn = MOMENTUM * bm2[slot, hid_rows, cols] + gbuf[slot, par, off + lb * piece:off + (lb + 1) * piece, :].astype(F32)
+                mn = MOMENTUM * bm2[slot, hid_rows, cols] + gbuf[slot, par, 1, lb * piece:(lb + 1) * piece, :].astype(F32)
                 wn = bw2[slot, hid_rows, cols] - step_size * mn
                 bm2[slot, hid_rows, cols] = mn
                 bw2[slot, hid_rows, cols] = wn

time: 548 us -> 547 us (level); the launches traced: 546 us -> 539 us
  Pallas kernels: 449 us -> 442 us
    pallas_call x1, Pallas kernels: 249 us -> 242 us  [local_grads(): pl.pallas_call(functools.partial(grads_kernel, dims), out_shape=[jax.Shap...]
  transfers between devices with their start and end apart: 12 -> 12, of which waited for: 2 -> 2; matrix products, arithmetic and copies ran while one was open for 0% -> 0% of each run, Pallas kernels for 27% -> 28%
where the time goes in v6:
time: 547 us; the launch traced here: 539 us
  Pallas kernels  442 us (81%)
  waiting for transfers between devices  87.6 us (16%)
  starting transfers between devices  8.75 us (2%)
    pallas_call x1, Pallas kernels, local_grads(): pl.pallas_call(functools.partial(grads_kernel, dims), out_shape=[jax.Shap...  242 us
    pallas_call x4, Pallas kernels, update(): pl.pallas_call(functools.partial(update_kernel, (layers, rows, d, piece),...  200 us
    ppermute x12, waiting for transfers between devices, send(): return lax.ppermute(array, 'data', swap[axis])  87.6 us
  transfers between devices with their start and end apart: 12, of which 2 were waited for; matrix products, arithmetic and copies ran while one was open for 0% of the time, Pallas kernels for 28%

profile of v6, /device:TPU:0, one launch (start us, length us, event | category | flops | bytes accessed | tf_op | source)
XLA Modules:
  0.0 539.2 jit_solution(9128898987313958531)
XLA Ops:
  0.6 242.1 %local_grads.1 = (bf16[2,2,2,1024,128]{4,3,2,1,0:T(8,128)(2,1)}, bf16[2,2,2,1024,128]{4,3,2,1,0:T(8,128)(2,1)}, bf16[2,2,2,1024,128]{4,3,2,1,0:T(8,128)(2,1)}, b...) custom-call(f32[16,512,2048]{2,1,0:T(8,128)} %refs_0_.7, ...), custom_call_target="tpu_custom_call" | custom-call | flops 17179869184 | bytes 268435456 | tf_op jit(solution)/shard_map/local_grads/pallas_call | solution.py:531
  242.8 3.2 collective-permute-start
  246.0 0.1 collective-permute-start.2
  246.1 0.1 collective-permute-start.4
  246.2 1.9 collective-permute-start.6
  248.1 0.1 collective-permute-start.10
  248.2 44.6 %collective-permute-done.refs_9_ = bf16[2,2,2,1024,128]{4,3,2,1,0:T(8,128)(2,1)} collective-permute-done((bf16[2,2,2,1024,128]{4,3,2,1,0:T(8,128)(2,1)}, bf16[2,2,2,1024,128]{4,3,2,1,0:T(8,128)(2,1)}, u32[]{:S(2)}, u32[]{:S(2)}) %collective-permute-start) | collective-permute-done | bytes 2097184 | tf_op jit(solution)/shard_map/ppermute | solution.py:731
  292.8 2.0 collective-permute-start.8
  294.8 0.0 collective-permute-done.2.refs_11_
  294.8 0.0 collective-permute-start.1
  294.8 42.9 %collective-permute-done.4.refs_9_ = bf16[2,2,2,1024,128]{4,3,2,1,0:T(8,128)(2,1)} collective-permute-done((bf16[2,2,2,1024,128]{4,3,2,1,0:T(8,128)(2,1)}, bf16[2,2,2,1024,128]{4,3,2,1,0:T(8,128)(2,1)}, u32[]{:S(2)}, u32[]{:S(2)}) %collective-permute-start.4) | collective-permute-done | bytes 2097184 | tf_op jit(solution)/shard_map/ppermute | solution.py:731
  337.8 0.0 collective-permute-start.3
  337.8 49.9 %shard_map.127 = (f32[16,512,2048]{2,1,0:T(8,128)}, f32[16,2048,512]{2,1,0:T(8,128)}, f32[16,512,2048]{2,1,0:T(8,128)}, f32[16,2048,512]{2,1,0:T(8,128)}, f32[64,512]{1,0:T(8,128)}) custom-call(f32[16,512,2048]{2,1,0:T(8,128)} %refs_0_.7, f32[16,512,2048]{2,1,0:T(8,128)} %refs_1_.7, f32[16,2048,512]{2,1,0:T(8,128)} %refs_2_.7, f32[16,2048,512]{2,1,0:T(8,128)} %refs_3_.7, ...), custom_call_target="tpu_custom_call" | custom-call | flops 49999998976 | bytes 150994944 | tf_op jit(solution)/shard_map/pallas_call | solution.py:701
  387.7 0.0 collective-permute-done.6.refs_11_
  387.7 0.7 collective-permute-start.5
  388.4 0.0 collective-permute-done.10.refs_11_
  388.4 0.1 collective-permute-start.7
  388.5 0.0 collective-permute-done.8.refs_9_
  388.5 0.4 collective-permute-start.11
  388.9 0.0 collective-permute-done.1.refs_10_
  388.9 0.1 collective-permute-start.9
  389.0 0.0 collective-permute-done.3.refs_12_
  389.0 50.0 %shard_map.128 = (f32[16,512,2048]{2,1,0:T(8,128)}, f32[16,2048,512]{2,1,0:T(8,128)}, f32[16,512,2048]{2,1,0:T(8,128)}, f32[16,2048,512]{2,1,0:T(8,128)}, f32[64,512]{1,0:T(8,128)}) custom-call(f32[16,512,2048]{2,1,0:T(8,128)} %refs_0_.7, f32[16,512,2048]{2,1,0:T(8,128)} %refs_1_.7, ...), custom_call_target="tpu_custom_call", output_to_operand_aliasing={{0}: (13, {}), {1}: (14, {}), {2}: (15, {}), {3}: (16, {})} | custom-call | flops 49999998976 | bytes 150994944 | tf_op jit(solution)/shard_map/pallas_call | solution.py:701
  439.0 0.0 collective-permute-done.5.refs_10_
  439.0 0.0 collective-permute-done.7.refs_12_
  439.0 50.0 %shard_map.129 = (f32[16,512,2048]{2,1,0:T(8,128)}, f32[16,2048,512]{2,1,0:T(8,128)}, f32[16,512,2048]{2,1,0:T(8,128)}, f32[16,2048,512]{2,1,0:T(8,128)}, f32[64,512]{1,0:T(8,128)}) custom-call(f32[16,512,2048]{2,1,0:T(8,128)} %refs_0_.7, f32[16,512,2048]{2,1,0:T(8,128)} %refs_1_.7, ...), custom_call_target="tpu_custom_call", output_to_operand_aliasing={{0}: (13, {}), {1}: (14, {}), {2}: (15, {}), {3}: (16, {})} | custom-call | flops 49999998976 | bytes 150994944 | tf_op jit(solution)/shard_map/pallas_call | solution.py:701
  489.0 0.0 collective-permute-done.11.refs_12_
  489.0 0.0 collective-permute-done.9.refs_10_
  489.0 50.0 %shard_map.130 = (f32[16,512,2048]{2,1,0:T(8,128)}, f32[16,2048,512]{2,1,0:T(8,128)}, f32[16,512,2048]{2,1,0:T(8,128)}, f32[16,2048,512]{2,1,0:T(8,128)}, f32[64,512]{1,0:T(8,128)}, /*index=5*/f32[64]{0:T(128)}) custom-call(f32[16,512,2048]{2,1,0:T(8,128)} %refs_0_.7, ...), custom_call_target="tpu_custom_call", output_to_operand_aliasing={{0}: (13, {}), {1}: (14, {}), {2}: (15, {}), {3}: (16, {})} | custom-call | flops 49999998976 | bytes 150994944 | tf_op jit(solution)/shard_map/pallas_call | solution.py:701
Async XLA Ops:
  242.8 50.0 %collective-permute-start = (bf16[2,2,2,1024,128]{4,3,2,1,0:T(8,128)(2,1)}, bf16[2,2,2,1024,128]{4,3,2,1,0:T(8,128)(2,1)}, u32[]{:S(2)}, u32[]{:S(2)}) collective-permute-start(bf16[2,2,2,1024,128]{4,3,2,1,0:T(8,128)(2,1)} %get-tuple-element.56.refs_5_), channel_id=1, source_target_pairs={{0,4},{1,5},{2,6},{3,7},{4,0},{5,1},{6,2},{7,3},{8,12},{9,13},{10,... | collective-permute-start | bytes 6291464 | tf_op jit(solution)/shard_map/ppermute | solution.py:731
  246.0 48.8 %collective-permute-start.2 = (bf16[2,2,2,1024,128]{4,3,2,1,0:T(8,128)(2,1)}, bf16[2,2,2,1024,128]{4,3,2,1,0:T(8,128)(2,1)}, u32[]{:S(2)}, u32[]{:S(2)}) collective-permute-start(bf16[2,2,2,1024,128]{4,3,2,1,0:T(8,128)(2,1)} %get-tuple-element.58.refs_7_), channel_id=1, source_target_pairs={{0,2},{1,3},{2,0},{3,1},{4,6},{5,7},{6,4},{7,5},{8,10},{9,11},{10,... | collective-permute-start | bytes 6291464 | tf_op jit(solution)/shard_map/ppermute | solution.py:731
  246.1 91.7 %collective-permute-start.4 = (bf16[2,2,2,1024,128]{4,3,2,1,0:T(8,128)(2,1)}, bf16[2,2,2,1024,128]{4,3,2,1,0:T(8,128)(2,1)}, u32[]{:S(2)}, u32[]{:S(2)}) collective-permute-start(bf16[2,2,2,1024,128]{4,3,2,1,0:T(8,128)(2,1)} %get-tuple-element.65.refs_5_), channel_id=1, source_target_pairs={{0,4},{1,5},{2,6},{3,7},{4,0},{5,1},{6,2},{7,3},{8,12},{9,13},{10,... | collective-permute-start | bytes 6291464 | tf_op jit(solution)/shard_map/ppermute | solution.py:731
  246.2 141.5 %collective-permute-start.6 = (bf16[2,2,2,1024,128]{4,3,2,1,0:T(8,128)(2,1)}, bf16[2,2,2,1024,128]{4,3,2,1,0:T(8,128)(2,1)}, u32[]{:S(2)}, u32[]{:S(2)}) collective-permute-start(bf16[2,2,2,1024,128]{4,3,2,1,0:T(8,128)(2,1)} %get-tuple-element.67.refs_7_), channel_id=1, source_target_pairs={{0,2},{1,3},{2,0},{3,1},{4,6},{5,7},{6,4},{7,5},{8,10},{9,11},{10,... | collective-permute-start | bytes 6291464 | tf_op jit(solution)/shard_map/ppermute | solution.py:731
  248.1 140.3 %collective-permute-start.10 = (bf16[2,2,2,1024,128]{4,3,2,1,0:T(8,128)(2,1)}, bf16[2,2,2,1024,128]{4,3,2,1,0:T(8,128)(2,1)}, u32[]{:S(2)}, u32[]{:S(2)}) collective-permute-start(bf16[2,2,2,1024,128]{4,3,2,1,0:T(8,128)(2,1)} %get-tuple-element.76.refs_7_), channel_id=1, source_target_pairs={{0,2},{1,3},{2,0},{3,1},{4,6},{5,7},{6,4},{7,5},{8,10},{9,11},{10,... | collective-permute-start | bytes 6291464 | tf_op jit(solution)/shard_map/ppermute | solution.py:731
  292.8 95.7 %collective-permute-start.8 = (bf16[2,2,2,1024,128]{4,3,2,1,0:T(8,128)(2,1)}, bf16[2,2,2,1024,128]{4,3,2,1,0:T(8,128)(2,1)}, u32[]{:S(2)}, u32[]{:S(2)}) collective-permute-start(bf16[2,2,2,1024,128]{4,3,2,1,0:T(8,128)(2,1)} %get-tuple-element.74.refs_5_), channel_id=1, source_target_pairs={{0,4},{1,5},{2,6},{3,7},{4,0},{5,1},{6,2},{7,3},{8,12},{9,13},{10,... | collective-permute-start | bytes 6291464 | tf_op jit(solution)/shard_map/ppermute | solution.py:731
  294.8 94.1 %collective-permute-start.1 = (bf16[2,2,2,1024,128]{4,3,2,1,0:T(8,128)(2,1)}, bf16[2,2,2,1024,128]{4,3,2,1,0:T(8,128)(2,1)}, u32[]{:S(2)}, u32[]{:S(2)}) collective-permute-start(bf16[2,2,2,1024,128]{4,3,2,1,0:T(8,128)(2,1)} %collective-permute-done.refs_9_), channel_id=1, source_target_pairs={{0,1},{1,0},{2,3},{3,2},{4,5},{5,4},{6,7},{7,6},{8,9},{9,8},{10,11... | collective-permute-start | bytes 6291464 | tf_op jit(solution)/shard_map/ppermute | solution.py:731
  337.8 51.3 %collective-permute-start.3 = (bf16[2,2,2,1024,128]{4,3,2,1,0:T(8,128)(2,1)}, bf16[2,2,2,1024,128]{4,3,2,1,0:T(8,128)(2,1)}, u32[]{:S(2)}, u32[]{:S(2)}) collective-permute-start(bf16[2,2,2,1024,128]{4,3,2,1,0:T(8,128)(2,1)} %collective-permute-done.2.refs_11_), channel_id=1, source_target_pairs={{0,1},{1,0},{2,3},{3,2},{4,5},{5,4},{6,7},{7,6},{8,9},{9,8},{10,11... | collective-permute-start | bytes 6291464 | tf_op jit(solution)/shard_map/ppermute | solution.py:731
  387.7 51.3 %collective-permute-start.5 = (bf16[2,2,2,1024,128]{4,3,2,1,0:T(8,128)(2,1)}, bf16[2,2,2,1024,128]{4,3,2,1,0:T(8,128)(2,1)}, u32[]{:S(2)}, u32[]{:S(2)}) collective-permute-start(bf16[2,2,2,1024,128]{4,3,2,1,0:T(8,128)(2,1)} %collective-permute-done.4.refs_9_), channel_id=1, source_target_pairs={{0,1},{1,0},{2,3},{3,2},{4,5},{5,4},{6,7},{7,6},{8,9},{9,8},{10,11... | collective-permute-start | bytes 6291464 | tf_op jit(solution)/shard_map/ppermute | solution.py:731
  388.4 50.6 %collective-permute-start.7 = (bf16[2,2,2,1024,128]{4,3,2,1,0:T(8,128)(2,1)}, bf16[2,2,2,1024,128]{4,3,2,1,0:T(8,128)(2,1)}, u32[]{:S(2)}, u32[]{:S(2)}) collective-permute-start(bf16[2,2,2,1024,128]{4,3,2,1,0:T(8,128)(2,1)} %collective-permute-done.6.refs_11_), channel_id=1, source_target_pairs={{0,1},{1,0},{2,3},{3,2},{4,5},{5,4},{6,7},{7,6},{8,9},{9,8},{10,11... | collective-permute-start | bytes 6291464 | tf_op jit(solution)/shard_map/ppermute | solution.py:731
  388.5 100.5 %collective-permute-start.11 = (bf16[2,2,2,1024,128]{4,3,2,1,0:T(8,128)(2,1)}, bf16[2,2,2,1024,128]{4,3,2,1,0:T(8,128)(2,1)}, u32[]{:S(2)}, u32[]{:S(2)}) collective-permute-start(bf16[2,2,2,1024,128]{4,3,2,1,0:T(8,128)(2,1)} %collective-permute-done.10.refs_11_), channel_id=1, source_target_pairs={{0,1},{1,0},{2,3},{3,2},{4,5},{5,4},{6,7},{7,6},{8,9},{9,8},{10,11... | collective-permute-start | bytes 6291464 | tf_op jit(solution)/shard_map/ppermute | solution.py:731
  388.9 100.1 %collective-permute-start.9 = (bf16[2,2,2,1024,128]{4,3,2,1,0:T(8,128)(2,1)}, bf16[2,2,2,1024,128]{4,3,2,1,0:T(8,128)(2,1)}, u32[]{:S(2)}, u32[]{:S(2)}) collective-permute-start(bf16[2,2,2,1024,128]{4,3,2,1,0:T(8,128)(2,1)} %collective-permute-done.8.refs_9_), channel_id=1, source_target_pairs={{0,1},{1,0},{2,3},{3,2},{4,5},{5,4},{6,7},{7,6},{8,9},{9,8},{10,11... | collective-permute-start | bytes 6291464 | tf_op jit(solution)/shard_map/ppermute | solution.py:731

commit v7 on v6

--- a/solution.py
+++ b/solution.py
@@ -25,44 +25,41 @@
     (
         (30000, 10000, 20000),
         (31000, 11000, 21000),
-        (32000, 22000),
+        (100, 10, 1, 10001, 20100, 32000),
         (),
-        (100, 10, 1, 10001, 1100, 1010, 1001, 33000, 12000, 21001, 101, 2010, 2, 10002, 20100, 2100, 1011, 1002, 13000,
-         21002, 102, 110, 3, 10003, 23000, 3100, 1012, 1003, 11010, 21003, 103, 3010, 2003, 12003, 22100, 1110, 1013,
-         3003, 13010, 23003, 2103, 2110, 2002, 12002, 3110, 3013, 3002, 23002, 2102, 2001, 12001, 3012, 3001, 23001,
-         2101, 3011),
+        (33000, 12000, 1100, 1010, 1001, 21001, 22000, 101, 110, 2, 10002, 13000, 2100, 1011, 1002, 21002, 23000, 102,
+         2010, 3, 10003, 11010, 3100, 1012, 1003, 21003, 22100, 103, 3010, 2003, 12003, 13010, 1110, 1013, 3003, 23003,
+         2103, 2110, 2002, 12002, 3110, 3013, 3002, 23002, 2102, 2001, 12001, 3012, 3001, 23001, 2101, 3011),
     ),
     (
         (30001, 40001, 10001),
         (21001, 31001, 41001),
-        (12001,),
+        (0, 101, 2, 10000, 20000, 30000, 40002, 10002),
         (),
-        (0, 101, 2, 20000, 30000, 40002, 10000, 1011, 1000, 1002, 21000, 2101, 31000, 41002, 10002, 10, 21002, 2000, 3,
-         100, 32000, 40003, 10003, 1010, 3000, 1003, 21003, 102, 33000, 41003, 11000, 1012, 22000, 2003, 103, 32001,
-         42003, 12003, 1013, 3003, 23003, 1100, 33001, 43003, 12000, 2010, 20100, 2002, 2103, 42002, 11010, 3013,
-         23000, 3002, 2100, 43002, 13000, 110, 23002, 1110, 42001, 12002, 3010, 22100, 3100, 43001, 13010, 3012, 23001,
-         2102, 2110, 3110, 3011),
+        (1011, 1000, 1002, 21000, 31000, 41002, 11000, 100, 21002, 10, 2000, 3, 32000, 40003, 10003, 102, 1010, 3000,
+         1003, 21003, 33000, 41003, 1100, 20100, 32001, 1012, 2003, 12003, 42003, 12000, 103, 33001, 1013, 3003, 23003,
+         43003, 11010, 2103, 22000, 110, 2002, 42002, 13000, 2100, 23000, 3013, 3002, 43002, 12002, 1110, 22100, 42001,
+         2010, 3100, 23002, 43001, 3010, 13010, 12001, 2102, 23001, 2110, 3110, 3012, 2101, 3011),
     ),
     (
         (30002, 40002, 10002),
         (21002, 31002, 41002),
-        (12002,),
+        (1, 102, 3, 10001, 30001, 40003, 10003),
         (),
-        (1, 102, 3, 30001, 40003, 10001, 23002, 1012, 1001, 1003, 21001, 2102, 31001, 41003, 10003, 3012, 0, 2003,
-         20000, 101, 30000, 42003, 10000, 1011, 1000, 3003, 21000, 103, 31000, 43003, 11000, 10, 2000, 22000, 100,
-         32000, 42002, 12000, 1010, 20100, 3000, 1100, 33000, 43002, 11010, 2010, 23000, 2001, 2100, 32001, 13000, 110,
-         22100, 3001, 1110, 33001, 3010, 13010, 21003, 3100, 32002, 12003, 2110, 23003, 3110, 33002, 12001, 1013,
-         23001, 2103, 3013, 2101, 3011),
+        (23002, 1012, 1001, 1003, 31001, 41003, 21001, 101, 0, 2003, 10000, 30000, 42003, 20000, 3012, 103, 1000, 3003,
+         11000, 31000, 43003, 21000, 1011, 100, 42002, 2000, 12000, 32000, 20100, 10, 12003, 1100, 43002, 3000, 33000,
+         22000, 1010, 13000, 2100, 2001, 32001, 23000, 110, 11010, 2103, 3001, 33001, 22100, 2010, 12001, 3100, 32002,
+         21003, 3010, 13010, 1110, 33002, 23003, 2110, 12002, 2101, 23001, 1013, 3110, 3013, 2102, 3011),
     ),
     (
         (40003, 10003),
         (21003, 41003),
-        (12003, 42003),
+        (2, 103, 10002, 42003, 12003),
         (),
-        (2, 103, 10002, 23003, 1013, 1002, 21002, 2103, 43003, 3013, 1, 10001, 102, 1012, 1001, 21001, 101, 0, 10000,
-         20000, 1011, 1000, 21000, 11000, 100, 10, 20100, 2000, 12000, 1100, 1010, 22000, 11010, 3000, 2100, 110,
-         13000, 23000, 2001, 1110, 2010, 22100, 12001, 3001, 3100, 3010, 13010, 23001, 2002, 2110, 2101, 12002, 3002,
-         23002, 3110, 3011, 3012, 2102),
+        (23003, 43003, 1013, 1002, 21002, 102, 1, 10001, 3013, 2103, 1001, 21001, 1012, 101, 0, 10000, 20000, 1011,
+         1000, 21000, 11000, 100, 10, 20100, 2000, 12000, 22000, 1100, 1010, 11010, 3000, 13000, 23000, 2100, 110,
+         2001, 22100, 12001, 1110, 2010, 3001, 23001, 3100, 3010, 13010, 2002, 12002, 2110, 2101, 3002, 23002, 3110,
+         3011, 3012, 2102),
     ),
 )
 VMEM_LIMIT = 67043328
@@ -89,7 +86,7 @@
     return z * cdf, slope
 
 
-def grads_kernel(dims, w1_hbm, w2_hbm, x_ref, y_ref, *rest):
+def grads_kernel(dims, w1_hbm, w2_hbm, x_hbm, y_hbm, *rest):
     n_dev, layers, rows, d, hid = dims
     chips = n_dev // 2
     hc = hid // 2
@@ -97,7 +94,7 @@
     chips_z = chips // 4
     n_out = 4 * chips_z + 4 * FIRST
     outs, rest = rest[:n_out], rest[n_out:]
-    (wb1, wb2, own2, far2, cw1, cw2, z_all, hb, eb, hcur, rh, re, ow1, ow2, acc1, acc2, own,
+    (x_ref, y_ref, xy_sem, wb1, wb2, own2, far2, cw1, cw2, z_all, hb, eb, hcur, rh, re, ow1, ow2, acc1, acc2, own,
      w1_sem, w2_sem, x_send, x_recv, free_sem, hs_sem, hr_sem, es_sem, er_sem, px_send, px_recv,
      sp_send, sp_recv, tw_send, tw_recv, own_sem) = rest
 
@@ -141,8 +138,12 @@
     def chunk(m):
         return (core + m) % 2
 
+    takes = [pltpu.make_async_copy(src, dst, xy_sem.at[i]) for i, (src, dst) in enumerate(((x_hbm, x_ref), (y_hbm, y_ref)))]
     for step in range(2):
         w2_copy(step, step).start()
+        if step == 0:
+            for copy in takes:
+                copy.start()
         for m in range(2):
             w1_copy(step, chunk(m), 2 * step + m).start()
     pl.semaphore_wait(barrier, chips)
@@ -190,6 +191,8 @@
         def _():
             re[core * chips + chip] = eb[l]
 
+    for copy in takes:
+        copy.wait()
     hcur[...] = x_ref[...].astype(F32)
 
     def ahead(step):
@@ -531,9 +534,12 @@
     return pl.pallas_call(
         functools.partial(grads_kernel, dims),
         out_shape=[jax.ShapeDtypeStruct((2, QUARTERS // 2, 2, part_rows, 128), BF16)] * n_out,
-        in_specs=[pl.BlockSpec(memory_space=pl.ANY)] * 2 + [pl.BlockSpec(memory_space=pltpu.VMEM)] * 2,
+        in_specs=[pl.BlockSpec(memory_space=pl.ANY)] * 4,
         out_specs=[pl.BlockSpec(memory_space=pl.ANY)] * n_out,
         scratch_shapes=[
+            pltpu.VMEM((rows, d), BF16),
+            pltpu.VMEM((rows, d), BF16),
+            pltpu.SemaphoreType.DMA((2,)),
             pltpu.VMEM((SLOTS, d, hc), F32),
             pltpu.VMEM((2, hc, d), F32),
             pltpu.VMEM((RING, hc, d), BF16),
@@ -579,17 +585,17 @@
     step_size = LR_SCALE / layers
     chunk = 2 * piece
     steps = 16
-    w1, m1, w2, m2, h_in = refs[:5]
+    w1, m1, w2, m2, h_hbm = refs[:5]
     sums = refs[5:13]
     refs = refs[13:]
     if group:
         refs = refs[4:]
     if last:
-        y_ref, refs = refs[0], refs[1:]
-    w1o, w2o, m1o, m2o, h_out = refs[:5]
+        y_hbm, refs = refs[0], refs[1:]
+    w1o, w2o, m1o, m2o, h_done = refs[:5]
     if last:
         loss_ref = refs[5]
-    bw1, bm1, bw2, bm2, gbuf, in_sem, out_sem, gsem, nb1, nb2, hb_ref = refs[-11:]
+    bw1, bm1, bw2, bm2, gbuf, in_sem, out_sem, gsem, nb1, nb2, hb_ref, y_ref, h_out, h_sem = refs[-14:]
     slots = bw1.shape[0]
 
     me = lax.axis_index("data")
@@ -624,9 +630,18 @@
                     def _(par=par, inner=inner, is_far=is_far, twin=twin):
                         pltpu.make_async_copy(sums[4 * is_far + 2 * par + twin].at[inner, q], gbuf.at[slot, par], gsem.at[par, slot]).start()
 
-    for t in range(AHEAD):
+    takes = [pltpu.make_async_copy(h_hbm, h_out if group else hb_ref, h_sem.at[0])]
+    if last:
+        takes.append(pltpu.make_async_copy(y_hbm, y_ref, h_sem.at[1]))
+    fetch(0, 0)
+    for copy in takes:
+        copy.start()
+    for t in range(1, AHEAD):
         fetch(t, t)
-    h_out[...] = h_in[...].astype(F32)
+    for copy in takes:
+        copy.wait()
+    if not group:
+        h_out[...] = hb_ref[...].astype(F32)
 
     def body(t, carry):
         slot = t % slots
@@ -637,6 +652,7 @@
 
         for copy in reads(t, slot):
             copy.wait()
+        done = writes(t, slot)
         for par in range(2):
             pltpu.make_async_copy(sums[0].at[0, 0], gbuf.at[slot, par], gsem.at[par, slot]).wait()
             for cb in range(piece // 128):
@@ -646,6 +662,9 @@
                 bm1[slot, :, cols] = mn
                 bw1[slot, :, cols] = wn
                 nb1[:, cols] = wn.astype(BF16)
+        for copy in done[:2]:
+            copy.start()
+        for par in range(2):
             hid_rows = slice(par * piece, (par + 1) * piece)
             for lb in range(d // 128):
                 cols = slice(lb * 128, (lb + 1) * 128)
@@ -654,7 +673,7 @@
                 bm2[slot, hid_rows, cols] = mn
                 bw2[slot, hid_rows, cols] = wn
                 nb2[hid_rows, cols] = wn.astype(BF16)
-        for copy in writes(t, slot):
+        for copy in done[2:]:
             copy.start()
 
         @pl.when(t + AHEAD < steps)
@@ -673,12 +692,15 @@
         return carry
 
     lax.fori_loop(0, steps, body, 0)
+    give = pltpu.make_async_copy(h_out, h_done, h_sem.at[0])
+    give.start()
+    if last:
+        diff = h_out[...] - y_ref[...].astype(F32)
+        loss_ref[...] = jnp.sum(diff * diff, axis=-1) / (2 * d)
     for t in range(steps - slots, steps):
         for copy in writes(t, t % slots):
             copy.wait()
-    if last:
-        diff = h_out[...] - y_ref[...].astype(F32)
-        loss_ref[...] = jnp.sum(diff * diff, axis=-1) / (2 * d)
+    give.wait()
 
 
 def update(group, w_in, m_in, w_out, m_out, h, sums, prev, y):
@@ -690,8 +712,8 @@
     whole = pl.BlockSpec(memory_space=pltpu.VMEM)
     any_spec = pl.BlockSpec(memory_space=pl.ANY)
     args = [w_in, m_in, w_out, m_out, h, *sums, *prev] + ([y] if last else [])
-    in_specs = [any_spec] * 4 + [whole] + [any_spec] * (8 + len(prev)) + ([whole] if last else [])
-    out_specs = [any_spec] * 4 + [whole]
+    in_specs = [any_spec] * len(args)
+    out_specs = [any_spec] * 5
     out_shape = [jax.ShapeDtypeStruct(a.shape, F32) for a in (w_in, w_out, m_in, m_out, h)]
     if last:
         out_specs.append(whole)
@@ -715,6 +737,9 @@
             pltpu.VMEM((d, chunk), BF16),
             pltpu.VMEM((chunk, d), BF16),
             pltpu.VMEM((rows, d), BF16),
+            pltpu.VMEM((rows, d), BF16),
+            pltpu.VMEM((rows, d), F32),
+            pltpu.SemaphoreType.DMA((2,)),
         ],
         input_output_aliases={13 + i: i for i in range(len(prev))},
         compiler_params=pltpu.CompilerParams(vmem_limit_bytes=VMEM_LIMIT),

time: 547 us -> 547 us (level)
    pallas_call x1, Pallas kernels: 242 us -> 235 us  [local_grads(): pl.pallas_call(functools.partial(grads_kernel, dims), out_shape=[jax.Shap...]
  transfers between devices with their start and end apart: 12 -> 12, of which waited for: 2 -> 2; matrix products, arithmetic and copies ran while one was open for 0% -> 0% of each run, Pallas kernels for 28% -> 29%
where the time goes in v7:
time: 547 us; the launch traced here: 537 us
  Pallas kernels  440 us (80%)
  waiting for transfers between devices  87.6 us (16%)
  starting transfers between devices  8.71 us (2%)
    pallas_call x1, Pallas kernels, local_grads(): pl.pallas_call(functools.partial(grads_kernel, dims), out_shape=[jax.Shap...  235 us
    pallas_call x4, Pallas kernels, update(): pl.pallas_call(functools.partial(update_kernel, (layers, rows, d, piece),...  205 us
    ppermute x12, waiting for transfers between devices, send(): return lax.ppermute(array, 'data', swap[axis])  87.6 us
  transfers between devices with their start and end apart: 12, of which 2 were waited for; matrix products, arithmetic and copies ran while one was open for 0% of the time, Pallas kernels for 29%

profile of v7, /device:TPU:0, one launch (start us, length us, event | category | flops | bytes accessed | tf_op | source)
XLA Modules:
  0.0 537.2 jit_solution(13818596181083158564)
XLA Ops:
  0.6 235.2 %local_grads.1 = (bf16[2,2,2,1024,128]{4,3,2,1,0:T(8,128)(2,1)}, bf16[2,2,2,1024,128]{4,3,2,1,0:T(8,128)(2,1)}, bf16[2,2,2,1024,128]{4,3,2,1,0:T(8,128)(2,1)}, b...) custom-call(f32[16,512,2048]{2,1,0:T(8,128)} %refs_0_.7, ...), custom_call_target="tpu_custom_call" | custom-call | flops 17179869184 | bytes 268435456 | tf_op jit(solution)/shard_map/local_grads/pallas_call | solution.py:534
  235.9 3.2 collective-permute-start
  239.1 0.1 collective-permute-start.2
  239.1 0.1 collective-permute-start.4
  239.2 1.9 collective-permute-start.6
  241.2 0.1 collective-permute-start.10
  241.3 44.6 %collective-permute-done.refs_9_ = bf16[2,2,2,1024,128]{4,3,2,1,0:T(8,128)(2,1)} collective-permute-done((bf16[2,2,2,1024,128]{4,3,2,1,0:T(8,128)(2,1)}, bf16[2,2,2,1024,128]{4,3,2,1,0:T(8,128)(2,1)}, u32[]{:S(2)}, u32[]{:S(2)}) %collective-permute-start) | collective-permute-done | bytes 2097184 | tf_op jit(solution)/shard_map/ppermute | solution.py:756
  285.9 2.0 collective-permute-start.8
  287.9 0.0 collective-permute-done.2.refs_11_
  287.9 0.0 collective-permute-start.1
  287.9 42.9 %collective-permute-done.4.refs_9_ = bf16[2,2,2,1024,128]{4,3,2,1,0:T(8,128)(2,1)} collective-permute-done((bf16[2,2,2,1024,128]{4,3,2,1,0:T(8,128)(2,1)}, bf16[2,2,2,1024,128]{4,3,2,1,0:T(8,128)(2,1)}, u32[]{:S(2)}, u32[]{:S(2)}) %collective-permute-start.4) | collective-permute-done | bytes 2097184 | tf_op jit(solution)/shard_map/ppermute | solution.py:756
  330.8 0.0 collective-permute-start.3
  330.8 50.8 %shard_map.127 = (f32[16,512,2048]{2,1,0:T(8,128)}, f32[16,2048,512]{2,1,0:T(8,128)}, f32[16,512,2048]{2,1,0:T(8,128)}, f32[16,2048,512]{2,1,0:T(8,128)}, f32[64,512]{1,0:T(8,128)}) custom-call(f32[16,512,2048]{2,1,0:T(8,128)} %refs_0_.7, f32[16,512,2048]{2,1,0:T(8,128)} %refs_1_.7, f32[16,2048,512]{2,1,0:T(8,128)} %refs_2_.7, f32[16,2048,512]{2,1,0:T(8,128)} %refs_3_.7, ...), custom_call_target="tpu_custom_call" | custom-call | flops 49999998976 | bytes 150994944 | tf_op jit(solution)/shard_map/pallas_call | solution.py:723
  381.7 0.0 collective-permute-done.6.refs_11_
  381.7 0.7 collective-permute-start.5
  382.4 0.0 collective-permute-done.10.refs_11_
  382.4 0.1 collective-permute-start.7
  382.5 0.0 collective-permute-done.8.refs_9_
  382.5 0.4 collective-permute-start.11
  382.9 0.0 collective-permute-done.1.refs_10_
  382.9 0.1 collective-permute-start.9
  383.0 0.0 collective-permute-done.3.refs_12_
  383.0 51.2 %shard_map.128 = (f32[16,512,2048]{2,1,0:T(8,128)}, f32[16,2048,512]{2,1,0:T(8,128)}, f32[16,512,2048]{2,1,0:T(8,128)}, f32[16,2048,512]{2,1,0:T(8,128)}, f32[64,512]{1,0:T(8,128)}) custom-call(f32[16,512,2048]{2,1,0:T(8,128)} %refs_0_.7, f32[16,512,2048]{2,1,0:T(8,128)} %refs_1_.7, ...), custom_call_target="tpu_custom_call", output_to_operand_aliasing={{0}: (13, {}), {1}: (14, {}), {2}: (15, {}), {3}: (16, {})} | custom-call | flops 49999998976 | bytes 150994944 | tf_op jit(solution)/shard_map/pallas_call | solution.py:723
  434.2 0.0 collective-permute-done.5.refs_10_
  434.2 0.0 collective-permute-done.7.refs_12_
  434.2 51.2 %shard_map.129 = (f32[16,512,2048]{2,1,0:T(8,128)}, f32[16,2048,512]{2,1,0:T(8,128)}, f32[16,512,2048]{2,1,0:T(8,128)}, f32[16,2048,512]{2,1,0:T(8,128)}, f32[64,512]{1,0:T(8,128)}) custom-call(f32[16,512,2048]{2,1,0:T(8,128)} %refs_0_.7, f32[16,512,2048]{2,1,0:T(8,128)} %refs_1_.7, ...), custom_call_target="tpu_custom_call", output_to_operand_aliasing={{0}: (13, {}), {1}: (14, {}), {2}: (15, {}), {3}: (16, {})} | custom-call | flops 49999998976 | bytes 150994944 | tf_op jit(solution)/shard_map/pallas_call | solution.py:723
  485.4 0.0 collective-permute-done.11.refs_12_
  485.5 0.0 collective-permute-done.9.refs_10_
  485.5 51.6 %shard_map.130 = (f32[16,512,2048]{2,1,0:T(8,128)}, f32[16,2048,512]{2,1,0:T(8,128)}, f32[16,512,2048]{2,1,0:T(8,128)}, f32[16,2048,512]{2,1,0:T(8,128)}, f32[64,512]{1,0:T(8,128)}, /*index=5*/f32[64]{0:T(128)}) custom-call(f32[16,512,2048]{2,1,0:T(8,128)} %refs_0_.7, ...), custom_call_target="tpu_custom_call", output_to_operand_aliasing={{0}: (13, {}), {1}: (14, {}), {2}: (15, {}), {3}: (16, {})} | custom-call | flops 49999998976 | bytes 150994944 | tf_op jit(solution)/shard_map/pallas_call | solution.py:723
Async XLA Ops:
  235.9 50.0 %collective-permute-start = (bf16[2,2,2,1024,128]{4,3,2,1,0:T(8,128)(2,1)}, bf16[2,2,2,1024,128]{4,3,2,1,0:T(8,128)(2,1)}, u32[]{:S(2)}, u32[]{:S(2)}) collective-permute-start(bf16[2,2,2,1024,128]{4,3,2,1,0:T(8,128)(2,1)} %get-tuple-element.56.refs_5_), channel_id=1, source_target_pairs={{0,4},{1,5},{2,6},{3,7},{4,0},{5,1},{6,2},{7,3},{8,12},{9,13},{10,... | collective-permute-start | bytes 6291464 | tf_op jit(solution)/shard_map/ppermute | solution.py:756
  239.1 48.8 %collective-permute-start.2 = (bf16[2,2,2,1024,128]{4,3,2,1,0:T(8,128)(2,1)}, bf16[2,2,2,1024,128]{4,3,2,1,0:T(8,128)(2,1)}, u32[]{:S(2)}, u32[]{:S(2)}) collective-permute-start(bf16[2,2,2,1024,128]{4,3,2,1,0:T(8,128)(2,1)} %get-tuple-element.58.refs_7_), channel_id=1, source_target_pairs={{0,2},{1,3},{2,0},{3,1},{4,6},{5,7},{6,4},{7,5},{8,10},{9,11},{10,... | collective-permute-start | bytes 6291464 | tf_op jit(solution)/shard_map/ppermute | solution.py:756
  239.1 91.7 %collective-permute-start.4 = (bf16[2,2,2,1024,128]{4,3,2,1,0:T(8,128)(2,1)}, bf16[2,2,2,1024,128]{4,3,2,1,0:T(8,128)(2,1)}, u32[]{:S(2)}, u32[]{:S(2)}) collective-permute-start(bf16[2,2,2,1024,128]{4,3,2,1,0:T(8,128)(2,1)} %get-tuple-element.65.refs_5_), channel_id=1, source_target_pairs={{0,4},{1,5},{2,6},{3,7},{4,0},{5,1},{6,2},{7,3},{8,12},{9,13},{10,... | collective-permute-start | bytes 6291464 | tf_op jit(solution)/shard_map/ppermute | solution.py:756
  239.2 142.4 %collective-permute-start.6 = (bf16[2,2,2,1024,128]{4,3,2,1,0:T(8,128)(2,1)}, bf16[2,2,2,1024,128]{4,3,2,1,0:T(8,128)(2,1)}, u32[]{:S(2)}, u32[]{:S(2)}) collective-permute-start(bf16[2,2,2,1024,128]{4,3,2,1,0:T(8,128)(2,1)} %get-tuple-element.67.refs_7_), channel_id=1, source_target_pairs={{0,2},{1,3},{2,0},{3,1},{4,6},{5,7},{6,4},{7,5},{8,10},{9,11},{10,... | collective-permute-start | bytes 6291464 | tf_op jit(solution)/shard_map/ppermute | solution.py:756
  241.2 141.2 %collective-permute-start.10 = (bf16[2,2,2,1024,128]{4,3,2,1,0:T(8,128)(2,1)}, bf16[2,2,2,1024,128]{4,3,2,1,0:T(8,128)(2,1)}, u32[]{:S(2)}, u32[]{:S(2)}) collective-permute-start(bf16[2,2,2,1024,128]{4,3,2,1,0:T(8,128)(2,1)} %get-tuple-element.76.refs_7_), channel_id=1, source_target_pairs={{0,2},{1,3},{2,0},{3,1},{4,6},{5,7},{6,4},{7,5},{8,10},{9,11},{10,... | collective-permute-start | bytes 6291464 | tf_op jit(solution)/shard_map/ppermute | solution.py:756
  285.9 96.6 %collective-permute-start.8 = (bf16[2,2,2,1024,128]{4,3,2,1,0:T(8,128)(2,1)}, bf16[2,2,2,1024,128]{4,3,2,1,0:T(8,128)(2,1)}, u32[]{:S(2)}, u32[]{:S(2)}) collective-permute-start(bf16[2,2,2,1024,128]{4,3,2,1,0:T(8,128)(2,1)} %get-tuple-element.74.refs_5_), channel_id=1, source_target_pairs={{0,4},{1,5},{2,6},{3,7},{4,0},{5,1},{6,2},{7,3},{8,12},{9,13},{10,... | collective-permute-start | bytes 6291464 | tf_op jit(solution)/shard_map/ppermute | solution.py:756
  287.9 95.0 %collective-permute-start.1 = (bf16[2,2,2,1024,128]{4,3,2,1,0:T(8,128)(2,1)}, bf16[2,2,2,1024,128]{4,3,2,1,0:T(8,128)(2,1)}, u32[]{:S(2)}, u32[]{:S(2)}) collective-permute-start(bf16[2,2,2,1024,128]{4,3,2,1,0:T(8,128)(2,1)} %collective-permute-done.refs_9_), channel_id=1, source_target_pairs={{0,1},{1,0},{2,3},{3,2},{4,5},{5,4},{6,7},{7,6},{8,9},{9,8},{10,11... | collective-permute-start | bytes 6291464 | tf_op jit(solution)/shard_map/ppermute | solution.py:756
  330.8 52.2 %collective-permute-start.3 = (bf16[2,2,2,1024,128]{4,3,2,1,0:T(8,128)(2,1)}, bf16[2,2,2,1024,128]{4,3,2,1,0:T(8,128)(2,1)}, u32[]{:S(2)}, u32[]{:S(2)}) collective-permute-start(bf16[2,2,2,1024,128]{4,3,2,1,0:T(8,128)(2,1)} %collective-permute-done.2.refs_11_), channel_id=1, source_target_pairs={{0,1},{1,0},{2,3},{3,2},{4,5},{5,4},{6,7},{7,6},{8,9},{9,8},{10,11... | collective-permute-start | bytes 6291464 | tf_op jit(solution)/shard_map/ppermute | solution.py:756
  381.7 52.5 %collective-permute-start.5 = (bf16[2,2,2,1024,128]{4,3,2,1,0:T(8,128)(2,1)}, bf16[2,2,2,1024,128]{4,3,2,1,0:T(8,128)(2,1)}, u32[]{:S(2)}, u32[]{:S(2)}) collective-permute-start(bf16[2,2,2,1024,128]{4,3,2,1,0:T(8,128)(2,1)} %collective-permute-done.4.refs_9_), channel_id=1, source_target_pairs={{0,1},{1,0},{2,3},{3,2},{4,5},{5,4},{6,7},{7,6},{8,9},{9,8},{10,11... | collective-permute-start | bytes 6291464 | tf_op jit(solution)/shard_map/ppermute | solution.py:756
  382.4 51.8 %collective-permute-start.7 = (bf16[2,2,2,1024,128]{4,3,2,1,0:T(8,128)(2,1)}, bf16[2,2,2,1024,128]{4,3,2,1,0:T(8,128)(2,1)}, u32[]{:S(2)}, u32[]{:S(2)}) collective-permute-start(bf16[2,2,2,1024,128]{4,3,2,1,0:T(8,128)(2,1)} %collective-permute-done.6.refs_11_), channel_id=1, source_target_pairs={{0,1},{1,0},{2,3},{3,2},{4,5},{5,4},{6,7},{7,6},{8,9},{9,8},{10,11... | collective-permute-start | bytes 6291464 | tf_op jit(solution)/shard_map/ppermute | solution.py:756
  382.5 103.0 %collective-permute-start.11 = (bf16[2,2,2,1024,128]{4,3,2,1,0:T(8,128)(2,1)}, bf16[2,2,2,1024,128]{4,3,2,1,0:T(8,128)(2,1)}, u32[]{:S(2)}, u32[]{:S(2)}) collective-permute-start(bf16[2,2,2,1024,128]{4,3,2,1,0:T(8,128)(2,1)} %collective-permute-done.10.refs_11_), channel_id=1, source_target_pairs={{0,1},{1,0},{2,3},{3,2},{4,5},{5,4},{6,7},{7,6},{8,9},{9,8},{10,11... | collective-permute-start | bytes 6291464 | tf_op jit(solution)/shard_map/ppermute | solution.py:756
  382.9 102.6 %collective-permute-start.9 = (bf16[2,2,2,1024,128]{4,3,2,1,0:T(8,128)(2,1)}, bf16[2,2,2,1024,128]{4,3,2,1,0:T(8,128)(2,1)}, u32[]{:S(2)}, u32[]{:S(2)}) collective-permute-start(bf16[2,2,2,1024,128]{4,3,2,1,0:T(8,128)(2,1)} %collective-permute-done.8.refs_9_), channel_id=1, source_target_pairs={{0,1},{1,0},{2,3},{3,2},{4,5},{5,4},{6,7},{7,6},{8,9},{9,8},{10,11... | collective-permute-start | bytes 6291464 | tf_op jit(solution)/shard_map/ppermute | solution.py:756

commit v8 on v7

--- a/solution.py
+++ b/solution.py
@@ -585,17 +585,17 @@
     step_size = LR_SCALE / layers
     chunk = 2 * piece
     steps = 16
-    w1, m1, w2, m2, h_hbm = refs[:5]
+    w1, m1, w2, m2, h_in = refs[:5]
     sums = refs[5:13]
     refs = refs[13:]
     if group:
         refs = refs[4:]
     if last:
-        y_hbm, refs = refs[0], refs[1:]
-    w1o, w2o, m1o, m2o, h_done = refs[:5]
+        y_ref, refs = refs[0], refs[1:]
+    w1o, w2o, m1o, m2o, h_out = refs[:5]
     if last:
         loss_ref = refs[5]
-    bw1, bm1, bw2, bm2, gbuf, in_sem, out_sem, gsem, nb1, nb2, hb_ref, y_ref, h_out, h_sem = refs[-14:]
+    bw1, bm1, bw2, bm2, gbuf, in_sem, out_sem, gsem, nb1, nb2, hb_ref = refs[-11:]
     slots = bw1.shape[0]
 
     me = lax.axis_index("data")
@@ -630,18 +630,9 @@
                     def _(par=par, inner=inner, is_far=is_far, twin=twin):
                         pltpu.make_async_copy(sums[4 * is_far + 2 * par + twin].at[inner, q], gbuf.at[slot, par], gsem.at[par, slot]).start()
 
-    takes = [pltpu.make_async_copy(h_hbm, h_out if group else hb_ref, h_sem.at[0])]
-    if last:
-        takes.append(pltpu.make_async_copy(y_hbm, y_ref, h_sem.at[1]))
-    fetch(0, 0)
-    for copy in takes:
-        copy.start()
-    for t in range(1, AHEAD):
+    for t in range(AHEAD):
         fetch(t, t)
-    for copy in takes:
-        copy.wait()
-    if not group:
-        h_out[...] = hb_ref[...].astype(F32)
+    h_out[...] = h_in[...].astype(F32)
 
     def body(t, carry):
         slot = t % slots
@@ -652,7 +643,6 @@
 
         for copy in reads(t, slot):
             copy.wait()
-        done = writes(t, slot)
         for par in range(2):
             pltpu.make_async_copy(sums[0].at[0, 0], gbuf.at[slot, par], gsem.at[par, slot]).wait()
             for cb in range(piece // 128):
@@ -662,9 +652,6 @@
                 bm1[slot, :, cols] = mn
                 bw1[slot, :, cols] = wn
                 nb1[:, cols] = wn.astype(BF16)
-        for copy in done[:2]:
-            copy.start()
-        for par in range(2):
             hid_rows = slice(par * piece, (par + 1) * piece)
             for lb in range(d // 128):
                 cols = slice(lb * 128, (lb + 1) * 128)
@@ -673,7 +660,7 @@
                 bm2[slot, hid_rows, cols] = mn
                 bw2[slot, hid_rows, cols] = wn
                 nb2[hid_rows, cols] = wn.astype(BF16)
-        for copy in done[2:]:
+        for copy in writes(t, slot):
             copy.start()
 
         @pl.when(t + AHEAD < steps)
@@ -692,15 +679,12 @@
         return carry
 
     lax.fori_loop(0, steps, body, 0)
-    give = pltpu.make_async_copy(h_out, h_done, h_sem.at[0])
-    give.start()
+    for t in range(steps - slots, steps):
+        for copy in writes(t, t % slots):
+            copy.wait()
     if last:
         diff = h_out[...] - y_ref[...].astype(F32)
         loss_ref[...] = jnp.sum(diff * diff, axis=-1) / (2 * d)
-    for t in range(steps - slots, steps):
-        for copy in writes(t, t % slots):
-            copy.wait()
-    give.wait()
 
 
 def update(group, w_in, m_in, w_out, m_out, h, sums, prev, y):
@@ -712,8 +696,8 @@
     whole = pl.BlockSpec(memory_space=pltpu.VMEM)
     any_spec = pl.BlockSpec(memory_space=pl.ANY)
     args = [w_in, m_in, w_out, m_out, h, *sums, *prev] + ([y] if last else [])
-    in_specs = [any_spec] * len(args)
-    out_specs = [any_spec] * 5
+    in_specs = [any_spec] * 4 + [whole] + [any_spec] * (8 + len(prev)) + ([whole] if last else [])
+    out_specs = [any_spec] * 4 + [whole]
     out_shape = [jax.ShapeDtypeStruct(a.shape, F32) for a in (w_in, w_out, m_in, m_out, h)]
     if last:
         out_specs.append(whole)
@@ -737,9 +721,6 @@
             pltpu.VMEM((d, chunk), BF16),
             pltpu.VMEM((chunk, d), BF16),
             pltpu.VMEM((rows, d), BF16),
-            pltpu.VMEM((rows, d), BF16),
-            pltpu.VMEM((rows, d), F32),
-            pltpu.SemaphoreType.DMA((2,)),
         ],
         input_output_aliases={13 + i: i for i in range(len(prev))},
         compiler_params=pltpu.CompilerParams(vmem_limit_bytes=VMEM_LIMIT),

time: 547 us -> 544 us (level)
  the two profiles are of different devices: /device:TPU:0 before, /device:TPU:21 now
where the time goes in v8:
time: 544 us
  Pallas kernels  448 us (82%)
  waiting for transfers between devices  87.7 us (16%)
  starting transfers between devices  7.34 us (1%)
    pallas_call x1, Pallas kernels, local_grads(): pl.pallas_call(functools.partial(grads_kernel, dims), out_shape=[jax.Shap...  245 us
    pallas_call x4, Pallas kernels, update(): pl.pallas_call(functools.partial(update_kernel, (layers, rows, d, piece),...  202 us
    ppermute x12, waiting for transfers between devices, send(): return lax.ppermute(array, 'data', swap[axis])  87.7 us
  transfers between devices with their start and end apart: 12, of which 2 were waited for; matrix products, arithmetic and copies ran while one was open for 0% of the time, Pallas kernels for 28%

profile of v8, /device:TPU:21, one launch (start us, length us, event | category | flops | bytes accessed | tf_op | source)
XLA Modules:
  0.0 543.5 jit_solution(12935737555411939808)
XLA Ops:
  0.6 245.4 %local_grads.1 = (bf16[2,2,2,1024,128]{4,3,2,1,0:T(8,128)(2,1)}, bf16[2,2,2,1024,128]{4,3,2,1,0:T(8,128)(2,1)}, bf16[2,2,2,1024,128]{4,3,2,1,0:T(8,128)(2,1)}, b...) custom-call(f32[16,512,2048]{2,1,0:T(8,128)} %refs_0_.7, ...), custom_call_target="tpu_custom_call" | custom-call | flops 17179869184 | bytes 268435456 | tf_op jit(solution)/shard_map/local_grads/pallas_call | solution.py:534
  246.0 0.1 collective-permute-start
  246.1 0.1 collective-permute-start.2
  246.2 1.4 collective-permute-start.4
  247.6 1.5 collective-permute-start.6
  249.0 0.0 collective-permute-start.10
  249.1 44.4 %collective-permute-done.refs_9_ = bf16[2,2,2,1024,128]{4,3,2,1,0:T(8,128)(2,1)} collective-permute-done((bf16[2,2,2,1024,128]{4,3,2,1,0:T(8,128)(2,1)}, bf16[2,2,2,1024,128]{4,3,2,1,0:T(8,128)(2,1)}, u32[]{:S(2)}, u32[]{:S(2)}) %collective-permute-start) | collective-permute-done | bytes 2097184 | tf_op jit(solution)/shard_map/ppermute | solution.py:737
  293.5 0.3 collective-permute-start.8
  293.8 0.0 collective-permute-done.2.refs_11_
  293.8 1.4 collective-permute-start.1
  295.1 43.3 %collective-permute-done.4.refs_9_ = bf16[2,2,2,1024,128]{4,3,2,1,0:T(8,128)(2,1)} collective-permute-done((bf16[2,2,2,1024,128]{4,3,2,1,0:T(8,128)(2,1)}, bf16[2,2,2,1024,128]{4,3,2,1,0:T(8,128)(2,1)}, u32[]{:S(2)}, u32[]{:S(2)}) %collective-permute-start.4) | collective-permute-done | bytes 2097184 | tf_op jit(solution)/shard_map/ppermute | solution.py:737
  338.4 1.6 collective-permute-start.3
  340.0 51.7 %shard_map.127 = (f32[16,512,2048]{2,1,0:T(8,128)}, f32[16,2048,512]{2,1,0:T(8,128)}, f32[16,512,2048]{2,1,0:T(8,128)}, f32[16,2048,512]{2,1,0:T(8,128)}, f32[64,512]{1,0:T(8,128)}) custom-call(f32[16,512,2048]{2,1,0:T(8,128)} %refs_0_.7, f32[16,512,2048]{2,1,0:T(8,128)} %refs_1_.7, f32[16,2048,512]{2,1,0:T(8,128)} %refs_2_.7, f32[16,2048,512]{2,1,0:T(8,128)} %refs_3_.7, ...), custom_call_target="tpu_custom_call" | custom-call | flops 49999998976 | bytes 150994944 | tf_op jit(solution)/shard_map/pallas_call | solution.py:707
  391.8 0.0 collective-permute-done.6.refs_11_
  391.8 0.1 collective-permute-start.5
  391.9 0.0 collective-permute-done.10.refs_11_
  391.9 0.5 collective-permute-start.7
  392.4 0.0 collective-permute-done.8.refs_9_
  392.4 0.1 collective-permute-start.11
  392.4 0.0 collective-permute-done.1.refs_10_
  392.4 0.4 collective-permute-start.9
  392.9 0.0 collective-permute-done.3.refs_12_
  392.9 50.1 %shard_map.128 = (f32[16,512,2048]{2,1,0:T(8,128)}, f32[16,2048,512]{2,1,0:T(8,128)}, f32[16,512,2048]{2,1,0:T(8,128)}, f32[16,2048,512]{2,1,0:T(8,128)}, f32[64,512]{1,0:T(8,128)}) custom-call(f32[16,512,2048]{2,1,0:T(8,128)} %refs_0_.7, f32[16,512,2048]{2,1,0:T(8,128)} %refs_1_.7, ...), custom_call_target="tpu_custom_call", output_to_operand_aliasing={{0}: (13, {}), {1}: (14, {}), {2}: (15, {}), {3}: (16, {})} | custom-call | flops 49999998976 | bytes 150994944 | tf_op jit(solution)/shard_map/pallas_call | solution.py:707
  443.0 0.0 collective-permute-done.5.refs_10_
  443.0 0.0 collective-permute-done.7.refs_12_
  443.0 50.1 %shard_map.129 = (f32[16,512,2048]{2,1,0:T(8,128)}, f32[16,2048,512]{2,1,0:T(8,128)}, f32[16,512,2048]{2,1,0:T(8,128)}, f32[16,2048,512]{2,1,0:T(8,128)}, f32[64,512]{1,0:T(8,128)}) custom-call(f32[16,512,2048]{2,1,0:T(8,128)} %refs_0_.7, f32[16,512,2048]{2,1,0:T(8,128)} %refs_1_.7, ...), custom_call_target="tpu_custom_call", output_to_operand_aliasing={{0}: (13, {}), {1}: (14, {}), {2}: (15, {}), {3}: (16, {})} | custom-call | flops 49999998976 | bytes 150994944 | tf_op jit(solution)/shard_map/pallas_call | solution.py:707
  493.1 0.0 collective-permute-done.11.refs_12_
  493.1 0.0 collective-permute-done.9.refs_10_
  493.2 50.2 %shard_map.130 = (f32[16,512,2048]{2,1,0:T(8,128)}, f32[16,2048,512]{2,1,0:T(8,128)}, f32[16,512,2048]{2,1,0:T(8,128)}, f32[16,2048,512]{2,1,0:T(8,128)}, f32[64,512]{1,0:T(8,128)}, /*index=5*/f32[64]{0:T(128)}) custom-call(f32[16,512,2048]{2,1,0:T(8,128)} %refs_0_.7, ...), custom_call_target="tpu_custom_call", output_to_operand_aliasing={{0}: (13, {}), {1}: (14, {}), {2}: (15, {}), {3}: (16, {})} | custom-call | flops 49999998976 | bytes 150994944 | tf_op jit(solution)/shard_map/pallas_call | solution.py:707
Async XLA Ops:
  246.0 47.4 %collective-permute-start = (bf16[2,2,2,1024,128]{4,3,2,1,0:T(8,128)(2,1)}, bf16[2,2,2,1024,128]{4,3,2,1,0:T(8,128)(2,1)}, u32[]{:S(2)}, u32[]{:S(2)}) collective-permute-start(bf16[2,2,2,1024,128]{4,3,2,1,0:T(8,128)(2,1)} %get-tuple-element.56.refs_5_), channel_id=1, source_target_pairs={{0,4},{1,5},{2,6},{3,7},{4,0},{5,1},{6,2},{7,3},{8,12},{9,13},{10,... | collective-permute-start | bytes 6291464 | tf_op jit(solution)/shard_map/ppermute | solution.py:737
  246.1 47.6 %collective-permute-start.2 = (bf16[2,2,2,1024,128]{4,3,2,1,0:T(8,128)(2,1)}, bf16[2,2,2,1024,128]{4,3,2,1,0:T(8,128)(2,1)}, u32[]{:S(2)}, u32[]{:S(2)}) collective-permute-start(bf16[2,2,2,1024,128]{4,3,2,1,0:T(8,128)(2,1)} %get-tuple-element.58.refs_7_), channel_id=1, source_target_pairs={{0,2},{1,3},{2,0},{3,1},{4,6},{5,7},{6,4},{7,5},{8,10},{9,11},{10,... | collective-permute-start | bytes 6291464 | tf_op jit(solution)/shard_map/ppermute | solution.py:737
  246.2 92.2 %collective-permute-start.4 = (bf16[2,2,2,1024,128]{4,3,2,1,0:T(8,128)(2,1)}, bf16[2,2,2,1024,128]{4,3,2,1,0:T(8,128)(2,1)}, u32[]{:S(2)}, u32[]{:S(2)}) collective-permute-start(bf16[2,2,2,1024,128]{4,3,2,1,0:T(8,128)(2,1)} %get-tuple-element.65.refs_5_), channel_id=1, source_target_pairs={{0,4},{1,5},{2,6},{3,7},{4,0},{5,1},{6,2},{7,3},{8,12},{9,13},{10,... | collective-permute-start | bytes 6291464 | tf_op jit(solution)/shard_map/ppermute | solution.py:737
  247.6 144.2 %collective-permute-start.6 = (bf16[2,2,2,1024,128]{4,3,2,1,0:T(8,128)(2,1)}, bf16[2,2,2,1024,128]{4,3,2,1,0:T(8,128)(2,1)}, u32[]{:S(2)}, u32[]{:S(2)}) collective-permute-start(bf16[2,2,2,1024,128]{4,3,2,1,0:T(8,128)(2,1)} %get-tuple-element.67.refs_7_), channel_id=1, source_target_pairs={{0,2},{1,3},{2,0},{3,1},{4,6},{5,7},{6,4},{7,5},{8,10},{9,11},{10,... | collective-permute-start | bytes 6291464 | tf_op jit(solution)/shard_map/ppermute | solution.py:737
  249.0 142.8 %collective-permute-start.10 = (bf16[2,2,2,1024,128]{4,3,2,1,0:T(8,128)(2,1)}, bf16[2,2,2,1024,128]{4,3,2,1,0:T(8,128)(2,1)}, u32[]{:S(2)}, u32[]{:S(2)}) collective-permute-start(bf16[2,2,2,1024,128]{4,3,2,1,0:T(8,128)(2,1)} %get-tuple-element.76.refs_7_), channel_id=1, source_target_pairs={{0,2},{1,3},{2,0},{3,1},{4,6},{5,7},{6,4},{7,5},{8,10},{9,11},{10,... | collective-permute-start | bytes 6291464 | tf_op jit(solution)/shard_map/ppermute | solution.py:737
  293.5 98.9 %collective-permute-start.8 = (bf16[2,2,2,1024,128]{4,3,2,1,0:T(8,128)(2,1)}, bf16[2,2,2,1024,128]{4,3,2,1,0:T(8,128)(2,1)}, u32[]{:S(2)}, u32[]{:S(2)}) collective-permute-start(bf16[2,2,2,1024,128]{4,3,2,1,0:T(8,128)(2,1)} %get-tuple-element.74.refs_5_), channel_id=1, source_target_pairs={{0,4},{1,5},{2,6},{3,7},{4,0},{5,1},{6,2},{7,3},{8,12},{9,13},{10,... | collective-permute-start | bytes 6291464 | tf_op jit(solution)/shard_map/ppermute | solution.py:737
  293.8 98.7 %collective-permute-start.1 = (bf16[2,2,2,1024,128]{4,3,2,1,0:T(8,128)(2,1)}, bf16[2,2,2,1024,128]{4,3,2,1,0:T(8,128)(2,1)}, u32[]{:S(2)}, u32[]{:S(2)}) collective-permute-start(bf16[2,2,2,1024,128]{4,3,2,1,0:T(8,128)(2,1)} %collective-permute-done.refs_9_), channel_id=1, source_target_pairs={{0,1},{1,0},{2,3},{3,2},{4,5},{5,4},{6,7},{7,6},{8,9},{9,8},{10,11... | collective-permute-start | bytes 6291464 | tf_op jit(solution)/shard_map/ppermute | solution.py:737
  338.4 54.5 %collective-permute-start.3 = (bf16[2,2,2,1024,128]{4,3,2,1,0:T(8,128)(2,1)}, bf16[2,2,2,1024,128]{4,3,2,1,0:T(8,128)(2,1)}, u32[]{:S(2)}, u32[]{:S(2)}) collective-permute-start(bf16[2,2,2,1024,128]{4,3,2,1,0:T(8,128)(2,1)} %collective-permute-done.2.refs_11_), channel_id=1, source_target_pairs={{0,1},{1,0},{2,3},{3,2},{4,5},{5,4},{6,7},{7,6},{8,9},{9,8},{10,11... | collective-permute-start | bytes 6291464 | tf_op jit(solution)/shard_map/ppermute | solution.py:737
  391.8 51.2 %collective-permute-start.5 = (bf16[2,2,2,1024,128]{4,3,2,1,0:T(8,128)(2,1)}, bf16[2,2,2,1024,128]{4,3,2,1,0:T(8,128)(2,1)}, u32[]{:S(2)}, u32[]{:S(2)}) collective-permute-start(bf16[2,2,2,1024,128]{4,3,2,1,0:T(8,128)(2,1)} %collective-permute-done.4.refs_9_), channel_id=1, source_target_pairs={{0,1},{1,0},{2,3},{3,2},{4,5},{5,4},{6,7},{7,6},{8,9},{9,8},{10,11... | collective-permute-start | bytes 6291464 | tf_op jit(solution)/shard_map/ppermute | solution.py:737
  391.9 51.1 %collective-permute-start.7 = (bf16[2,2,2,1024,128]{4,3,2,1,0:T(8,128)(2,1)}, bf16[2,2,2,1024,128]{4,3,2,1,0:T(8,128)(2,1)}, u32[]{:S(2)}, u32[]{:S(2)}) collective-permute-start(bf16[2,2,2,1024,128]{4,3,2,1,0:T(8,128)(2,1)} %collective-permute-done.6.refs_11_), channel_id=1, source_target_pairs={{0,1},{1,0},{2,3},{3,2},{4,5},{5,4},{6,7},{7,6},{8,9},{9,8},{10,11... | collective-permute-start | bytes 6291464 | tf_op jit(solution)/shard_map/ppermute | solution.py:737
  392.4 100.8 %collective-permute-start.11 = (bf16[2,2,2,1024,128]{4,3,2,1,0:T(8,128)(2,1)}, bf16[2,2,2,1024,128]{4,3,2,1,0:T(8,128)(2,1)}, u32[]{:S(2)}, u32[]{:S(2)}) collective-permute-start(bf16[2,2,2,1024,128]{4,3,2,1,0:T(8,128)(2,1)} %collective-permute-done.10.refs_11_), channel_id=1, source_target_pairs={{0,1},{1,0},{2,3},{3,2},{4,5},{5,4},{6,7},{7,6},{8,9},{9,8},{10,11... | collective-permute-start | bytes 6291464 | tf_op jit(solution)/shard_map/ppermute | solution.py:737
  392.4 100.7 %collective-permute-start.9 = (bf16[2,2,2,1024,128]{4,3,2,1,0:T(8,128)(2,1)}, bf16[2,2,2,1024,128]{4,3,2,1,0:T(8,128)(2,1)}, u32[]{:S(2)}, u32[]{:S(2)}) collective-permute-start(bf16[2,2,2,1024,128]{4,3,2,1,0:T(8,128)(2,1)} %collective-permute-done.8.refs_9_), channel_id=1, source_target_pairs={{0,1},{1,0},{2,3},{3,2},{4,5},{5,4},{6,7},{7,6},{8,9},{9,8},{10,11... | collective-permute-start | bytes 6291464 | tf_op jit(solution)/shard_map/ppermute | solution.py:737

commit v9 on v8

--- a/solution.py
+++ b/solution.py
@@ -19,7 +19,7 @@
 RING = 3
 QUARTERS = 4
 AHEAD = 4
-CACHED = 6
+CACHED = 7
 FIRST = 1
 RELAYS = (
     (
@@ -94,7 +94,7 @@
     chips_z = chips // 4
     n_out = 4 * chips_z + 4 * FIRST
     outs, rest = rest[:n_out], rest[n_out:]
-    (x_ref, y_ref, xy_sem, wb1, wb2, own2, far2, cw1, cw2, z_all, hb, eb, hcur, rh, re, ow1, ow2, acc1, acc2, own,
+    (x_ref, y_ref, xy_sem, wb1, wb2, own2, far2, cw1, cw2, z_kept, hb, eb, hcur, rh, re, ow1, ow2, acc1, acc2, own,
      w1_sem, w2_sem, x_send, x_recv, free_sem, hs_sem, hr_sem, es_sem, er_sem, px_send, px_recv,
      sp_send, sp_recv, tw_send, tw_recv, own_sem) = rest
 
@@ -228,14 +228,14 @@
                 pass_copy(step).wait_recv()
             w2 = own2 if m == 0 else far2
             z = mm(hb[step], wb1[slot].astype(BF16))
-            z_all[2 * step + j] = z
             hcur[...] += mm(gelu(z).astype(BF16), w2[step % RING])
             if m == 0:
                 pass_copy(step + 2).start()
 
             @pl.when(step >= layers - CACHED)
-            def _(m=m, j=j, slot=slot, w2=w2):
+            def _(m=m, j=j, slot=slot, w2=w2, z=z):
                 kept = 2 * (step - (layers - CACHED)) + j
+                z_kept[kept] = z
                 cw1[kept] = wb1[slot].astype(BF16)
                 cw2[kept] = w2[step % RING]
 
@@ -262,9 +262,9 @@
         src_ref=re.at[pl.ds(core * chips, chips)], dst_ref=re.at[pl.ds(core * chips, chips)],
         send_sem=px_send.at[1], recv_sem=px_recv.at[1], device_id=(partner,), device_id_type=MESH)
 
-    def error_step(l, j, w1, w2):
+    def error_step(l, z, w1, w2):
         q = mm(eb[l], w2, NT)
-        slope = gelu_grad(z_all[2 * l + j])[1]
+        slope = gelu_grad(z)[1]
         hcur[...] += mm((slope * q).astype(BF16), w1, NT)
 
     def backward_cached(i, carry):
@@ -272,7 +272,7 @@
         eb[l] = hcur[...].astype(BF16)
         for j in range(2):
             kept = 2 * (l - (layers - CACHED)) + j
-            error_step(l, j, cw1[kept], cw2[kept])
+            error_step(l, z_kept[kept], cw1[kept], cw2[kept])
         send_e(l)
         return carry
 
@@ -297,7 +297,8 @@
             w1_copy(0, 0, slot).wait()
             if m == 1:
                 pass_copy(step).wait_recv()
-            error_step(l, j, wb1[slot].astype(BF16), (own2 if m == 0 else far2)[step % RING])
+            w1 = wb1[slot].astype(BF16)
+            error_step(l, mm(hb[l], w1), w1, (own2 if m == 0 else far2)[step % RING])
 
             @pl.when(step + 2 < n_steps)
             def _(m=m, j=j, slot=slot):
@@ -313,34 +314,32 @@
         send_e(l)
         return carry
 
+    def h_in(c, carry):
+        @pl.when(c != chip)
+        def _():
+            h_arrival(c).wait_recv()
+
+        return carry
+
+    def e_in(c, carry):
+        @pl.when(c != chip)
+        def _():
+            e_arrival(c).wait_recv()
+
+        return carry
+
     lax.fori_loop(0, CACHED, backward_cached, 0)
     lax.fori_loop(0, n_bwd, backward, 0)
     eb[0] = hcur[...].astype(BF16)
-
+    send_e(0)
+    lax.fori_loop(0, chips, h_in, 0)
+    h_swap.start()
+    lax.fori_loop(0, chips, e_in, 0)
+    e_swap.start()
     w1_copy(0, 0, (2 * n_steps) % SLOTS).wait()
     w2_copy(0, n_steps % 2).wait()
     ow1[...] = wb1[(2 * n_steps) % SLOTS].astype(BF16)
     ow2[...] = wb2[n_steps % 2].astype(BF16)
-    send_e(0)
-
-    def h_in(c, carry):
-        @pl.when(c != chip)
-        def _():
-            h_arrival(c).wait_recv()
-
-        return carry
-
-    def e_in(c, carry):
-        @pl.when(c != chip)
-        def _():
-            e_arrival(c).wait_recv()
-
-        return carry
-
-    lax.fori_loop(0, chips, h_in, 0)
-    h_swap.start()
-    lax.fori_loop(0, chips, e_in, 0)
-    e_swap.start()
 
     def place(n, rx, ry, sz, twin):
         sx = 1 - cx if rx else cx
@@ -444,12 +443,14 @@
 
     def first_out(base, hg, eg):
         a, slope = gelu_grad(mm(hg, ow1[:, :piece]))
-        z_all[pl.ds(base, group), :, :piece] = slope.reshape(group, rows, piece)
+        for b in range(group):
+            z_kept[base // group, :, b * piece:(b + 1) * piece] = slope[b * rows:(b + 1) * rows]
         add_out(base, a.astype(BF16))
 
     def first_in(base, hg, eg):
         q = mm(eg, ow2[:piece, :], NT)
-        add_in(base, (z_all[pl.ds(base, group), :, :piece].reshape(group * rows, piece) * q).astype(BF16))
+        slope = jnp.concatenate([z_kept[base // group, :, b * piece:(b + 1) * piece] for b in range(group)], axis=0)
+        add_in(base, (slope * q).astype(BF16))
 
     row_groups(first_out, wait=True)
     store_out(0)
@@ -546,7 +547,7 @@
             pltpu.VMEM((RING, hc, d), BF16),
             pltpu.VMEM((2 * CACHED, d, hc), BF16),
             pltpu.VMEM((2 * CACHED, hc, d), BF16),
-            pltpu.VMEM((2 * layers, rows, hc), F32),
+            pltpu.VMEM((2 * CACHED, rows, hc), F32),
             pltpu.VMEM((layers, rows, d), BF16),
             pltpu.VMEM((layers, rows, d), BF16),
             pltpu.VMEM((rows, d), F32),

time: 544 us -> 541 us (level)
  the two profiles are of different devices: /device:TPU:21 before, /device:TPU:0 now
where the time goes in v9:
time: 541 us; the launch traced here: 534 us
  Pallas kernels  436 us (81%)
  waiting for transfers between devices  87.6 us (16%)
  starting transfers between devices  8.94 us (2%)
    pallas_call x1, Pallas kernels, local_grads(): pl.pallas_call(functools.partial(grads_kernel, dims), out_shape=[jax.Shap...  237 us
    pallas_call x4, Pallas kernels, update(): pl.pallas_call(functools.partial(update_kernel, (layers, rows, d, piece),...  200 us
    ppermute x12, waiting for transfers between devices, send(): return lax.ppermute(array, 'data', swap[axis])  87.6 us
  transfers between devices with their start and end apart: 12, of which 2 were waited for; matrix products, arithmetic and copies ran while one was open for 0% of the time, Pallas kernels for 28%

profile of v9, /device:TPU:0, one launch (start us, length us, event | category | flops | bytes accessed | tf_op | source)
XLA Modules:
  0.0 533.9 jit_solution(14674014372379913807)
XLA Ops:
  0.6 236.6 %local_grads.1 = (bf16[2,2,2,1024,128]{4,3,2,1,0:T(8,128)(2,1)}, bf16[2,2,2,1024,128]{4,3,2,1,0:T(8,128)(2,1)}, bf16[2,2,2,1024,128]{4,3,2,1,0:T(8,128)(2,1)}, b...) custom-call(f32[16,512,2048]{2,1,0:T(8,128)} %refs_0_.7, ...), custom_call_target="tpu_custom_call" | custom-call | flops 17179869184 | bytes 268435456 | tf_op jit(solution)/shard_map/local_grads/pallas_call | solution.py:535
  237.3 3.4 collective-permute-start
  240.7 0.0 collective-permute-start.2
  240.7 0.2 collective-permute-start.4
  240.8 1.9 collective-permute-start.6
  242.8 0.1 collective-permute-start.10
  242.9 44.6 %collective-permute-done.refs_9_ = bf16[2,2,2,1024,128]{4,3,2,1,0:T(8,128)(2,1)} collective-permute-done((bf16[2,2,2,1024,128]{4,3,2,1,0:T(8,128)(2,1)}, bf16[2,2,2,1024,128]{4,3,2,1,0:T(8,128)(2,1)}, u32[]{:S(2)}, u32[]{:S(2)}) %collective-permute-start) | collective-permute-done | bytes 2097184 | tf_op jit(solution)/shard_map/ppermute | solution.py:738
  287.5 2.0 collective-permute-start.8
  289.5 0.0 collective-permute-done.2.refs_11_
  289.5 0.0 collective-permute-start.1
  289.5 42.9 %collective-permute-done.4.refs_9_ = bf16[2,2,2,1024,128]{4,3,2,1,0:T(8,128)(2,1)} collective-permute-done((bf16[2,2,2,1024,128]{4,3,2,1,0:T(8,128)(2,1)}, bf16[2,2,2,1024,128]{4,3,2,1,0:T(8,128)(2,1)}, u32[]{:S(2)}, u32[]{:S(2)}) %collective-permute-start.4) | collective-permute-done | bytes 2097184 | tf_op jit(solution)/shard_map/ppermute | solution.py:738
  332.4 0.0 collective-permute-start.3
  332.4 49.9 %shard_map.127 = (f32[16,512,2048]{2,1,0:T(8,128)}, f32[16,2048,512]{2,1,0:T(8,128)}, f32[16,512,2048]{2,1,0:T(8,128)}, f32[16,2048,512]{2,1,0:T(8,128)}, f32[64,512]{1,0:T(8,128)}) custom-call(f32[16,512,2048]{2,1,0:T(8,128)} %refs_0_.7, f32[16,512,2048]{2,1,0:T(8,128)} %refs_1_.7, f32[16,2048,512]{2,1,0:T(8,128)} %refs_2_.7, f32[16,2048,512]{2,1,0:T(8,128)} %refs_3_.7, ...), custom_call_target="tpu_custom_call" | custom-call | flops 49999998976 | bytes 150994944 | tf_op jit(solution)/shard_map/pallas_call | solution.py:708
  382.3 0.0 collective-permute-done.6.refs_11_
  382.3 0.7 collective-permute-start.5
  383.1 0.0 collective-permute-done.10.refs_11_
  383.1 0.1 collective-permute-start.7
  383.1 0.0 collective-permute-done.8.refs_9_
  383.1 0.4 collective-permute-start.11
  383.6 0.0 collective-permute-done.1.refs_10_
  383.6 0.1 collective-permute-start.9
  383.7 0.0 collective-permute-done.3.refs_12_
  383.7 50.0 %shard_map.128 = (f32[16,512,2048]{2,1,0:T(8,128)}, f32[16,2048,512]{2,1,0:T(8,128)}, f32[16,512,2048]{2,1,0:T(8,128)}, f32[16,2048,512]{2,1,0:T(8,128)}, f32[64,512]{1,0:T(8,128)}) custom-call(f32[16,512,2048]{2,1,0:T(8,128)} %refs_0_.7, f32[16,512,2048]{2,1,0:T(8,128)} %refs_1_.7, ...), custom_call_target="tpu_custom_call", output_to_operand_aliasing={{0}: (13, {}), {1}: (14, {}), {2}: (15, {}), {3}: (16, {})} | custom-call | flops 49999998976 | bytes 150994944 | tf_op jit(solution)/shard_map/pallas_call | solution.py:708
  433.6 0.0 collective-permute-done.5.refs_10_
  433.6 0.0 collective-permute-done.7.refs_12_
  433.6 50.0 %shard_map.129 = (f32[16,512,2048]{2,1,0:T(8,128)}, f32[16,2048,512]{2,1,0:T(8,128)}, f32[16,512,2048]{2,1,0:T(8,128)}, f32[16,2048,512]{2,1,0:T(8,128)}, f32[64,512]{1,0:T(8,128)}) custom-call(f32[16,512,2048]{2,1,0:T(8,128)} %refs_0_.7, f32[16,512,2048]{2,1,0:T(8,128)} %refs_1_.7, ...), custom_call_target="tpu_custom_call", output_to_operand_aliasing={{0}: (13, {}), {1}: (14, {}), {2}: (15, {}), {3}: (16, {})} | custom-call | flops 49999998976 | bytes 150994944 | tf_op jit(solution)/shard_map/pallas_call | solution.py:708
  483.6 0.0 collective-permute-done.11.refs_12_
  483.6 0.0 collective-permute-done.9.refs_10_
  483.6 50.0 %shard_map.130 = (f32[16,512,2048]{2,1,0:T(8,128)}, f32[16,2048,512]{2,1,0:T(8,128)}, f32[16,512,2048]{2,1,0:T(8,128)}, f32[16,2048,512]{2,1,0:T(8,128)}, f32[64,512]{1,0:T(8,128)}, /*index=5*/f32[64]{0:T(128)}) custom-call(f32[16,512,2048]{2,1,0:T(8,128)} %refs_0_.7, ...), custom_call_target="tpu_custom_call", output_to_operand_aliasing={{0}: (13, {}), {1}: (14, {}), {2}: (15, {}), {3}: (16, {})} | custom-call | flops 49999998976 | bytes 150994944 | tf_op jit(solution)/shard_map/pallas_call | solution.py:708
Async XLA Ops:
  237.3 50.2 %collective-permute-start = (bf16[2,2,2,1024,128]{4,3,2,1,0:T(8,128)(2,1)}, bf16[2,2,2,1024,128]{4,3,2,1,0:T(8,128)(2,1)}, u32[]{:S(2)}, u32[]{:S(2)}) collective-permute-start(bf16[2,2,2,1024,128]{4,3,2,1,0:T(8,128)(2,1)} %get-tuple-element.56.refs_5_), channel_id=1, source_target_pairs={{0,4},{1,5},{2,6},{3,7},{4,0},{5,1},{6,2},{7,3},{8,12},{9,13},{10,... | collective-permute-start | bytes 6291464 | tf_op jit(solution)/shard_map/ppermute | solution.py:738
  240.7 48.8 %collective-permute-start.2 = (bf16[2,2,2,1024,128]{4,3,2,1,0:T(8,128)(2,1)}, bf16[2,2,2,1024,128]{4,3,2,1,0:T(8,128)(2,1)}, u32[]{:S(2)}, u32[]{:S(2)}) collective-permute-start(bf16[2,2,2,1024,128]{4,3,2,1,0:T(8,128)(2,1)} %get-tuple-element.58.refs_7_), channel_id=1, source_target_pairs={{0,2},{1,3},{2,0},{3,1},{4,6},{5,7},{6,4},{7,5},{8,10},{9,11},{10,... | collective-permute-start | bytes 6291464 | tf_op jit(solution)/shard_map/ppermute | solution.py:738
  240.7 91.7 %collective-permute-start.4 = (bf16[2,2,2,1024,128]{4,3,2,1,0:T(8,128)(2,1)}, bf16[2,2,2,1024,128]{4,3,2,1,0:T(8,128)(2,1)}, u32[]{:S(2)}, u32[]{:S(2)}) collective-permute-start(bf16[2,2,2,1024,128]{4,3,2,1,0:T(8,128)(2,1)} %get-tuple-element.65.refs_5_), channel_id=1, source_target_pairs={{0,4},{1,5},{2,6},{3,7},{4,0},{5,1},{6,2},{7,3},{8,12},{9,13},{10,... | collective-permute-start | bytes 6291464 | tf_op jit(solution)/shard_map/ppermute | solution.py:738
  240.8 141.5 %collective-permute-start.6 = (bf16[2,2,2,1024,128]{4,3,2,1,0:T(8,128)(2,1)}, bf16[2,2,2,1024,128]{4,3,2,1,0:T(8,128)(2,1)}, u32[]{:S(2)}, u32[]{:S(2)}) collective-permute-start(bf16[2,2,2,1024,128]{4,3,2,1,0:T(8,128)(2,1)} %get-tuple-element.67.refs_7_), channel_id=1, source_target_pairs={{0,2},{1,3},{2,0},{3,1},{4,6},{5,7},{6,4},{7,5},{8,10},{9,11},{10,... | collective-permute-start | bytes 6291464 | tf_op jit(solution)/shard_map/ppermute | solution.py:738
  242.8 140.3 %collective-permute-start.10 = (bf16[2,2,2,1024,128]{4,3,2,1,0:T(8,128)(2,1)}, bf16[2,2,2,1024,128]{4,3,2,1,0:T(8,128)(2,1)}, u32[]{:S(2)}, u32[]{:S(2)}) collective-permute-start(bf16[2,2,2,1024,128]{4,3,2,1,0:T(8,128)(2,1)} %get-tuple-element.76.refs_7_), channel_id=1, source_target_pairs={{0,2},{1,3},{2,0},{3,1},{4,6},{5,7},{6,4},{7,5},{8,10},{9,11},{10,... | collective-permute-start | bytes 6291464 | tf_op jit(solution)/shard_map/ppermute | solution.py:738
  287.5 95.7 %collective-permute-start.8 = (bf16[2,2,2,1024,128]{4,3,2,1,0:T(8,128)(2,1)}, bf16[2,2,2,1024,128]{4,3,2,1,0:T(8,128)(2,1)}, u32[]{:S(2)}, u32[]{:S(2)}) collective-permute-start(bf16[2,2,2,1024,128]{4,3,2,1,0:T(8,128)(2,1)} %get-tuple-element.74.refs_5_), channel_id=1, source_target_pairs={{0,4},{1,5},{2,6},{3,7},{4,0},{5,1},{6,2},{7,3},{8,12},{9,13},{10,... | collective-permute-start | bytes 6291464 | tf_op jit(solution)/shard_map/ppermute | solution.py:738
  289.5 94.1 %collective-permute-start.1 = (bf16[2,2,2,1024,128]{4,3,2,1,0:T(8,128)(2,1)}, bf16[2,2,2,1024,128]{4,3,2,1,0:T(8,128)(2,1)}, u32[]{:S(2)}, u32[]{:S(2)}) collective-permute-start(bf16[2,2,2,1024,128]{4,3,2,1,0:T(8,128)(2,1)} %collective-permute-done.refs_9_), channel_id=1, source_target_pairs={{0,1},{1,0},{2,3},{3,2},{4,5},{5,4},{6,7},{7,6},{8,9},{9,8},{10,11... | collective-permute-start | bytes 6291464 | tf_op jit(solution)/shard_map/ppermute | solution.py:738
  332.4 51.3 %collective-permute-start.3 = (bf16[2,2,2,1024,128]{4,3,2,1,0:T(8,128)(2,1)}, bf16[2,2,2,1024,128]{4,3,2,1,0:T(8,128)(2,1)}, u32[]{:S(2)}, u32[]{:S(2)}) collective-permute-start(bf16[2,2,2,1024,128]{4,3,2,1,0:T(8,128)(2,1)} %collective-permute-done.2.refs_11_), channel_id=1, source_target_pairs={{0,1},{1,0},{2,3},{3,2},{4,5},{5,4},{6,7},{7,6},{8,9},{9,8},{10,11... | collective-permute-start | bytes 6291464 | tf_op jit(solution)/shard_map/ppermute | solution.py:738
  382.3 51.3 %collective-permute-start.5 = (bf16[2,2,2,1024,128]{4,3,2,1,0:T(8,128)(2,1)}, bf16[2,2,2,1024,128]{4,3,2,1,0:T(8,128)(2,1)}, u32[]{:S(2)}, u32[]{:S(2)}) collective-permute-start(bf16[2,2,2,1024,128]{4,3,2,1,0:T(8,128)(2,1)} %collective-permute-done.4.refs_9_), channel_id=1, source_target_pairs={{0,1},{1,0},{2,3},{3,2},{4,5},{5,4},{6,7},{7,6},{8,9},{9,8},{10,11... | collective-permute-start | bytes 6291464 | tf_op jit(solution)/shard_map/ppermute | solution.py:738
  383.1 50.6 %collective-permute-start.7 = (bf16[2,2,2,1024,128]{4,3,2,1,0:T(8,128)(2,1)}, bf16[2,2,2,1024,128]{4,3,2,1,0:T(8,128)(2,1)}, u32[]{:S(2)}, u32[]{:S(2)}) collective-permute-start(bf16[2,2,2,1024,128]{4,3,2,1,0:T(8,128)(2,1)} %collective-permute-done.6.refs_11_), channel_id=1, source_target_pairs={{0,1},{1,0},{2,3},{3,2},{4,5},{5,4},{6,7},{7,6},{8,9},{9,8},{10,11... | collective-permute-start | bytes 6291464 | tf_op jit(solution)/shard_map/ppermute | solution.py:738
  383.1 100.5 %collective-permute-start.11 = (bf16[2,2,2,1024,128]{4,3,2,1,0:T(8,128)(2,1)}, bf16[2,2,2,1024,128]{4,3,2,1,0:T(8,128)(2,1)}, u32[]{:S(2)}, u32[]{:S(2)}) collective-permute-start(bf16[2,2,2,1024,128]{4,3,2,1,0:T(8,128)(2,1)} %collective-permute-done.10.refs_11_), channel_id=1, source_target_pairs={{0,1},{1,0},{2,3},{3,2},{4,5},{5,4},{6,7},{7,6},{8,9},{9,8},{10,11... | collective-permute-start | bytes 6291464 | tf_op jit(solution)/shard_map/ppermute | solution.py:738
  383.6 100.1 %collective-permute-start.9 = (bf16[2,2,2,1024,128]{4,3,2,1,0:T(8,128)(2,1)}, bf16[2,2,2,1024,128]{4,3,2,1,0:T(8,128)(2,1)}, u32[]{:S(2)}, u32[]{:S(2)}) collective-permute-start(bf16[2,2,2,1024,128]{4,3,2,1,0:T(8,128)(2,1)} %collective-permute-done.8.refs_9_), channel_id=1, source_target_pairs={{0,1},{1,0},{2,3},{3,2},{4,5},{5,4},{6,7},{7,6},{8,9},{9,8},{10,11... | collective-permute-start | bytes 6291464 | tf_op jit(solution)/shard_map/ppermute | solution.py:738
